TPU v7x, 128 devices: a whole 4x4x4 slice. The times are simulated.
128 devices in a mesh: group: 4 (over y), inner: 32 (over z, x, core).
Axes of the slice: x: 4, y: 4, z: 4, core: 2. Of those that a mesh axis runs over, the one named last changes fastest.
Arguments:
- tokens_fwd: bfloat16 [8192, 2048], P(('group', 'inner')), may hold values from -6 to 6
- experts_fwd: int32 [8192, 8], P(('group', 'inner')), may hold values from 0 to 127, all different within a row; in each aligned block of 64 rows (0 to 63, 64 to 127, ...) at most 6 rows name the same one
- scores_fwd: float32 [8192, 8], P(('group', 'inner')), may hold values from 0.05 to 1
- tokens_bwd: bfloat16 [8192, 2048], P(('group', 'inner')), may hold values from -6 to 6
- experts_bwd: int32 [8192, 8], P(('group', 'inner')), may hold values from 0 to 127, all different within a row; in each aligned block of 64 rows (0 to 63, 64 to 127, ...) at most 6 rows name the same one
- scores_bwd: float32 [8192, 8], P(('group', 'inner')), may hold values from 0.05 to 1
- cotangent: bfloat16 [8192, 2048], P(('group', 'inner')), may hold values from -6 to 6
- w_in: bfloat16 [128, 2048, 1536], P(('group', 'inner')), may hold values from -0.125 to 0.125
- w_down: bfloat16 [128, 768, 2048], P(('group', 'inner')), may hold values from -0.21875 to 0.21875
Outputs:
- output_fwd: bfloat16 [8192, 2048], P(('group', 'inner'))
- grad_tokens: bfloat16 [8192, 2048], P(('group', 'inner'))
- grad_w_in: bfloat16 [128, 2048, 1536], P(('group', 'inner'))
- grad_w_down: bfloat16 [128, 768, 2048], P(('group', 'inner'))
Inputs may be any that keep to these rules, and one draw needn't show every extreme that they name: `experts_fwd`: each token names 8 different experts; among the tokens of one device at most 6 name any one expert. `experts_bwd`: each token names 8 different experts; among the tokens of one device at most 6 name any one expert.
All inputs are finite; a program needn't handle non-finite values.
Results may differ from a plain program's by a relative error of at most 0.0064.
Values may be sent and summed in bfloat16 or wider, within the bound.
No kernel may reach another device: no remote copies, remote signals or barrier semaphores. Data moves between devices by JAX's collectives and lax.ppermute only.
A program may use at most 128 MiB of HBM per device.

v0:
```python
import jax
import jax.numpy as jnp
from jax import lax
from jax.sharding import PartitionSpec as P


def expert_forward(tok_rows, w_in_e, w_down_e):
    width = w_down_e.shape[0]
    projected = jnp.dot(tok_rows, w_in_e, preferred_element_type=jnp.float32)
    gate_part = projected[:, :width]
    up_part = projected[:, width:]
    hidden = (gate_part * jax.nn.sigmoid(gate_part) * up_part).astype(jnp.bfloat16)
    return jnp.dot(hidden, w_down_e, preferred_element_type=jnp.float32).astype(jnp.bfloat16)


def expert_backward(tok_rows, cot_rows, w_in_e, w_down_e):
    width = w_down_e.shape[0]
    projected = jnp.dot(tok_rows, w_in_e, preferred_element_type=jnp.float32)
    gate_part = projected[:, :width]
    up_part = projected[:, width:]
    sigmoid_gate = jax.nn.sigmoid(gate_part)
    hidden = (gate_part * sigmoid_gate * up_part).astype(jnp.bfloat16)
    contract_rows = (((0,), (0,)), ((), ()))
    contract_cols = (((1,), (1,)), ((), ()))
    grad_down = lax.dot_general(
        hidden, cot_rows, contract_rows, preferred_element_type=jnp.float32
    ).astype(jnp.bfloat16)
    d_hidden = lax.dot_general(
        cot_rows, w_down_e, contract_cols, preferred_element_type=jnp.float32
    )
    d_gate = d_hidden * up_part * sigmoid_gate * (1.0 + gate_part * (1.0 - sigmoid_gate))
    d_up = d_hidden * gate_part * sigmoid_gate
    d_proj = jnp.concatenate([d_gate, d_up], axis=1).astype(jnp.bfloat16)
    grad_inner = lax.dot_general(
        tok_rows, d_proj, contract_rows, preferred_element_type=jnp.float32
    ).astype(jnp.bfloat16)
    row_grad = lax.dot_general(
        d_proj, w_in_e, contract_cols, preferred_element_type=jnp.float32
    ).astype(jnp.bfloat16)
    return (row_grad, grad_inner, grad_down)


def place_table(expert_ids, devices, capacity):
    tok_count, top_count = expert_ids.shape
    flat_ids = expert_ids.reshape(-1)
    labels = jnp.arange(devices, dtype=jnp.int32)
    onehot = (flat_ids[:, None] == labels[None, :]).astype(jnp.int32)
    before = jnp.cumsum(onehot, axis=0) - onehot
    slot_pos = jnp.sum(before * onehot, axis=1)
    target = flat_ids * capacity + slot_pos
    assigned = (
        jnp.full((devices * capacity,), tok_count * top_count, jnp.int32)
        .at[target]
        .set(jnp.arange(tok_count * top_count, dtype=jnp.int32))
    )
    return (target, assigned)


def shards(
    tokens_fwd,
    experts_fwd,
    scores_fwd,
    tokens_bwd,
    experts_bwd,
    scores_bwd,
    cotangent,
    w_in,
    w_down,
):
    group_count = lax.axis_size("group")
    inner_count = lax.axis_size("inner")
    devices = group_count * inner_count
    tok_count, top_count = experts_fwd.shape
    width = tokens_fwd.shape[1]
    capacity = max(2, 3 * tok_count * top_count // (2 * devices))
    flat_shape = (devices * capacity, width)
    shape_four = (group_count, inner_count, capacity * width)
    target_fwd, assigned_fwd = place_table(experts_fwd, devices, capacity)
    target_bwd, assigned_bwd = place_table(experts_bwd, devices, capacity)
    weights_fwd = scores_fwd / jnp.sum(scores_fwd, axis=1, keepdims=True)
    weights_bwd = scores_bwd / jnp.sum(scores_bwd, axis=1, keepdims=True)
    zero_row = jnp.zeros((1, width), jnp.bfloat16)
    fwd_padded = jnp.concatenate([tokens_fwd, zero_row], axis=0)
    bwd_padded = jnp.concatenate([tokens_bwd, zero_row], axis=0)
    cot_assign = (
        weights_bwd.reshape(-1)[:, None]
        * jnp.repeat(cotangent, top_count, axis=0).astype(jnp.float32)
    ).astype(jnp.bfloat16)
    cot_padded = jnp.concatenate([cot_assign, zero_row], axis=0)
    send_fwd = fwd_padded[assigned_fwd // top_count]
    send_bwd = bwd_padded[assigned_bwd // top_count]
    send_cot = cot_padded[assigned_bwd]
    recv_fwd, recv_bwd, recv_cot = (
        lax.all_to_all(
            lax.all_to_all(
                send_fwd.reshape(shape_four), "inner", split_axis=1, concat_axis=1, tiled=True
            ),
            "group",
            split_axis=0,
            concat_axis=0,
            tiled=True,
        ),
        lax.all_to_all(
            lax.all_to_all(
                send_bwd.reshape(shape_four), "inner", split_axis=1, concat_axis=1, tiled=True
            ),
            "group",
            split_axis=0,
            concat_axis=0,
            tiled=True,
        ),
        lax.all_to_all(
            lax.all_to_all(
                send_cot.reshape(shape_four), "inner", split_axis=1, concat_axis=1, tiled=True
            ),
            "group",
            split_axis=0,
            concat_axis=0,
            tiled=True,
        ),
    )
    expert_out = expert_forward(recv_fwd.reshape(flat_shape), w_in[0], w_down[0])
    row_grad, grad_inner, grad_down = expert_backward(
        recv_bwd.reshape(flat_shape), recv_cot.reshape(flat_shape), w_in[0], w_down[0]
    )
    back_out, back_grad = (
        lax.all_to_all(
            lax.all_to_all(
                expert_out.reshape(shape_four), "inner", split_axis=1, concat_axis=1, tiled=True
            ),
            "group",
            split_axis=0,
            concat_axis=0,
            tiled=True,
        ),
        lax.all_to_all(
            lax.all_to_all(
                row_grad.reshape(shape_four), "inner", split_axis=1, concat_axis=1, tiled=True
            ),
            "group",
            split_axis=0,
            concat_axis=0,
            tiled=True,
        ),
    )
    picked_out = back_out.reshape(flat_shape)[target_fwd].reshape(tok_count, top_count, width)
    output_fwd = jnp.sum(weights_fwd[:, :, None] * picked_out.astype(jnp.float32), axis=1).astype(
        jnp.bfloat16
    )
    picked_grad = back_grad.reshape(flat_shape)[target_bwd].reshape(tok_count, top_count, width)
    grad_tokens = jnp.sum(picked_grad.astype(jnp.float32), axis=1).astype(jnp.bfloat16)
    return (output_fwd, grad_tokens, grad_inner[None], grad_down[None])


def solution(mesh):
    return jax.shard_map(
        shards,
        mesh=mesh,
        in_specs=(
            P(("group", "inner"), None),
            P(("group", "inner"), None),
            P(("group", "inner"), None),
            P(("group", "inner"), None),
            P(("group", "inner"), None),
            P(("group", "inner"), None),
            P(("group", "inner"), None),
            P(("group", "inner"), None, None),
            P(("group", "inner"), None, None),
        ),
        out_specs=(
            P(("group", "inner"), None),
            P(("group", "inner"), None),
            P(("group", "inner"), None, None),
            P(("group", "inner"), None, None),
        ),
        check_vma=False,
    )
```

profile of v0, /device:TPU:6, one launch (start us, length us, event | category | flops | bytes accessed | tf_op | source)
XLA Modules:
  0.0 506.0 jit_solution(9216711920134629974)
XLA Ops:
  10.3 9.0 %gather_fusion.2 = bf16[768,2048]{1,0:T(8,128)(2,1)} fusion(bf16[513,2048]{1,0:T(8,128)(2,1)} %concatenate.14, s32[1024]{0:T(1024)S(1)} %get-tuple-element.9), kind=kCustom, calls=%fused_computation.2 | custom fusion | bytes 6294528 | tf_op jit(solution)/shard_map/gather | solution.py:92
  19.2 6.8 %reshape.148 = bf16[4,32,12288]{2,1,0:T(8,128)(2,1)} reshape(bf16[768,2048]{1,0:T(8,128)(2,1)} %gather_fusion.2) | data formatting | bytes 6291456 | tf_op jit(solution)/shard_map/reshape | solution.py:114
  32.0 8.9 %all-to-all-start.4 = ((bf16[4,32,12288]{2,0,1:T(4,128)(2,1)}), bf16[4,32,12288]{2,0,1:T(4,128)(2,1)}, u32[]{:S(2)}, u32[]{:S(2)}) async-start(bf16[4,32,12288]{2,0,1:T(4,128)(2,1)} %copy.91), calls=%async_computation.4 | async-start | bytes 6291456 | tf_op jit(solution)/shard_map/all_to_all | solution.py:113
  46.2 6.8 %reshape.150 = bf16[4,32,12288]{2,1,0:T(8,128)(2,1)} reshape(bf16[768,2048]{1,0:T(8,128)(2,1)} %gather_fusion.3) | data formatting | bytes 6291456 | tf_op jit(solution)/shard_map/reshape | solution.py:105
  52.9 6.0 %copy.93 = bf16[4,32,12288]{2,0,1:T(4,128)(2,1)} copy(bf16[4,32,12288]{2,1,0:T(8,128)(2,1)} %reshape.150) | data formatting | bytes 6291456 | tf_op jit(solution)/shard_map/reshape | solution.py:105
  58.9 19.9 %all-to-all-done.4 = bf16[4,32,12288]{2,0,1:T(4,128)(2,1)} async-done(((bf16[4,32,12288]{2,0,1:T(4,128)(2,1)}), bf16[4,32,12288]{2,0,1:T(4,128)(2,1)}, u32[]{:S(2)}, u32[]{:S(2)}) %all-to-all-start.4) | async-done | bytes 3145760 | tf_op jit(solution)/shard_map/all_to_all | solution.py:113
  78.8 8.7 %all-to-all-start.6 = ((bf16[4,32,12288]{2,0,1:T(4,128)(2,1)}), bf16[4,32,12288]{2,0,1:T(4,128)(2,1)}, u32[]{:S(2)}, u32[]{:S(2)}) async-start(bf16[4,32,12288]{2,0,1:T(4,128)(2,1)} %copy.93), calls=%async_computation.6 | async-start | bytes 6291456 | tf_op jit(solution)/shard_map/all_to_all | solution.py:104
  96.3 6.8 %reshape.143 = bf16[4,32,12288]{2,1,0:T(8,128)(2,1)} reshape(bf16[768,2048]{1,0:T(8,128)(2,1)} %gather_fusion) | data formatting | bytes 6291456 | tf_op jit(solution)/shard_map/reshape | solution.py:96
  109.1 16.2 %all-to-all-done.6 = bf16[4,32,12288]{2,0,1:T(4,128)(2,1)} async-done(((bf16[4,32,12288]{2,0,1:T(4,128)(2,1)}), bf16[4,32,12288]{2,0,1:T(4,128)(2,1)}, u32[]{:S(2)}, u32[]{:S(2)}) %all-to-all-start.6) | async-done | bytes 3145760 | tf_op jit(solution)/shard_map/all_to_all | solution.py:104
  125.3 9.7 %all-to-all-start = ((bf16[4,32,12288]{2,0,1:T(4,128)(2,1)}), bf16[4,32,12288]{2,0,1:T(4,128)(2,1)}, u32[]{:S(2)}, u32[]{:S(2)}) async-start(bf16[4,32,12288]{2,0,1:T(4,128)(2,1)} %copy.81), calls=%async_computation | async-start | bytes 6291456 | tf_op jit(solution)/shard_map/all_to_all | solution.py:95
  140.3 32.7 %all-to-all-done = bf16[4,32,12288]{2,0,1:T(4,128)(2,1)} async-done(((bf16[4,32,12288]{2,0,1:T(4,128)(2,1)}), bf16[4,32,12288]{2,0,1:T(4,128)(2,1)}, u32[]{:S(2)}, u32[]{:S(2)}) %all-to-all-start) | async-done | bytes 3145760 | tf_op jit(solution)/shard_map/all_to_all | solution.py:95
  182.9 33.6 %all-to-all-done.7 = bf16[4,32,12288]{2,1,0:T(8,128)(2,1)} async-done(((bf16[4,32,12288]{2,1,0:T(8,128)(2,1)}), bf16[4,32,12288]{2,1,0:T(8,128)(2,1)}, u32[]{:S(2)}, u32[]{:S(2)}) %all-to-all-start.7) | async-done | bytes 3145760 | tf_op jit(solution)/shard_map/all_to_all | solution.py:103
  226.4 6.8 %reshape.151 = bf16[768,2048]{1,0:T(8,128)(2,1)} reshape(bf16[4,32,12288]{2,1,0:T(8,128)(2,1)} %all-to-all-done.7) | data formatting | bytes 6291456 | tf_op jit(solution)/shard_map/reshape | solution.py:124
  233.2 26.0 %all-to-all-done.5 = bf16[4,32,12288]{2,1,0:T(8,128)(2,1)} async-done(((bf16[4,32,12288]{2,1,0:T(8,128)(2,1)}), bf16[4,32,12288]{2,1,0:T(8,128)(2,1)}, u32[]{:S(2)}, u32[]{:S(2)}) %all-to-all-start.5) | async-done | bytes 3145760 | tf_op jit(solution)/shard_map/all_to_all | solution.py:112
  264.0 9.5 %fusion.3 = f32[768,1536]{1,0:T(8,128)} fusion(bf16[768,2048]{1,0:T(8,128)(2,1)} %reshape.151, bf16[1,2048,1536]{2,1,0:T(8,128)(2,1)} %param.16), kind=kOutput, calls=%fused_computation.11 | convolution fusion | flops 4831838208 | bytes 14155776 | tf_op jit(solution)/shard_map/dot_general | solution.py:18
  273.5 6.8 %reshape.149 = bf16[768,2048]{1,0:T(8,128)(2,1)} reshape(bf16[4,32,12288]{2,1,0:T(8,128)(2,1)} %all-to-all-done.5) | data formatting | bytes 6291456 | tf_op jit(solution)/shard_map/reshape | solution.py:124
  280.3 6.5 %multiply_convert_fusion.2 = (bf16[768,768]{1,0:T(8,128)(2,1)S(1)}, bf16[768,768]{1,0:T(8,128)(2,1)S(1)}) fusion(f32[768,1536]{1,0:T(8,128)} %fusion.3, bf16[768,2048]{1,0:T(8,128)(2,1)} %reshape.149, bf16[1,768,2048]{2,1,0:T(8,128)(2,1)S(1)} %copy-done), kind=kOutput, calls=%fused_computation.31 | convolution fusion | flops 2423586816 | bytes 13369344 | tf_op jit(solution)/shard_map/dot_general | solution.py:28
  288.2 9.2 %fusion.9 = bf16[768,2048]{1,0:T(8,128)(2,1)} fusion(bf16[1,2048,1536]{2,1,0:T(8,128)(2,1)} %param.16, bf16[768,768]{1,0:T(8,128)(2,1)S(1)} %get-tuple-element.5, bf16[768,768]{1,0:T(8,128)(2,1)S(1)} %get-tuple-element.4), kind=kOutput, calls=%fused_computation.21 | convolution fusion | flops 4838129664 | bytes 11796480 | tf_op jit(solution)/shard_map/dot_general | solution.py:37
  297.4 6.8 %reshape.152 = bf16[4,32,12288]{2,1,0:T(8,128)(2,1)} reshape(bf16[768,2048]{1,0:T(8,128)(2,1)} %fusion.9) | data formatting | bytes 6291456 | tf_op jit(solution)/shard_map/reshape | solution.py:138
  316.0 6.8 %reshape.144 = bf16[768,2048]{1,0:T(8,128)(2,1)} reshape(bf16[4,32,12288]{2,1,0:T(8,128)(2,1)} %all-to-all-done.1) | data formatting | bytes 6291456 | tf_op jit(solution)/shard_map/reshape | solution.py:122
  322.8 8.1 %fusion.5 = f32[768,1536]{1,0:T(8,128)S(1)} fusion(bf16[768,2048]{1,0:T(8,128)(2,1)} %reshape.144, bf16[1,2048,1536]{2,1,0:T(8,128)(2,1)} %param.16), kind=kOutput, calls=%fused_computation.13 | convolution fusion | flops 4831838208 | bytes 14155776 | tf_op jit(solution)/shard_map/dot_general | solution.py:9
  335.0 6.8 %reshape.145 = bf16[4,32,12288]{2,1,0:T(8,128)(2,1)} reshape(bf16[768,2048]{1,0:T(8,128)(2,1)} %convolution_convert_fusion.2) | data formatting | bytes 6291456 | tf_op jit(solution)/shard_map/reshape | solution.py:129
  347.7 6.2 %all-to-all-done.8 = bf16[4,32,12288]{2,0,1:T(4,128)(2,1)} async-done(((bf16[4,32,12288]{2,0,1:T(4,128)(2,1)}), bf16[4,32,12288]{2,0,1:T(4,128)(2,1)}, u32[]{:S(2)}, u32[]{:S(2)}) %all-to-all-start.8) | async-done | bytes 3145760 | tf_op jit(solution)/shard_map/all_to_all | solution.py:137
  353.9 8.7 %all-to-all-start.2 = ((bf16[4,32,12288]{2,0,1:T(4,128)(2,1)}), bf16[4,32,12288]{2,0,1:T(4,128)(2,1)}, u32[]{:S(2)}, u32[]{:S(2)}) async-start(bf16[4,32,12288]{2,0,1:T(4,128)(2,1)} %copy.83), calls=%async_computation.2 | async-start | bytes 6291456 | tf_op jit(solution)/shard_map/all_to_all | solution.py:128
  367.9 32.5 %all-to-all-done.2 = bf16[4,32,12288]{2,0,1:T(4,128)(2,1)} async-done(((bf16[4,32,12288]{2,0,1:T(4,128)(2,1)}), bf16[4,32,12288]{2,0,1:T(4,128)(2,1)}, u32[]{:S(2)}, u32[]{:S(2)}) %all-to-all-start.2) | async-done | bytes 3145760 | tf_op jit(solution)/shard_map/all_to_all | solution.py:128
  410.6 33.4 %all-to-all-done.9 = bf16[4,32,12288]{2,1,0:T(8,128)(2,1)} async-done(((bf16[4,32,12288]{2,1,0:T(8,128)(2,1)}), bf16[4,32,12288]{2,1,0:T(8,128)(2,1)}, u32[]{:S(2)}, u32[]{:S(2)}) %all-to-all-start.9) | async-done | bytes 3145760 | tf_op jit(solution)/shard_map/all_to_all | solution.py:136
  449.1 7.8 %fusion.15 = bf16[1,768,2048]{2,1,0:T(8,128)(2,1)} fusion(bf16[768,2048]{1,0:T(8,128)(2,1)} %reshape.149, f32[768,1536]{1,0:T(8,128)} %fusion.3), kind=kOutput, calls=%fused_computation.25 | convolution fusion | flops 2421030912 | bytes 11010048 | tf_op jit(solution)/shard_map/dot_general | solution.py:25
  456.9 7.4 %fusion = bf16[1,2048,1536]{2,1,0:T(8,128)(2,1)} fusion(bf16[768,2048]{1,0:T(8,128)(2,1)S(1)} %copy-done.1, bf16[768,768]{1,0:T(8,128)(2,1)S(1)} %copy-done.7, bf16[768,768]{1,0:T(8,128)(2,1)S(1)} %copy-done.5), kind=kOutput, calls=%fused_computation.8 | convolution fusion | flops 4839702528 | bytes 11796480 | tf_op jit(solution)/shard_map/dot_general | solution.py:34
  464.3 6.8 %reshape.153 = bf16[768,2048]{1,0:T(8,128)(2,1)} reshape(bf16[4,32,12288]{2,1,0:T(8,128)(2,1)} %all-to-all-done.9) | data formatting | bytes 6291456 | tf_op jit(solution)/shard_map/reshape | solution.py:150
  471.0 7.5 %gather_fusion.4 = bf16[512,2048]{1,0:T(8,128)(2,1)} fusion(bf16[768,2048]{1,0:T(8,128)(2,1)} %reshape.153, s32[1024]{0:T(1024)S(1)} %pad_clamp_fusion), kind=kCustom, calls=%fused_computation.4 | custom fusion | bytes 4196352 | tf_op jit(solution)/shard_map/gather | solution.py:150
  487.2 6.8 %reshape.146 = bf16[768,2048]{1,0:T(8,128)(2,1)} reshape(bf16[4,32,12288]{2,1,0:T(8,128)(2,1)} %all-to-all-done.3) | data formatting | bytes 6291456 | tf_op jit(solution)/shard_map/reshape | solution.py:146
  494.0 7.7 %gather_fusion.1 = bf16[512,2048]{1,0:T(8,128)(2,1)} fusion(bf16[768,2048]{1,0:T(8,128)(2,1)} %reshape.146, s32[1024]{0:T(1024)S(1)} %pad_clamp_fusion.3), kind=kCustom, calls=%fused_computation.1 | custom fusion | bytes 4196352 | tf_op jit(solution)/shard_map/gather | solution.py:146
  (92 shorter events, 122.1 us)
Async XLA Ops:
  0.6 279.6 %copy-start = (bf16[1,768,2048]{2,1,0:T(8,128)(2,1)S(1)}, bf16[1,768,2048]{2,1,0:T(8,128)(2,1)}, u32[]{:S(2)}) copy-start(bf16[1,768,2048]{2,1,0:T(8,128)(2,1)} %param.17) | copy-start | bytes 9437188
  32.0 46.8 %all-to-all-start.4 = ((bf16[4,32,12288]{2,0,1:T(4,128)(2,1)}), bf16[4,32,12288]{2,0,1:T(4,128)(2,1)}, u32[]{:S(2)}, u32[]{:S(2)}) async-start(bf16[4,32,12288]{2,0,1:T(4,128)(2,1)} %copy.91), calls=%async_computation.4 | async-start | bytes 6291456 | tf_op jit(solution)/shard_map/all_to_all | solution.py:113
  58.9 28.5 %copy-start.2 = (s32[64,8]{0,1:T(8,128)S(1)}, s32[64,8]{0,1:T(8,128)}, u32[]{:S(2)}) copy-start(s32[64,8]{0,1:T(8,128)} %param.10) | copy-start | bytes 6148
  78.8 46.5 %all-to-all-start.6 = ((bf16[4,32,12288]{2,0,1:T(4,128)(2,1)}), bf16[4,32,12288]{2,0,1:T(4,128)(2,1)}, u32[]{:S(2)}, u32[]{:S(2)}) async-start(bf16[4,32,12288]{2,0,1:T(4,128)(2,1)} %copy.93), calls=%async_computation.6 | async-start | bytes 6291456 | tf_op jit(solution)/shard_map/all_to_all | solution.py:104
  125.3 47.7 %all-to-all-start = ((bf16[4,32,12288]{2,0,1:T(4,128)(2,1)}), bf16[4,32,12288]{2,0,1:T(4,128)(2,1)}, u32[]{:S(2)}, u32[]{:S(2)}) async-start(bf16[4,32,12288]{2,0,1:T(4,128)(2,1)} %copy.81), calls=%async_computation | async-start | bytes 6291456 | tf_op jit(solution)/shard_map/all_to_all | solution.py:95
  173.0 43.6 %all-to-all-start.7 = ((bf16[4,32,12288]{2,1,0:T(8,128)(2,1)}), bf16[4,32,12288]{2,1,0:T(8,128)(2,1)}, u32[]{:S(2)}, u32[]{:S(2)}) async-start(bf16[4,32,12288]{2,1,0:T(8,128)(2,1)} %copy.94), calls=%async_computation.7 | async-start | bytes 6291456 | tf_op jit(solution)/shard_map/all_to_all | solution.py:103
  216.5 42.7 %all-to-all-start.5 = ((bf16[4,32,12288]{2,1,0:T(8,128)(2,1)}), bf16[4,32,12288]{2,1,0:T(8,128)(2,1)}, u32[]{:S(2)}, u32[]{:S(2)}) async-start(bf16[4,32,12288]{2,1,0:T(8,128)(2,1)} %copy.92), calls=%async_computation.5 | async-start | bytes 6291456 | tf_op jit(solution)/shard_map/all_to_all | solution.py:112
  259.2 51.0 %all-to-all-start.1 = ((bf16[4,32,12288]{2,1,0:T(8,128)(2,1)}), bf16[4,32,12288]{2,1,0:T(8,128)(2,1)}, u32[]{:S(2)}, u32[]{:S(2)}) async-start(bf16[4,32,12288]{2,1,0:T(8,128)(2,1)} %copy.82), calls=%async_computation.1 | async-start | bytes 6291456 | tf_op jit(solution)/shard_map/all_to_all | solution.py:94
  286.8 1.0 copy-start.4
  286.8 1.4 copy-start.6
  310.2 43.7 %all-to-all-start.8 = ((bf16[4,32,12288]{2,0,1:T(4,128)(2,1)}), bf16[4,32,12288]{2,0,1:T(4,128)(2,1)}, u32[]{:S(2)}, u32[]{:S(2)}) async-start(bf16[4,32,12288]{2,0,1:T(4,128)(2,1)} %copy.97), calls=%async_computation.8 | async-start | bytes 6291456 | tf_op jit(solution)/shard_map/all_to_all | solution.py:137
  353.9 46.5 %all-to-all-start.2 = ((bf16[4,32,12288]{2,0,1:T(4,128)(2,1)}), bf16[4,32,12288]{2,0,1:T(4,128)(2,1)}, u32[]{:S(2)}, u32[]{:S(2)}) async-start(bf16[4,32,12288]{2,0,1:T(4,128)(2,1)} %copy.83), calls=%async_computation.2 | async-start | bytes 6291456 | tf_op jit(solution)/shard_map/all_to_all | solution.py:128
  367.9 37.3 %copy-start.3 = (f32[64,8]{0,1:T(8,128)S(1)}, f32[64,8]{0,1:T(8,128)}, u32[]{:S(2)}) copy-start(f32[64,8]{0,1:T(8,128)} %param.11) | copy-start | bytes 6148
  400.4 43.6 %all-to-all-start.9 = ((bf16[4,32,12288]{2,1,0:T(8,128)(2,1)}), bf16[4,32,12288]{2,1,0:T(8,128)(2,1)}, u32[]{:S(2)}, u32[]{:S(2)}) async-start(bf16[4,32,12288]{2,1,0:T(8,128)(2,1)} %copy.98), calls=%async_computation.9 | async-start | bytes 6291456 | tf_op jit(solution)/shard_map/all_to_all | solution.py:136
  444.0 43.2 %all-to-all-start.3 = ((bf16[4,32,12288]{2,1,0:T(8,128)(2,1)}), bf16[4,32,12288]{2,1,0:T(8,128)(2,1)}, u32[]{:S(2)}, u32[]{:S(2)}) async-start(bf16[4,32,12288]{2,1,0:T(8,128)(2,1)} %copy.84), calls=%async_computation.3 | async-start | bytes 6291456 | tf_op jit(solution)/shard_map/all_to_all | solution.py:127
  449.0 7.9 %copy-start.1 = (bf16[768,2048]{1,0:T(8,128)(2,1)S(1)}, bf16[768,2048]{1,0:T(8,128)(2,1)}, u32[]{:S(2)}) copy-start(bf16[768,2048]{1,0:T(8,128)(2,1)} %reshape.151) | copy-start | bytes 9437188
  449.1 7.8 %copy-start.5 = (bf16[768,768]{1,0:T(8,128)(2,1)S(1)}, bf16[768,768]{1,0:T(8,128)(2,1)}, u32[]{:S(2)}) copy-start(bf16[768,768]{1,0:T(8,128)(2,1)} %copy-done.4) | copy-start | bytes 3538948
  449.1 7.8 %copy-start.7 = (bf16[768,768]{1,0:T(8,128)(2,1)S(1)}, bf16[768,768]{1,0:T(8,128)(2,1)}, u32[]{:S(2)}) copy-start(bf16[768,768]{1,0:T(8,128)(2,1)} %copy-done.6) | copy-start | bytes 3538948
where the time goes:
time: 515 us; the launch traced here: 506 us
  waiting for transfers between devices  205 us (40%)
  local copies, waits for them, and re-layouts  169 us (33%)
  starting transfers between devices  65.7 us (13%)
  matrix products  52.6 us (10%)
  other arithmetic  12.5 us (2%)
    all_to_all x1, waiting for transfers between devices, shards(): lax.all_to_all(lax.all_to_all(send_bwd.reshape(shape_four), 'inner', spli...  33.6 us
    all_to_all x1, waiting for transfers between devices, shards(): lax.all_to_all(lax.all_to_all(row_grad.reshape(shape_four), 'inner', spli...  33.4 us
    all_to_all x1, waiting for transfers between devices, shards(): lax.all_to_all(send_fwd.reshape(shape_four), 'inner', split_axis=1, conca...  32.7 us
    all_to_all x1, waiting for transfers between devices, shards(): lax.all_to_all(expert_out.reshape(shape_four), 'inner', split_axis=1, con...  32.5 us
    all_to_all x1, waiting for transfers between devices, shards(): lax.all_to_all(lax.all_to_all(send_cot.reshape(shape_four), 'inner', spli...  26 us
    all_to_all x1, waiting for transfers between devices, shards(): lax.all_to_all(send_cot.reshape(shape_four), 'inner', split_axis=1, conca...  19.9 us
    all_to_all x1, waiting for transfers between devices, shards(): lax.all_to_all(send_bwd.reshape(shape_four), 'inner', split_axis=1, conca...  16.2 us
    reshape x2, local copies, waits for them, and re-layouts, shards(): send_bwd.reshape(shape_four)  12.8 us
  transfers between devices with their start and end apart: 10, of which 9 were waited for; matrix products, arithmetic and copies ran while one was open for 36% of the time, Pallas kernels for 0%

commit v1 on v0

v1 whole, which is shorter than its diff:
```python
import functools

import jax
import jax.numpy as jnp
import numpy as np
from jax import lax
from jax.experimental import pallas as pl
from jax.experimental.pallas import tpu as pltpu
from jax.sharding import PartitionSpec as P

AXES = ("group", "inner")
PARTS = 4
GROUP = 8
F32 = jnp.float32
BF16 = jnp.bfloat16
ROWS_BY_ROWS = (((0,), (0,)), ((), ()))
COLS_BY_COLS = (((1,), (1,)), ((), ()))


def call(body, grid, in_specs, out_specs, out_shape, cost, scratch=()):
    return pl.pallas_call(
        body,
        grid=grid,
        in_specs=in_specs,
        out_specs=out_specs,
        out_shape=out_shape,
        scratch_shapes=list(scratch),
        compiler_params=pltpu.CompilerParams(
            dimension_semantics=("arbitrary",) * len(grid)
        ),
        cost_estimate=pl.CostEstimate(
            flops=cost[0], bytes_accessed=cost[1], transcendentals=0
        ),
    )


def whole(shape):
    return pl.BlockSpec(shape, lambda i: (0,) * len(shape))


def slots_body(experts, chunk, capacity, ids_f, sc_f, ids_b, sc_b, key_f, wgt_f, key_b, wgt_b):
    tok, top = ids_f.shape
    wide = PARTS * tok
    lane = lax.broadcasted_iota(jnp.int32, (tok, wide), 1)
    row = lax.broadcasted_iota(jnp.int32, (tok, wide), 0)
    spread = jnp.where(lane % tok == row, 1.0, 0.0)
    earlier = jnp.where(row < lane % tok, 1.0, 0.0).astype(BF16)
    label = lax.broadcasted_iota(jnp.int32, (experts, wide), 0)
    part = lax.broadcasted_iota(jnp.int32, (1, wide), 1) // tok
    for ids, sc, key, wgt in ((ids_f, sc_f, key_f, wgt_f), (ids_b, sc_b, key_b, wgt_b)):
        named = lax.dot_general(
            ids[...].astype(F32).astype(BF16), spread.astype(BF16), ROWS_BY_ROWS,
            preferred_element_type=F32,
        ).astype(jnp.int32)
        hits = [label == named[j : j + 1, :] for j in range(top)]
        chosen = jnp.zeros((experts, wide), F32)
        for hit in hits:
            chosen = chosen + jnp.where(hit, 1.0, 0.0)
        before = jnp.dot(
            chosen[:, :tok].astype(BF16), earlier, preferred_element_type=F32
        )
        for j in range(top):
            slot = jnp.sum(jnp.where(hits[j], before, 0.0), axis=0, keepdims=True)
            key[j : j + 1, :] = (
                named[j : j + 1, :] * chunk + part * capacity + slot.astype(jnp.int32)
            )
        share = lax.dot_general(
            sc[...], spread, ROWS_BY_ROWS,
            preferred_element_type=F32, precision=lax.Precision.HIGHEST,
        )
        wgt[...] = share / jnp.sum(share, axis=0, keepdims=True)


def slots(experts, capacity, ids_f, sc_f, ids_b, sc_b):
    tok, top = ids_f.shape
    small = (top, PARTS * tok)
    return call(
        functools.partial(slots_body, experts, PARTS * capacity, capacity),
        (1,),
        [whole((tok, top))] * 4,
        [whole(small)] * 4,
        [
            jax.ShapeDtypeStruct(small, jnp.int32),
            jax.ShapeDtypeStruct(small, F32),
        ]
        * 2,
        (10_000_000, 100_000),
    )(ids_f, sc_f, ids_b, sc_b)


def stacked(ref):
    step = ref.shape[1] // PARTS
    return jnp.concatenate([ref[:, q * step : (q + 1) * step] for q in range(PARTS)], axis=0)


def send_body(rows, weighted, key, wgt, *refs):
    *tables, out = refs
    top, wide = key.shape
    step = tables[0].shape[1] // PARTS
    mine = pl.program_id(0) * rows + lax.broadcasted_iota(jnp.int32, (rows, wide), 0)
    pick = jnp.zeros((rows, wide), F32)
    load = jnp.zeros((rows, wide), F32)
    for j in range(top):
        hit = mine == key[j : j + 1, :]
        pick = jnp.where(hit, 1.0, pick)
        if any(weighted):
            load = jnp.where(hit, wgt[j : j + 1, :], load)
    pick = pick.astype(BF16)
    scale = jnp.sum(load, axis=1, keepdims=True) if any(weighted) else None
    for i, table in enumerate(tables):
        got = jnp.dot(pick, stacked(table), preferred_element_type=F32)
        if weighted[i]:
            got = got * scale
        out[:, i * step : (i + 1) * step] = got.astype(BF16)


def send(total, key, wgt, tables, weighted):
    tok, width = tables[0].shape
    top, wide = key.shape
    n = len(tables)
    rows = total // 8
    return call(
        functools.partial(send_body, rows, weighted),
        (8,),
        [whole((top, wide))] * 2 + [whole((tok, width))] * n,
        pl.BlockSpec((rows, n * width // PARTS), lambda i: (i, 0)),
        jax.ShapeDtypeStruct((total, n * width // PARTS), BF16),
        (2 * total * wide * n * width // PARTS, 2 * total * n * width // PARTS),
    )(key, wgt, *tables)


def order(capacity):
    size = GROUP * PARTS * capacity
    matrix = np.zeros((size, size), np.float32)
    for s in range(GROUP):
        for q in range(PARTS):
            for c in range(capacity):
                matrix[(q * GROUP + s) * capacity + c, (s * PARTS + q) * capacity + c] = 1.0
    return matrix


def unpack_body(n, perm, got, *outs):
    step = got.shape[1] // n
    count = outs[0].shape[0]
    rows = jnp.dot(perm[...], got[...], preferred_element_type=F32).astype(BF16)
    for i, out in enumerate(outs):
        for q in range(PARTS):
            out[:, q * step : (q + 1) * step] = rows[
                q * count : (q + 1) * count, i * step : (i + 1) * step
            ]


def unpack(perm, got, n):
    size = perm.shape[0]
    total, wide = got.shape
    count = size // PARTS
    step = wide // n
    shape = (total // PARTS, PARTS * step)
    return call(
        functools.partial(unpack_body, n),
        (total // size,),
        [whole((size, size)), pl.BlockSpec((size, wide), lambda i: (i, 0))],
        [pl.BlockSpec((count, PARTS * step), lambda i: (i, 0))] * n,
        [jax.ShapeDtypeStruct(shape, BF16)] * n,
        (2 * total * size * wide, 4 * total * wide),
    )(perm, got)


def pack_body(perm, rows, out):
    out[...] = lax.dot_general(
        perm[...], stacked(rows), ROWS_BY_ROWS, preferred_element_type=F32
    ).astype(BF16)


def pack(perm, rows):
    size = perm.shape[0]
    total, width = rows.shape
    count = size // PARTS
    return call(
        pack_body,
        (total // count,),
        [whole((size, size)), pl.BlockSpec((count, width), lambda i: (i, 0))],
        pl.BlockSpec((size, width // PARTS), lambda i: (i, 0)),
        jax.ShapeDtypeStruct((total * PARTS, width // PARTS), BF16),
        (2 * total * size * width, 4 * total * width),
    )(perm, rows)


def combine_body(rows, weighted, key, wgt, got, out, total):
    top, wide = key.shape
    step = pl.program_id(0)
    mine = step * rows + lax.broadcasted_iota(jnp.int32, (rows, wide), 0)
    load = jnp.zeros((rows, wide), F32)
    for j in range(top):
        load = jnp.where(mine == key[j : j + 1, :], wgt[j : j + 1, :] if weighted else 1.0, load)
    high = load.astype(BF16)
    part = lax.dot_general(high, got[...], ROWS_BY_ROWS, preferred_element_type=F32)
    if weighted:
        low = (load - high.astype(F32)).astype(BF16)
        part = part + lax.dot_general(low, got[...], ROWS_BY_ROWS, preferred_element_type=F32)

    @pl.when(step == 0)
    def _():
        total[...] = part

    @pl.when(step > 0)
    def _():
        total[...] += part

    @pl.when(step == pl.num_programs(0) - 1)
    def _():
        tok, width = out.shape
        piece = width // PARTS
        for q in range(PARTS):
            out[:, q * piece : (q + 1) * piece] = total[q * tok : (q + 1) * tok, :].astype(BF16)


def combine(key, wgt, got, weighted):
    top, wide = key.shape
    count, piece = got.shape
    rows = count // 8
    tok = wide // PARTS
    return call(
        functools.partial(combine_body, rows, weighted),
        (8,),
        [whole((top, wide))] * 2 + [pl.BlockSpec((rows, piece), lambda i: (i, 0))],
        whole((tok, piece * PARTS)),
        jax.ShapeDtypeStruct((tok, piece * PARTS), BF16),
        (4 * count * wide * piece, 2 * count * piece),
        [pltpu.VMEM((wide, piece), F32)],
    )(key, wgt, got)


def exchange(x):
    return lax.all_to_all(x, AXES, split_axis=0, concat_axis=0, tiled=True)


def expert_forward(x, w_in, w_down):
    width = w_down.shape[0]
    projected = jnp.dot(x, w_in, preferred_element_type=F32)
    g, u = projected[:, :width], projected[:, width:]
    hidden = (g * jax.nn.sigmoid(g) * u).astype(BF16)
    return jnp.dot(hidden, w_down, preferred_element_type=F32).astype(BF16)


def expert_backward(x, cot, w_in, w_down):
    width = w_down.shape[0]
    projected = jnp.dot(x, w_in, preferred_element_type=F32)
    g, u = projected[:, :width], projected[:, width:]
    s = jax.nn.sigmoid(g)
    hidden = (g * s * u).astype(BF16)
    d_hidden = lax.dot_general(cot, w_down, COLS_BY_COLS, preferred_element_type=F32)
    d_gate = d_hidden * u * s * (1.0 + g * (1.0 - s))
    d_up = d_hidden * g * s
    d_proj = jnp.concatenate([d_gate, d_up], axis=1).astype(BF16)
    row_grad = lax.dot_general(
        d_proj, w_in, COLS_BY_COLS, preferred_element_type=F32
    ).astype(BF16)
    return row_grad, hidden, d_proj


def shards(
    tokens_fwd, experts_fwd, scores_fwd, tokens_bwd, experts_bwd, scores_bwd, cotangent, w_in, w_down
):
    devices = lax.axis_size("group") * lax.axis_size("inner")
    tok, top = experts_fwd.shape
    capacity = max(2, 3 * tok * top // (2 * devices))
    total = devices * capacity * PARTS
    perm = jnp.asarray(order(capacity), BF16)
    w_in, w_down = w_in[0], w_down[0]

    key_f, wgt_f, key_b, wgt_b = slots(
        devices, capacity, experts_fwd, scores_fwd, experts_bwd, scores_bwd
    )
    out_b = send(total, key_b, wgt_b, (tokens_bwd, cotangent), (False, True))
    in_b = exchange(out_b)
    out_f = send(total, key_f, wgt_f, (tokens_fwd,), (False,))
    out_f, in_b = lax.optimization_barrier((out_f, in_b))
    in_f = exchange(out_f)

    rows_b, cot_b = unpack(perm, in_b, 2)
    row_grad, hidden, d_proj = expert_backward(rows_b, cot_b, w_in, w_down)
    back_b = pack(perm, row_grad)
    back_b, in_f = lax.optimization_barrier((back_b, in_f))
    home_b = exchange(back_b)

    (rows_f,) = unpack(perm, in_f, 1)
    back_f = pack(perm, expert_forward(rows_f, w_in, w_down))
    grad_down = lax.dot_general(
        hidden, cot_b, ROWS_BY_ROWS, preferred_element_type=F32
    ).astype(BF16)
    grad_in = lax.dot_general(
        rows_b, d_proj, ROWS_BY_ROWS, preferred_element_type=F32
    ).astype(BF16)
    back_f, home_b = lax.optimization_barrier((back_f, home_b))
    home_f = exchange(back_f)

    grad_tokens = combine(key_b, wgt_b, home_b, False)
    output_fwd = combine(key_f, wgt_f, home_f, True)
    return output_fwd, grad_tokens, grad_in[None], grad_down[None]


def solution(mesh):
    rows = P(AXES, None)
    cube = P(AXES, None, None)
    return jax.shard_map(
        shards,
        mesh=mesh,
        in_specs=(rows,) * 7 + (cube,) * 2,
        out_specs=(rows, rows, cube, cube),
        check_vma=False,
    )
```

time: 515 us -> 267 us (0.52)
  local copies, waits for them, and re-layouts: 169 us -> 7.09 us
  waiting for transfers between devices: 205 us -> 91.5 us
  Pallas kernels: 0 us -> 77.4 us
  starting transfers between devices: 65.7 us -> 36.4 us
  other arithmetic: 12.5 us -> 0 us
    all_to_all x10 -> x4, waiting for transfers between devices: 205 us -> 91.5 us  [exchange(): return lax.all_to_all(x, AXES, split_axis=0, concat_axis=0, tiled=True)]
    reshape x15 -> x0, local copies, waits for them, and re-layouts: 97.6 us -> none  [the longest x2 12.8 us: shards(): send_bwd.reshape(shape_four)]
    pallas_call x0 -> x9, Pallas kernels: none -> 77.4 us  [the longest x2 23.4 us: unpack(): call(functools.partial(unpack_body, n), (total // size,), [whole((size, s...]
    gather x5 -> x0, local copies, waits for them, and re-layouts: 32.6 us -> none  [the longest x1 8.96 us: shards(): send_cot = cot_padded[assigned_bwd]]
    all_to_all x10 -> x4, starting transfers between devices: 65.7 us -> 36.4 us  [exchange(): return lax.all_to_all(x, AXES, split_axis=0, concat_axis=0, tiled=True)]
    all_to_all x5 -> x0, local copies, waits for them, and re-layouts: 26.5 us -> none  [the longest x1 5.32 us: shards(): lax.all_to_all(expert_out.reshape(shape_four), 'inner', split_axis=1, con...]
    reduce_sum x6 -> x0, other arithmetic: 9.05 us -> none  [the longest x1 4.14 us: shards(): jnp.sum(weights_fwd[:, :, None] * picked_out.astype(jnp.float32), axis=1)]
  transfers between devices with their start and end apart: 10 -> 4, of which waited for: 9 -> 3; matrix products, arithmetic and copies ran while one was open for 36% -> 19% of each run, Pallas kernels for 0% -> 23%
where the time goes in v1:
time: 267 us; the launch traced here: 263 us
  waiting for transfers between devices  91.5 us (34%)
  Pallas kernels  77.4 us (29%)
  matrix products  49.5 us (19%)
  starting transfers between devices  36.4 us (14%)
  local copies, waits for them, and re-layouts  7.09 us (3%)
    all_to_all x4, waiting for transfers between devices, exchange(): return lax.all_to_all(x, AXES, split_axis=0, concat_axis=0, tiled=True)  91.5 us
    all_to_all x4, starting transfers between devices, exchange(): return lax.all_to_all(x, AXES, split_axis=0, concat_axis=0, tiled=True)  36.4 us
    pallas_call x2, Pallas kernels, unpack(): call(functools.partial(unpack_body, n), (total // size,), [whole((size, s...  23.4 us
    pallas_call x2, Pallas kernels, pack(): call(pack_body, (total // count,), [whole((size, size)), pl.BlockSpec((co...  22.8 us
    pallas_call x2, Pallas kernels, combine(): call(functools.partial(combine_body, rows, weighted), (8,), [whole((top,...  15.7 us
    pallas_call x2, Pallas kernels, send(): call(functools.partial(send_body, rows, weighted), (8,), [whole((top, wid...  13.4 us
    dot_general x1, matrix products, expert_backward(): lax.dot_general(d_proj, w_in, COLS_BY_COLS, preferred_element_type=F32)  9.38 us
    dot_general x1, matrix products, expert_backward(): projected = jnp.dot(x, w_in, preferred_element_type=F32)  8.59 us
  transfers between devices with their start and end apart: 4, of which 3 were waited for; matrix products, arithmetic and copies ran while one was open for 19% of the time, Pallas kernels for 23%

profile of v1, /device:TPU:6, one launch (start us, length us, event | category | flops | bytes accessed | tf_op | source)
XLA Modules:
  0.0 262.6 jit_solution(6351245389492391087)
XLA Ops:
  0.6 0.0 copy-start
  0.6 1.5 copy.14.ids_f
  2.2 1.4 copy.15.sc_f
  3.6 1.4 copy.16.ids_b
  4.9 1.4 copy.17.sc_b
  6.3 2.2 shard_map.129
  8.5 7.5 %shard_map.131 = bf16[3072,1024]{1,0:T(8,128)(2,1)} custom-call(s32[8,256]{1,0:T(8,128)} %get-tuple-element.18.key, f32[8,256]{1,0:T(8,128)} %get-tuple-element.19.wgt, bf16[64,2048]{1,0:T(8,128)(2,1)} %refs_0_.3, bf16[64,2048]{1,0:T(8,128)(2,1)} %refs_1_.1), custom_call_target="tpu_custom_call" | custom-call | flops 1610612736 | bytes 6291456 | tf_op jit(solution)/shard_map/pallas_call | solution.py:122
  16.0 10.9 %all-to-all-start = ((bf16[128,24,1024]{2,1,0:T(8,128)(2,1)}), bf16[128,24,1024]{2,1,0:T(8,128)(2,1)}, u32[]{:S(2)}, u32[]{:S(2)}) async-start(bf16[128,24,1024]{2,1,0:T(8,128)(2,1)} %bitcast.33), calls=%async_computation | async-start | bytes 12582912 | tf_op jit(solution)/shard_map/all_to_all | solution.py:235
  26.9 5.8 %shard_map.130 = bf16[3072,512]{1,0:T(8,128)(2,1)} custom-call(s32[8,256]{1,0:T(8,128)} %get-tuple-element.16.key, f32[8,256]{1,0:T(8,128)} %get-tuple-element.17.wgt, bf16[64,2048]{1,0:T(8,128)(2,1)} %refs_0_.2), custom_call_target="tpu_custom_call" | custom-call | flops 805306368 | bytes 3145728 | tf_op jit(solution)/shard_map/pallas_call | solution.py:122
  32.7 69.9 %all-to-all-done = bf16[128,24,1024]{2,1,0:T(8,128)(2,1)} async-done(((bf16[128,24,1024]{2,1,0:T(8,128)(2,1)}), bf16[128,24,1024]{2,1,0:T(8,128)(2,1)}, u32[]{:S(2)}, u32[]{:S(2)}) %all-to-all-start) | async-done | bytes 6291488 | tf_op jit(solution)/shard_map/all_to_all | solution.py:235
  102.6 8.3 %all-to-all-start.1 = ((bf16[128,24,512]{2,1,0:T(8,128)(2,1)}), bf16[128,24,512]{2,1,0:T(8,128)(2,1)}, u32[]{:S(2)}, u32[]{:S(2)}) async-start(bf16[128,24,512]{2,1,0:T(8,128)(2,1)} %bitcast.34), calls=%async_computation.1 | async-start | bytes 6291456 | tf_op jit(solution)/shard_map/all_to_all | solution.py:235
  110.9 12.3 %shard_map.132 = (bf16[768,2048]{1,0:T(8,128)(2,1)}, bf16[768,2048]{1,0:T(8,128)(2,1)}) custom-call(bf16[192,192]{1,0:T(8,128)(2,1)} %constant.4.clone.perm, bf16[3072,1024]{1,0:T(8,128)(2,1)} %bitcast.1.got), custom_call_target="tpu_custom_call" | custom-call | flops 1207959552 | bytes 12582912 | tf_op jit(solution)/shard_map/pallas_call | solution.py:159
  123.2 8.6 %fusion.5 = f32[768,1536]{0,1:T(8,128)S(1)} fusion(bf16[768,2048]{1,0:T(8,128)(2,1)} %get-tuple-element.22, bf16[1,2048,1536]{2,1,0:T(8,128)(2,1)} %param.17), kind=kOutput, calls=%fused_computation.6 | convolution fusion | flops 4831838208 | bytes 14155776 | tf_op jit(solution)/shard_map/dot_general | solution.py:248
  131.8 0.0 copy-start.3
  131.8 3.3 %multiply_convert_fusion.2 = (bf16[768,768]{0,1:T(8,128)(2,1)S(1)}, bf16[768,768]{0,1:T(8,128)(2,1)S(1)}) fusion(f32[768,1536]{0,1:T(8,128)S(1)} %fusion.5, bf16[768,2048]{1,0:T(8,128)(2,1)S(1)} %copy-done.2, bf16[1,768,2048]{2,1,0:T(8,128)(2,1)S(1)} %copy-done), kind=kOutput, calls=%fused_computation.20 | convolution fusion | flops 2423586816 | bytes 13369344 | tf_op jit(solution)/shard_map/dot_general | solution.py:252
  135.2 1.0 copy-done.4
  136.2 0.3 copy-done.6
  136.5 9.4 %fusion.7.rows = bf16[768,2048]{1,0:T(8,128)(2,1)} fusion(bf16[1,2048,1536]{2,1,0:T(8,128)(2,1)} %param.17, bf16[768,768]{0,1:T(8,128)(2,1)S(1)} %get-tuple-element.29, bf16[768,768]{0,1:T(8,128)(2,1)S(1)} %get-tuple-element.28), kind=kOutput, calls=%fused_computation.10 | convolution fusion | flops 4838129664 | bytes 11796480 | tf_op jit(solution)/shard_map/dot_general | solution.py:256
  145.9 11.4 %shard_map.133 = bf16[3072,512]{1,0:T(8,128)(2,1)} custom-call(bf16[192,192]{1,0:T(8,128)(2,1)} %constant.4.clone.perm, bf16[768,2048]{1,0:T(8,128)(2,1)} %fusion.7.rows), custom_call_target="tpu_custom_call" | custom-call | flops 603979776 | bytes 6291456 | tf_op jit(solution)/shard_map/pallas_call | solution.py:179
  157.3 0.0 all-to-all-done.1
  157.3 10.2 %all-to-all-start.2 = ((bf16[128,24,512]{2,1,0:T(8,128)(2,1)}), bf16[128,24,512]{2,1,0:T(8,128)(2,1)}, u32[]{:S(2)}, u32[]{:S(2)}) async-start(bf16[128,24,512]{2,1,0:T(8,128)(2,1)} %bitcast.36), calls=%async_computation.2 | async-start | bytes 6291456 | tf_op jit(solution)/shard_map/all_to_all | solution.py:235
  167.5 11.1 %shard_map.134 = bf16[768,2048]{1,0:T(8,128)(2,1)} custom-call(bf16[192,192]{1,0:T(8,128)(2,1)} %constant.4.clone.perm, bf16[3072,512]{1,0:T(8,128)(2,1)} %bitcast.5.got), custom_call_target="tpu_custom_call" | custom-call | flops 603979776 | bytes 6291456 | tf_op jit(solution)/shard_map/pallas_call | solution.py:159
  178.6 8.5 %fusion.1 = f32[768,1536]{0,1:T(8,128)S(1)} fusion(bf16[768,2048]{1,0:T(8,128)(2,1)} %shard_map.134, bf16[1,2048,1536]{2,1,0:T(8,128)(2,1)} %param.17), kind=kOutput, calls=%fused_computation.2 | convolution fusion | flops 4831838208 | bytes 14155776 | tf_op jit(solution)/shard_map/dot_general | solution.py:240
  187.1 4.2 %convolution_convert_fusion.2.rows = bf16[768,2048]{1,0:T(8,128)(2,1)} fusion(bf16[1,768,2048]{2,1,0:T(8,128)(2,1)S(1)} %copy-done, f32[768,1536]{0,1:T(8,128)S(1)} %fusion.1), kind=kOutput, calls=%fused_computation.9 | convolution fusion | flops 2421030912 | bytes 11010048 | tf_op jit(solution)/shard_map/dot_general | solution.py:243
  191.3 11.4 %shard_map.135 = bf16[3072,512]{1,0:T(8,128)(2,1)} custom-call(bf16[192,192]{1,0:T(8,128)(2,1)} %constant.4.clone.perm, bf16[768,2048]{1,0:T(8,128)(2,1)} %convolution_convert_fusion.2.rows), custom_call_target="tpu_custom_call" | custom-call | flops 603979776 | bytes 6291456 | tf_op jit(solution)/shard_map/pallas_call | solution.py:179
  202.7 4.6 %all-to-all-done.2 = bf16[128,24,512]{2,1,0:T(8,128)(2,1)} async-done(((bf16[128,24,512]{2,1,0:T(8,128)(2,1)}), bf16[128,24,512]{2,1,0:T(8,128)(2,1)}, u32[]{:S(2)}, u32[]{:S(2)}) %all-to-all-start.2) | async-done | bytes 3145760 | tf_op jit(solution)/shard_map/all_to_all | solution.py:235
  207.3 7.1 %all-to-all-start.3 = ((bf16[128,24,512]{2,1,0:T(8,128)(2,1)}), bf16[128,24,512]{2,1,0:T(8,128)(2,1)}, u32[]{:S(2)}, u32[]{:S(2)}) async-start(bf16[128,24,512]{2,1,0:T(8,128)(2,1)} %bitcast.35), calls=%async_computation.3 | async-start | bytes 6291456 | tf_op jit(solution)/shard_map/all_to_all | solution.py:235
  214.4 7.8 %fusion.13 = bf16[1,768,2048]{2,1,0:T(8,128)(2,1)} fusion(bf16[768,2048]{1,0:T(8,128)(2,1)} %get-tuple-element.21, f32[768,1536]{0,1:T(8,128)} %copy-done.3), kind=kOutput, calls=%fused_computation.14 | convolution fusion | flops 2421030912 | bytes 11010048 | tf_op jit(solution)/shard_map/dot_general | solution.py:289
  222.2 7.8 %fusion = bf16[1,2048,1536]{2,1,0:T(8,128)(2,1)} fusion(bf16[768,2048]{1,0:T(8,128)(2,1)S(1)} %copy-done.1, bf16[768,768]{0,1:T(8,128)(2,1)S(1)} %copy-done.7, bf16[768,768]{0,1:T(8,128)(2,1)S(1)} %copy-done.5), kind=kOutput, calls=%fused_computation.1 | convolution fusion | flops 4839702528 | bytes 11796480 | tf_op jit(solution)/shard_map/dot_general | solution.py:292
  230.0 7.3 %shard_map.137 = bf16[64,2048]{1,0:T(8,128)(2,1)} custom-call(s32[8,256]{1,0:T(8,128)} %get-tuple-element.18.key, f32[8,256]{1,0:T(8,128)} %get-tuple-element.19.wgt, bf16[3072,512]{1,0:T(8,128)(2,1)} %bitcast.7.got), custom_call_target="tpu_custom_call" | custom-call | flops 1610612736 | bytes 3145728 | tf_op jit(solution)/shard_map/pallas_call | solution.py:223
  237.3 17.0 %all-to-all-done.3 = bf16[128,24,512]{2,1,0:T(8,128)(2,1)} async-done(((bf16[128,24,512]{2,1,0:T(8,128)(2,1)}), bf16[128,24,512]{2,1,0:T(8,128)(2,1)}, u32[]{:S(2)}, u32[]{:S(2)}) %all-to-all-start.3) | async-done | bytes 3145760 | tf_op jit(solution)/shard_map/all_to_all | solution.py:235
  254.3 8.3 %shard_map.136 = bf16[64,2048]{1,0:T(8,128)(2,1)} custom-call(s32[8,256]{1,0:T(8,128)} %get-tuple-element.16.key, f32[8,256]{1,0:T(8,128)} %get-tuple-element.17.wgt, bf16[3072,512]{1,0:T(8,128)(2,1)} %bitcast.9.got), custom_call_target="tpu_custom_call" | custom-call | flops 1610612736 | bytes 3145728 | tf_op jit(solution)/shard_map/pallas_call | solution.py:223
  (12 shorter events, 0.0 us)
Async XLA Ops:
  0.6 131.2 %copy-start = (bf16[1,768,2048]{2,1,0:T(8,128)(2,1)S(1)}, bf16[1,768,2048]{2,1,0:T(8,128)(2,1)}, u32[]{:S(2)}) copy-start(bf16[1,768,2048]{2,1,0:T(8,128)(2,1)} %param.18) | copy-start | bytes 9437188
  16.0 86.6 %all-to-all-start = ((bf16[128,24,1024]{2,1,0:T(8,128)(2,1)}), bf16[128,24,1024]{2,1,0:T(8,128)(2,1)}, u32[]{:S(2)}, u32[]{:S(2)}) async-start(bf16[128,24,1024]{2,1,0:T(8,128)(2,1)} %bitcast.33), calls=%async_computation | async-start | bytes 12582912 | tf_op jit(solution)/shard_map/all_to_all | solution.py:235
  102.6 54.7 %all-to-all-start.1 = ((bf16[128,24,512]{2,1,0:T(8,128)(2,1)}), bf16[128,24,512]{2,1,0:T(8,128)(2,1)}, u32[]{:S(2)}, u32[]{:S(2)}) async-start(bf16[128,24,512]{2,1,0:T(8,128)(2,1)} %bitcast.34), calls=%async_computation.1 | async-start | bytes 6291456 | tf_op jit(solution)/shard_map/all_to_all | solution.py:235
  123.2 8.6 %copy-start.2 = (bf16[768,2048]{1,0:T(8,128)(2,1)S(1)}, bf16[768,2048]{1,0:T(8,128)(2,1)}, u32[]{:S(2)}) copy-start(bf16[768,2048]{1,0:T(8,128)(2,1)} %get-tuple-element.21) | copy-start | bytes 9437188
  131.8 3.4 %copy-start.3 = (f32[768,1536]{0,1:T(8,128)}, f32[768,1536]{0,1:T(8,128)S(1)}, u32[]{:S(2)}) copy-start(f32[768,1536]{0,1:T(8,128)S(1)} %fusion.5) | copy-start | bytes 14155780
  135.2 1.0 copy-start.4
  135.2 1.4 copy-start.6
  157.3 50.0 %all-to-all-start.2 = ((bf16[128,24,512]{2,1,0:T(8,128)(2,1)}), bf16[128,24,512]{2,1,0:T(8,128)(2,1)}, u32[]{:S(2)}, u32[]{:S(2)}) async-start(bf16[128,24,512]{2,1,0:T(8,128)(2,1)} %bitcast.36), calls=%async_computation.2 | async-start | bytes 6291456 | tf_op jit(solution)/shard_map/all_to_all | solution.py:235
  207.3 47.0 %all-to-all-start.3 = ((bf16[128,24,512]{2,1,0:T(8,128)(2,1)}), bf16[128,24,512]{2,1,0:T(8,128)(2,1)}, u32[]{:S(2)}, u32[]{:S(2)}) async-start(bf16[128,24,512]{2,1,0:T(8,128)(2,1)} %bitcast.35), calls=%async_computation.3 | async-start | bytes 6291456 | tf_op jit(solution)/shard_map/all_to_all | solution.py:235
  214.4 7.8 %copy-start.1 = (bf16[768,2048]{1,0:T(8,128)(2,1)S(1)}, bf16[768,2048]{1,0:T(8,128)(2,1)}, u32[]{:S(2)}) copy-start(bf16[768,2048]{1,0:T(8,128)(2,1)} %get-tuple-element.22) | copy-start | bytes 9437188
  214.4 7.8 %copy-start.5 = (bf16[768,768]{0,1:T(8,128)(2,1)S(1)}, bf16[768,768]{0,1:T(8,128)(2,1)}, u32[]{:S(2)}) copy-start(bf16[768,768]{0,1:T(8,128)(2,1)} %copy-done.4) | copy-start | bytes 3538948
  214.4 7.8 %copy-start.7 = (bf16[768,768]{0,1:T(8,128)(2,1)S(1)}, bf16[768,768]{0,1:T(8,128)(2,1)}, u32[]{:S(2)}) copy-start(bf16[768,768]{0,1:T(8,128)(2,1)} %copy-done.6) | copy-start | bytes 3538948

commit v2 on v1

v2 whole, which is shorter than its diff:
```python
import functools

import jax
import jax.numpy as jnp
from jax import lax
from jax.experimental import pallas as pl
from jax.experimental.pallas import tpu as pltpu
from jax.sharding import PartitionSpec as P


AXES = ("group", "inner")
PARTS = 4
LANES = 128
F32 = jnp.float32
BF16 = jnp.bfloat16
ROWS_BY_ROWS = (((0,), (0,)), ((), ()))
COLS_BY_COLS = (((1,), (1,)), ((), ()))


def call(body, grid, in_specs, out_specs, out_shape, cost, scratch=()):
    return pl.pallas_call(
        body,
        grid=grid,
        in_specs=in_specs,
        out_specs=out_specs,
        out_shape=out_shape,
        scratch_shapes=list(scratch),
        compiler_params=pltpu.CompilerParams(
            dimension_semantics=("arbitrary",) * len(grid)
        ),
        cost_estimate=pl.CostEstimate(
            flops=cost[0], bytes_accessed=cost[1], transcendentals=0
        ),
    )


def whole(shape):
    return pl.BlockSpec(shape, lambda i: (0,) * len(shape))


def spread(pieces, q, rows):
    count, piece = rows.shape
    for k in range(piece // LANES):
        pieces[k, pl.ds(q, count, stride=PARTS), :] = rows[:, k * LANES : (k + 1) * LANES]


def collected(pieces, q, first, piece):
    count = pieces.shape[1] // PARTS
    return jnp.concatenate(
        [
            pieces[k, pl.ds(q, count, stride=PARTS), :]
            for k in range(first // LANES, (first + piece) // LANES)
        ],
        axis=1,
    ).astype(BF16)


def fill(pieces, chunks):
    for k in range(pieces.shape[0]):
        pieces[k] = chunks[:, k * LANES : (k + 1) * LANES].astype(F32)


def flush(pieces, out, first):
    for k in range(pieces.shape[0]):
        out[:, first + k * LANES : first + (k + 1) * LANES] = pieces[k].astype(BF16)


def place(experts, capacity, ids, sc, key, wgt):
    top, tok = ids.shape
    label = lax.broadcasted_iota(jnp.int32, (experts, tok), 0)
    hits = [label == ids[j : j + 1, :] for j in range(top)]
    chosen = jnp.zeros((experts, tok), F32)
    for hit in hits:
        chosen = jnp.where(hit, 1.0, chosen)
    earlier = lax.broadcasted_iota(jnp.int32, (tok, tok), 0) < lax.broadcasted_iota(
        jnp.int32, (tok, tok), 1
    )
    before = jnp.dot(
        chosen.astype(BF16),
        jnp.where(earlier, 1.0, 0.0).astype(BF16),
        preferred_element_type=F32,
    )
    for j in range(top):
        slot = jnp.sum(jnp.where(hits[j], before, 0.0), axis=0, keepdims=True)
        key[j : j + 1, :] = ids[j : j + 1, :] * capacity + slot.astype(jnp.int32)
    share = sc[...]
    wgt[...] = share / jnp.sum(share, axis=0, keepdims=True)


def send_body(experts, capacity, weighted, ids, sc, *refs):
    *tables, out, key, wgt, pieces = refs
    top, tok = ids.shape
    rows = out.shape[0] // PARTS
    piece = tables[0].shape[1] // PARTS

    @pl.when(pl.program_id(0) == 0)
    def _():
        place(experts, capacity, ids, sc, key, wgt)

    mine = pl.program_id(0) * rows + lax.broadcasted_iota(jnp.int32, (rows, tok), 0)
    pick = jnp.zeros((rows, tok), F32)
    load = jnp.zeros((rows, tok), F32)
    for j in range(top):
        hit = mine == key[j : j + 1, :]
        pick = jnp.where(hit, 1.0, pick)
        load = jnp.where(hit, wgt[j : j + 1, :], load)
    pick = pick.astype(BF16)
    scale = jnp.sum(load, axis=1, keepdims=True)
    for i, table in enumerate(tables):
        for q in range(PARTS):
            got = jnp.dot(
                pick, table[:, q * piece : (q + 1) * piece], preferred_element_type=F32
            )
            if weighted[i]:
                got = got * scale
            spread(pieces, q, got)
        flush(pieces, out, i * piece)


def send(experts, capacity, ids, sc, tables, weighted):
    tok, width = tables[0].shape
    n = len(tables)
    total = experts * capacity * PARTS
    piece = width // PARTS
    steps = 8
    return call(
        functools.partial(send_body, experts, capacity, weighted),
        (steps,),
        [whole(ids.shape)] * 2 + [whole((tok, width))] * n,
        [
            pl.BlockSpec((total // steps, n * piece), lambda i: (i, 0)),
            whole(ids.shape),
            whole(ids.shape),
        ],
        [
            jax.ShapeDtypeStruct((total, n * piece), BF16),
            jax.ShapeDtypeStruct(ids.shape, jnp.int32),
            jax.ShapeDtypeStruct(ids.shape, F32),
        ],
        (2 * total * tok * n * piece, 2 * total * n * piece),
        [pltpu.VMEM((piece // LANES, total // steps, LANES), F32)],
    )(ids, sc, *tables)


def unpack_body(n, got, *refs):
    *outs, pieces = refs
    piece = got.shape[1] // n
    fill(pieces, got)
    for i, out in enumerate(outs):
        for q in range(PARTS):
            out[:, q * piece : (q + 1) * piece] = collected(pieces, q, i * piece, piece)


def unpack(got, n):
    total, wide = got.shape
    steps = 8
    width = PARTS * wide // n
    return call(
        functools.partial(unpack_body, n),
        (steps,),
        [pl.BlockSpec((total // steps, wide), lambda i: (i, 0))],
        [pl.BlockSpec((total // PARTS // steps, width), lambda i: (i, 0))] * n,
        [jax.ShapeDtypeStruct((total // PARTS, width), BF16)] * n,
        (400 * total * wide, 4 * total * wide),
        [pltpu.VMEM((wide // LANES, total // steps, LANES), F32)],
    )(got)


def pack_body(rows, out, pieces):
    width = rows.shape[1]
    piece = width // PARTS
    for q in range(PARTS):
        spread(pieces, q, rows[:, q * piece : (q + 1) * piece].astype(F32))
    flush(pieces, out, 0)


def pack(rows):
    total, width = rows.shape
    steps = 8
    piece = width // PARTS
    count = total // steps
    return call(
        pack_body,
        (steps,),
        [pl.BlockSpec((count, width), lambda i: (i, 0))],
        pl.BlockSpec((count * PARTS, piece), lambda i: (i, 0)),
        jax.ShapeDtypeStruct((total * PARTS, piece), BF16),
        (400 * total * width, 4 * total * width),
        [pltpu.VMEM((piece // LANES, count * PARTS, LANES), F32)],
    )(rows)


def combine_body(weighted, key, wgt, got, out, total, pieces):
    top, tok = key.shape
    step = pl.program_id(0)
    rows = got.shape[0] // PARTS
    piece = got.shape[1]
    mine = step * rows + lax.broadcasted_iota(jnp.int32, (rows, tok), 0)
    load = jnp.zeros((rows, tok), F32)
    for j in range(top):
        load = jnp.where(mine == key[j : j + 1, :], wgt[j : j + 1, :] if weighted else 1.0, load)
    high = load.astype(BF16)
    low = (load - high.astype(F32)).astype(BF16)
    fill(pieces, got)

    @pl.when(step == 0)
    def _():
        total[...] = jnp.zeros_like(total)

    for q in range(PARTS):
        lanes = slice(q * piece, (q + 1) * piece)
        part = collected(pieces, q, 0, piece)
        more = lax.dot_general(high, part, ROWS_BY_ROWS, preferred_element_type=F32)
        if weighted:
            more = more + lax.dot_general(low, part, ROWS_BY_ROWS, preferred_element_type=F32)
        total[:, lanes] += more

    @pl.when(step == pl.num_programs(0) - 1)
    def _():
        out[...] = total[...].astype(BF16)


def combine(key, wgt, got, weighted):
    top, tok = key.shape
    count, piece = got.shape
    steps = 4
    rows = count // steps
    return call(
        functools.partial(combine_body, weighted),
        (steps,),
        [whole((top, tok))] * 2 + [pl.BlockSpec((rows, piece), lambda i: (i, 0))],
        whole((tok, piece * PARTS)),
        jax.ShapeDtypeStruct((tok, piece * PARTS), BF16),
        (4 * count * tok * piece, 2 * count * piece),
        [pltpu.VMEM((tok, piece * PARTS), F32), pltpu.VMEM((piece // LANES, rows, LANES), F32)],
    )(key, wgt, got)


def exchange(x):
    return lax.all_to_all(x, AXES, split_axis=0, concat_axis=0, tiled=True)


def expert_forward(x, w_in, w_down):
    width = w_down.shape[0]
    projected = jnp.dot(x, w_in, preferred_element_type=F32)
    g, u = projected[:, :width], projected[:, width:]
    hidden = (g * jax.nn.sigmoid(g) * u).astype(BF16)
    return jnp.dot(hidden, w_down, preferred_element_type=F32).astype(BF16)


def expert_backward(x, cot, w_in, w_down):
    width = w_down.shape[0]
    projected = jnp.dot(x, w_in, preferred_element_type=F32)
    g, u = projected[:, :width], projected[:, width:]
    s = jax.nn.sigmoid(g)
    hidden = (g * s * u).astype(BF16)
    d_hidden = lax.dot_general(cot, w_down, COLS_BY_COLS, preferred_element_type=F32)
    d_gate = d_hidden * u * s * (1.0 + g * (1.0 - s))
    d_up = d_hidden * g * s
    d_proj = jnp.concatenate([d_gate, d_up], axis=1).astype(BF16)
    row_grad = lax.dot_general(
        d_proj, w_in, COLS_BY_COLS, preferred_element_type=F32
    ).astype(BF16)
    return row_grad, hidden, d_proj


def layer(
    tokens_fwd, experts_fwd, scores_fwd, tokens_bwd, experts_bwd, scores_bwd, cotangent, w_in, w_down
):
    devices = lax.axis_size("group") * lax.axis_size("inner")
    tok, top = experts_fwd.shape
    capacity = max(2, 3 * tok * top // (2 * devices))
    w_in, w_down = w_in[0], w_down[0]

    out_b, key_b, wgt_b = send(
        devices, capacity, experts_bwd.T, scores_bwd.T, (tokens_bwd, cotangent), (False, True)
    )
    in_b = exchange(out_b)
    out_f, key_f, wgt_f = send(
        devices, capacity, experts_fwd.T, scores_fwd.T, (tokens_fwd,), (False,)
    )
    out_f, in_b = lax.optimization_barrier((out_f, in_b))
    in_f = exchange(out_f)

    rows_b, cot_b = unpack(in_b, 2)
    row_grad, hidden, d_proj = expert_backward(rows_b, cot_b, w_in, w_down)
    back_b = pack(row_grad)
    back_b, in_f = lax.optimization_barrier((back_b, in_f))
    home_b = exchange(back_b)

    (rows_f,) = unpack(in_f, 1)
    back_f = pack(expert_forward(rows_f, w_in, w_down))
    grad_down = lax.dot_general(
        hidden, cot_b, ROWS_BY_ROWS, preferred_element_type=F32
    ).astype(BF16)
    grad_in = lax.dot_general(
        rows_b, d_proj, ROWS_BY_ROWS, preferred_element_type=F32
    ).astype(BF16)
    back_f, home_b = lax.optimization_barrier((back_f, home_b))
    home_f = exchange(back_f)

    grad_tokens = combine(key_b, wgt_b, home_b, False)
    output_fwd = combine(key_f, wgt_f, home_f, True)
    return output_fwd, grad_tokens, grad_in[None], grad_down[None]


def solution(mesh):
    rows = P(AXES, None)
    cube = P(AXES, None, None)
    return jax.shard_map(
        layer,
        mesh=mesh,
        in_specs=(rows,) * 7 + (cube,) * 2,
        out_specs=(rows, rows, cube, cube),
        check_vma=False,
    )
```

time: 267 us -> 254 us (0.951)
  Pallas kernels: 77.4 us -> 50.5 us
  waiting for transfers between devices: 91.5 us -> 114 us
  local copies, waits for them, and re-layouts: 7.09 us -> 1.43 us
  starting transfers between devices: 36.4 us -> 33.3 us
    pallas_call x9 -> x8, Pallas kernels: 77.4 us -> 50.5 us  [the longest x2 14.6 us: unpack(): call(functools.partial(unpack_body, n), (steps,), [pl.BlockSpec((total //...]
    all_to_all x4, waiting for transfers between devices: 91.5 us -> 114 us  [exchange(): return lax.all_to_all(x, AXES, split_axis=0, concat_axis=0, tiled=True)]
    unnamed x20 -> x16, local copies, waits for them, and re-layouts: 7.09 us -> 1.43 us
    all_to_all x4, starting transfers between devices: 36.4 us -> 33.3 us  [exchange(): return lax.all_to_all(x, AXES, split_axis=0, concat_axis=0, tiled=True)]
  transfers between devices with their start and end apart: 4 -> 4, of which waited for: 3 -> 4; matrix products, arithmetic and copies ran while one was open for 19% -> 20% of each run, Pallas kernels for 23% -> 12%
where the time goes in v2:
time: 254 us; the launch traced here: 250 us
  waiting for transfers between devices  114 us (45%)
  Pallas kernels  50.5 us (20%)
  matrix products  49.5 us (19%)
  starting transfers between devices  33.3 us (13%)
    all_to_all x4, waiting for transfers between devices, exchange(): return lax.all_to_all(x, AXES, split_axis=0, concat_axis=0, tiled=True)  114 us
    all_to_all x4, starting transfers between devices, exchange(): return lax.all_to_all(x, AXES, split_axis=0, concat_axis=0, tiled=True)  33.3 us
    pallas_call x2, Pallas kernels, unpack(): call(functools.partial(unpack_body, n), (steps,), [pl.BlockSpec((total //...  14.6 us
    pallas_call x2, Pallas kernels, pack(): call(pack_body, (steps,), [pl.BlockSpec((count, width), lambda i: (i, 0))...  13.3 us
    pallas_call x2, Pallas kernels, send(): call(functools.partial(send_body, experts, capacity, weighted), (steps,),...  13.2 us
    pallas_call x2, Pallas kernels, combine(): call(functools.partial(combine_body, weighted), (steps,), [whole((top, to...  9.56 us
    dot_general x1, matrix products, expert_backward(): lax.dot_general(d_proj, w_in, COLS_BY_COLS, preferred_element_type=F32)  9.37 us
    dot_general x1, matrix products, expert_backward(): projected = jnp.dot(x, w_in, preferred_element_type=F32)  8.6 us
  transfers between devices with their start and end apart: 4, of which 4 were waited for; matrix products, arithmetic and copies ran while one was open for 20% of the time, Pallas kernels for 12%

profile of v2, /device:TPU:6, one launch (start us, length us, event | category | flops | bytes accessed | tf_op | source)
XLA Modules:
  0.0 249.9 jit_solution(15618764661216634777)
XLA Ops:
  0.6 0.0 copy-start
  0.6 7.4 %shard_map.121 = (bf16[3072,1024]{1,0:T(8,128)(2,1)}, s32[8,64]{1,0:T(8,128)}, f32[8,64]{1,0:T(8,128)}) custom-call(s32[8,64]{1,0:T(8,128)} %bitcast.41, f32[8,64]{1,0:T(8,128)} %bitcast.42, bf16[64,2048]{1,0:T(8,128)(2,1)} %refs_0_.3, bf16[64,2048]{1,0:T(8,128)(2,1)} %refs_1_.1), custom_call_target="tpu_custom_call" | custom-call | flops 402653184 | bytes 6291456 | tf_op jit(solution)/shard_map/pallas_call | solution.py:126
  8.1 10.9 %all-to-all-start = ((bf16[128,24,1024]{2,1,0:T(8,128)(2,1)}), bf16[128,24,1024]{2,1,0:T(8,128)(2,1)}, u32[]{:S(2)}, u32[]{:S(2)}) async-start(bf16[128,24,1024]{2,1,0:T(8,128)(2,1)} %bitcast.39), calls=%async_computation | async-start | bytes 12582912 | tf_op jit(solution)/shard_map/all_to_all | solution.py:240
  19.0 5.7 %shard_map.120 = (bf16[3072,512]{1,0:T(8,128)(2,1)}, s32[8,64]{1,0:T(8,128)}, f32[8,64]{1,0:T(8,128)}) custom-call(s32[8,64]{1,0:T(8,128)} %bitcast.43, f32[8,64]{1,0:T(8,128)} %bitcast.44, bf16[64,2048]{1,0:T(8,128)(2,1)} %refs_0_.2), custom_call_target="tpu_custom_call" | custom-call | flops 201326592 | bytes 3145728 | tf_op jit(solution)/shard_map/pallas_call | solution.py:126
  24.7 70.0 %all-to-all-done = bf16[128,24,1024]{2,1,0:T(8,128)(2,1)} async-done(((bf16[128,24,1024]{2,1,0:T(8,128)(2,1)}), bf16[128,24,1024]{2,1,0:T(8,128)(2,1)}, u32[]{:S(2)}, u32[]{:S(2)}) %all-to-all-start) | async-done | bytes 6291488 | tf_op jit(solution)/shard_map/all_to_all | solution.py:240
  94.7 8.2 %shard_map.122 = (bf16[768,2048]{1,0:T(8,128)(2,1)}, bf16[768,2048]{1,0:T(8,128)(2,1)}) custom-call(bf16[3072,1024]{1,0:T(8,128)(2,1)} %bitcast.5.got), custom_call_target="tpu_custom_call" | custom-call | flops 1258291200 | bytes 12582912 | tf_op jit(solution)/shard_map/pallas_call | solution.py:158
  102.9 8.3 %all-to-all-start.1 = ((bf16[128,24,512]{2,1,0:T(8,128)(2,1)}), bf16[128,24,512]{2,1,0:T(8,128)(2,1)}, u32[]{:S(2)}, u32[]{:S(2)}) async-start(bf16[128,24,512]{2,1,0:T(8,128)(2,1)} %bitcast.40), calls=%async_computation.1 | async-start | bytes 6291456 | tf_op jit(solution)/shard_map/all_to_all | solution.py:240
  111.1 0.0 copy-start.2
  111.1 8.6 %fusion.5 = f32[768,1536]{0,1:T(8,128)S(1)} fusion(bf16[768,2048]{1,0:T(8,128)(2,1)} %get-tuple-element.24, bf16[1,2048,1536]{2,1,0:T(8,128)(2,1)} %param.16), kind=kOutput, calls=%fused_computation.6 | convolution fusion | flops 4831838208 | bytes 14155776 | tf_op jit(solution)/shard_map/dot_general | solution.py:253
  119.8 0.0 copy-start.3
  119.8 0.0 copy-done
  119.8 3.3 %multiply_convert_fusion.2 = (bf16[768,768]{0,1:T(8,128)(2,1)S(1)}, bf16[768,768]{0,1:T(8,128)(2,1)S(1)}) fusion(f32[768,1536]{0,1:T(8,128)S(1)} %fusion.5, bf16[768,2048]{1,0:T(8,128)(2,1)S(1)} %copy-done.2, bf16[1,768,2048]{2,1,0:T(8,128)(2,1)S(1)} %copy-done), kind=kOutput, calls=%fused_computation.20 | convolution fusion | flops 2423586816 | bytes 13369344 | tf_op jit(solution)/shard_map/dot_general | solution.py:257
  123.1 0.0 copy-done.3
  123.1 0.0 copy-start.4
  123.1 0.0 copy-start.6
  123.1 1.0 copy-done.4
  124.1 0.4 copy-done.6
  124.5 9.4 %fusion.7.rows = bf16[768,2048]{1,0:T(8,128)(2,1)} fusion(bf16[1,2048,1536]{2,1,0:T(8,128)(2,1)} %param.16, bf16[768,768]{0,1:T(8,128)(2,1)S(1)} %get-tuple-element.33, bf16[768,768]{0,1:T(8,128)(2,1)S(1)} %get-tuple-element.32), kind=kOutput, calls=%fused_computation.10 | convolution fusion | flops 4838129664 | bytes 11796480 | tf_op jit(solution)/shard_map/dot_general | solution.py:261
  133.9 6.7 %shard_map.123 = bf16[3072,512]{1,0:T(8,128)(2,1)} custom-call(bf16[768,2048]{1,0:T(8,128)(2,1)} %fusion.7.rows), custom_call_target="tpu_custom_call" | custom-call | flops 629145600 | bytes 6291456 | tf_op jit(solution)/shard_map/pallas_call | solution.py:182
  140.5 10.4 %all-to-all-done.1 = bf16[128,24,512]{2,1,0:T(8,128)(2,1)} async-done(((bf16[128,24,512]{2,1,0:T(8,128)(2,1)}), bf16[128,24,512]{2,1,0:T(8,128)(2,1)}, u32[]{:S(2)}, u32[]{:S(2)}) %all-to-all-start.1) | async-done | bytes 3145760 | tf_op jit(solution)/shard_map/all_to_all | solution.py:240
  150.9 7.1 %all-to-all-start.2 = ((bf16[128,24,512]{2,1,0:T(8,128)(2,1)}), bf16[128,24,512]{2,1,0:T(8,128)(2,1)}, u32[]{:S(2)}, u32[]{:S(2)}) async-start(bf16[128,24,512]{2,1,0:T(8,128)(2,1)} %bitcast.38), calls=%async_computation.2 | async-start | bytes 6291456 | tf_op jit(solution)/shard_map/all_to_all | solution.py:240
  158.0 6.4 %shard_map.124 = bf16[768,2048]{1,0:T(8,128)(2,1)} custom-call(bf16[3072,512]{1,0:T(8,128)(2,1)} %bitcast.9.got), custom_call_target="tpu_custom_call" | custom-call | flops 629145600 | bytes 6291456 | tf_op jit(solution)/shard_map/pallas_call | solution.py:158
  164.4 8.4 %fusion.1 = f32[768,1536]{0,1:T(8,128)S(1)} fusion(bf16[768,2048]{1,0:T(8,128)(2,1)} %shard_map.124, bf16[1,2048,1536]{2,1,0:T(8,128)(2,1)} %param.16), kind=kOutput, calls=%fused_computation.2 | convolution fusion | flops 4831838208 | bytes 14155776 | tf_op jit(solution)/shard_map/dot_general | solution.py:245
  172.9 4.2 %convolution_convert_fusion.2.rows = bf16[768,2048]{1,0:T(8,128)(2,1)} fusion(bf16[1,768,2048]{2,1,0:T(8,128)(2,1)S(1)} %copy-done, f32[768,1536]{0,1:T(8,128)S(1)} %fusion.1), kind=kOutput, calls=%fused_computation.9 | convolution fusion | flops 2421030912 | bytes 11010048 | tf_op jit(solution)/shard_map/dot_general | solution.py:248
  177.0 6.6 %shard_map.125 = bf16[3072,512]{1,0:T(8,128)(2,1)} custom-call(bf16[768,2048]{1,0:T(8,128)(2,1)} %convolution_convert_fusion.2.rows), custom_call_target="tpu_custom_call" | custom-call | flops 629145600 | bytes 6291456 | tf_op jit(solution)/shard_map/pallas_call | solution.py:182
  183.7 14.2 %all-to-all-done.2 = bf16[128,24,512]{2,1,0:T(8,128)(2,1)} async-done(((bf16[128,24,512]{2,1,0:T(8,128)(2,1)}), bf16[128,24,512]{2,1,0:T(8,128)(2,1)}, u32[]{:S(2)}, u32[]{:S(2)}) %all-to-all-start.2) | async-done | bytes 3145760 | tf_op jit(solution)/shard_map/all_to_all | solution.py:240
  197.9 7.1 %all-to-all-start.3 = ((bf16[128,24,512]{2,1,0:T(8,128)(2,1)}), bf16[128,24,512]{2,1,0:T(8,128)(2,1)}, u32[]{:S(2)}, u32[]{:S(2)}) async-start(bf16[128,24,512]{2,1,0:T(8,128)(2,1)} %bitcast.37), calls=%async_computation.3 | async-start | bytes 6291456 | tf_op jit(solution)/shard_map/all_to_all | solution.py:240
  205.0 7.8 %fusion.13 = bf16[1,768,2048]{2,1,0:T(8,128)(2,1)} fusion(bf16[768,2048]{1,0:T(8,128)(2,1)} %get-tuple-element.23, f32[768,1536]{0,1:T(8,128)} %copy-done.3), kind=kOutput, calls=%fused_computation.14 | convolution fusion | flops 2421030912 | bytes 11010048 | tf_op jit(solution)/shard_map/dot_general | solution.py:293
  212.8 7.8 %fusion = bf16[1,2048,1536]{2,1,0:T(8,128)(2,1)} fusion(bf16[768,2048]{1,0:T(8,128)(2,1)S(1)} %copy-done.1, bf16[768,768]{0,1:T(8,128)(2,1)S(1)} %copy-done.7, bf16[768,768]{0,1:T(8,128)(2,1)S(1)} %copy-done.5), kind=kOutput, calls=%fused_computation.1 | convolution fusion | flops 4839702528 | bytes 11796480 | tf_op jit(solution)/shard_map/dot_general | solution.py:296
  220.6 4.5 %shard_map.127 = bf16[64,2048]{1,0:T(8,128)(2,1)} custom-call(s32[8,64]{1,0:T(8,128)} %get-tuple-element.29.key, f32[8,64]{1,0:T(8,128)} %get-tuple-element.30.wgt, bf16[3072,512]{1,0:T(8,128)(2,1)} %bitcast.11.got), custom_call_target="tpu_custom_call" | custom-call | flops 402653184 | bytes 3145728 | tf_op jit(solution)/shard_map/pallas_call | solution.py:228
  225.1 19.8 %all-to-all-done.3 = bf16[128,24,512]{2,1,0:T(8,128)(2,1)} async-done(((bf16[128,24,512]{2,1,0:T(8,128)(2,1)}), bf16[128,24,512]{2,1,0:T(8,128)(2,1)}, u32[]{:S(2)}, u32[]{:S(2)}) %all-to-all-start.3) | async-done | bytes 3145760 | tf_op jit(solution)/shard_map/all_to_all | solution.py:240
  244.9 5.0 %shard_map.126 = bf16[64,2048]{1,0:T(8,128)(2,1)} custom-call(s32[8,64]{1,0:T(8,128)} %get-tuple-element.18.key, f32[8,64]{1,0:T(8,128)} %get-tuple-element.19.wgt, bf16[3072,512]{1,0:T(8,128)(2,1)} %bitcast.13.got), custom_call_target="tpu_custom_call" | custom-call | flops 402653184 | bytes 3145728 | tf_op jit(solution)/shard_map/pallas_call | solution.py:228
  (7 shorter events, 0.0 us)
Async XLA Ops:
  0.6 119.1 %copy-start = (bf16[1,768,2048]{2,1,0:T(8,128)(2,1)S(1)}, bf16[1,768,2048]{2,1,0:T(8,128)(2,1)}, u32[]{:S(2)}) copy-start(bf16[1,768,2048]{2,1,0:T(8,128)(2,1)} %param.17) | copy-start | bytes 9437188
  8.1 86.6 %all-to-all-start = ((bf16[128,24,1024]{2,1,0:T(8,128)(2,1)}), bf16[128,24,1024]{2,1,0:T(8,128)(2,1)}, u32[]{:S(2)}, u32[]{:S(2)}) async-start(bf16[128,24,1024]{2,1,0:T(8,128)(2,1)} %bitcast.39), calls=%async_computation | async-start | bytes 12582912 | tf_op jit(solution)/shard_map/all_to_all | solution.py:240
  102.9 48.1 %all-to-all-start.1 = ((bf16[128,24,512]{2,1,0:T(8,128)(2,1)}), bf16[128,24,512]{2,1,0:T(8,128)(2,1)}, u32[]{:S(2)}, u32[]{:S(2)}) async-start(bf16[128,24,512]{2,1,0:T(8,128)(2,1)} %bitcast.40), calls=%async_computation.1 | async-start | bytes 6291456 | tf_op jit(solution)/shard_map/all_to_all | solution.py:240
  111.1 8.6 %copy-start.2 = (bf16[768,2048]{1,0:T(8,128)(2,1)S(1)}, bf16[768,2048]{1,0:T(8,128)(2,1)}, u32[]{:S(2)}) copy-start(bf16[768,2048]{1,0:T(8,128)(2,1)} %get-tuple-element.23) | copy-start | bytes 9437188
  119.8 3.3 %copy-start.3 = (f32[768,1536]{0,1:T(8,128)}, f32[768,1536]{0,1:T(8,128)S(1)}, u32[]{:S(2)}) copy-start(f32[768,1536]{0,1:T(8,128)S(1)} %fusion.5) | copy-start | bytes 14155780
  123.1 1.0 copy-start.4
  123.1 1.4 copy-start.6
  150.9 47.0 %all-to-all-start.2 = ((bf16[128,24,512]{2,1,0:T(8,128)(2,1)}), bf16[128,24,512]{2,1,0:T(8,128)(2,1)}, u32[]{:S(2)}, u32[]{:S(2)}) async-start(bf16[128,24,512]{2,1,0:T(8,128)(2,1)} %bitcast.38), calls=%async_computation.2 | async-start | bytes 6291456 | tf_op jit(solution)/shard_map/all_to_all | solution.py:240
  197.9 47.0 %all-to-all-start.3 = ((bf16[128,24,512]{2,1,0:T(8,128)(2,1)}), bf16[128,24,512]{2,1,0:T(8,128)(2,1)}, u32[]{:S(2)}, u32[]{:S(2)}) async-start(bf16[128,24,512]{2,1,0:T(8,128)(2,1)} %bitcast.37), calls=%async_computation.3 | async-start | bytes 6291456 | tf_op jit(solution)/shard_map/all_to_all | solution.py:240
  205.0 7.8 %copy-start.1 = (bf16[768,2048]{1,0:T(8,128)(2,1)S(1)}, bf16[768,2048]{1,0:T(8,128)(2,1)}, u32[]{:S(2)}) copy-start(bf16[768,2048]{1,0:T(8,128)(2,1)} %get-tuple-element.24) | copy-start | bytes 9437188
  205.0 7.8 %copy-start.5 = (bf16[768,768]{0,1:T(8,128)(2,1)S(1)}, bf16[768,768]{0,1:T(8,128)(2,1)}, u32[]{:S(2)}) copy-start(bf16[768,768]{0,1:T(8,128)(2,1)} %copy-done.4) | copy-start | bytes 3538948
  205.0 7.8 %copy-start.7 = (bf16[768,768]{0,1:T(8,128)(2,1)S(1)}, bf16[768,768]{0,1:T(8,128)(2,1)}, u32[]{:S(2)}) copy-start(bf16[768,768]{0,1:T(8,128)(2,1)} %copy-done.6) | copy-start | bytes 3538948

commit v3 on v2

--- a/solution.py
+++ b/solution.py
@@ -122,7 +122,7 @@
     n = len(tables)
     total = experts * capacity * PARTS
     piece = width // PARTS
-    steps = 8
+    steps = 2
     return call(
         functools.partial(send_body, experts, capacity, weighted),
         (steps,),
@@ -153,7 +153,7 @@
 
 def unpack(got, n):
     total, wide = got.shape
-    steps = 8
+    steps = 2
     width = PARTS * wide // n
     return call(
         functools.partial(unpack_body, n),
@@ -176,7 +176,7 @@
 
 def pack(rows):
     total, width = rows.shape
-    steps = 8
+    steps = 2
     piece = width // PARTS
     count = total // steps
     return call(
@@ -223,7 +223,7 @@
 def combine(key, wgt, got, weighted):
     top, tok = key.shape
     count, piece = got.shape
-    steps = 4
+    steps = 2
     rows = count // steps
     return call(
         functools.partial(combine_body, weighted),
@@ -272,35 +272,35 @@
     capacity = max(2, 3 * tok * top // (2 * devices))
     w_in, w_down = w_in[0], w_down[0]
 
+    out_f, key_f, wgt_f = send(
+        devices, capacity, experts_fwd.T, scores_fwd.T, (tokens_fwd,), (False,)
+    )
+    in_f = exchange(out_f)
     out_b, key_b, wgt_b = send(
         devices, capacity, experts_bwd.T, scores_bwd.T, (tokens_bwd, cotangent), (False, True)
     )
+    out_b, in_f = lax.optimization_barrier((out_b, in_f))
     in_b = exchange(out_b)
-    out_f, key_f, wgt_f = send(
-        devices, capacity, experts_fwd.T, scores_fwd.T, (tokens_fwd,), (False,)
-    )
-    out_f, in_b = lax.optimization_barrier((out_f, in_b))
-    in_f = exchange(out_f)
+
+    (rows_f,) = unpack(in_f, 1)
+    back_f = pack(expert_forward(rows_f, w_in, w_down))
+    back_f, in_b = lax.optimization_barrier((back_f, in_b))
+    home_f = exchange(back_f)
 
     rows_b, cot_b = unpack(in_b, 2)
     row_grad, hidden, d_proj = expert_backward(rows_b, cot_b, w_in, w_down)
     back_b = pack(row_grad)
-    back_b, in_f = lax.optimization_barrier((back_b, in_f))
+    back_b, home_f = lax.optimization_barrier((back_b, home_f))
     home_b = exchange(back_b)
 
-    (rows_f,) = unpack(in_f, 1)
-    back_f = pack(expert_forward(rows_f, w_in, w_down))
+    output_fwd = combine(key_f, wgt_f, home_f, True)
     grad_down = lax.dot_general(
         hidden, cot_b, ROWS_BY_ROWS, preferred_element_type=F32
     ).astype(BF16)
     grad_in = lax.dot_general(
         rows_b, d_proj, ROWS_BY_ROWS, preferred_element_type=F32
     ).astype(BF16)
-    back_f, home_b = lax.optimization_barrier((back_f, home_b))
-    home_f = exchange(back_f)
-
     grad_tokens = combine(key_b, wgt_b, home_b, False)
-    output_fwd = combine(key_f, wgt_f, home_f, True)
     return output_fwd, grad_tokens, grad_in[None], grad_down[None]
 
 

time: 254 us -> 247 us (0.972)
  Pallas kernels: 50.5 us -> 36.8 us
  waiting for transfers between devices: 114 us -> 126 us
  matrix products: 49.5 us -> 45.1 us
    all_to_all x4, waiting for transfers between devices: 114 us -> 126 us  [exchange(): return lax.all_to_all(x, AXES, split_axis=0, concat_axis=0, tiled=True)]
    pallas_call x2, Pallas kernels: 13.3 us -> 7.98 us  [pack(): call(pack_body, (steps,), [pl.BlockSpec((count, width), lambda i: (i, 0))...]
    pallas_call x2, Pallas kernels: 14.6 us -> 9.78 us  [unpack(): call(functools.partial(unpack_body, n), (steps,), [pl.BlockSpec((total //...]
    dot_general x1, matrix products: 9.37 us -> 6.41 us  [expert_backward(): lax.dot_general(d_proj, w_in, COLS_BY_COLS, preferred_element_type=F32)]
    pallas_call x2, Pallas kernels: 13.2 us -> 10.4 us  [send(): call(functools.partial(send_body, experts, capacity, weighted), (steps,),...]
  transfers between devices with their start and end apart: 4 -> 4, of which waited for: 4 -> 4; matrix products, arithmetic and copies ran while one was open for 20% -> 19% of each run, Pallas kernels for 12% -> 9%
where the time goes in v3:
time: 247 us; the launch traced here: 244 us
  waiting for transfers between devices  126 us (51%)
  matrix products  45.1 us (18%)
  Pallas kernels  36.8 us (15%)
  starting transfers between devices  33.4 us (14%)
    all_to_all x4, waiting for transfers between devices, exchange(): return lax.all_to_all(x, AXES, split_axis=0, concat_axis=0, tiled=True)  126 us
    all_to_all x4, starting transfers between devices, exchange(): return lax.all_to_all(x, AXES, split_axis=0, concat_axis=0, tiled=True)  33.4 us
    pallas_call x2, Pallas kernels, send(): call(functools.partial(send_body, experts, capacity, weighted), (steps,),...  10.4 us
    pallas_call x2, Pallas kernels, unpack(): call(functools.partial(unpack_body, n), (steps,), [pl.BlockSpec((total //...  9.78 us
    pallas_call x2, Pallas kernels, combine(): call(functools.partial(combine_body, weighted), (steps,), [whole((top, to...  8.67 us
    dot_general x1, matrix products, expert_backward(): projected = jnp.dot(x, w_in, preferred_element_type=F32)  8.23 us
    dot_general x1, matrix products, expert_forward(): projected = jnp.dot(x, w_in, preferred_element_type=F32)  8.08 us
    pallas_call x2, Pallas kernels, pack(): call(pack_body, (steps,), [pl.BlockSpec((count, width), lambda i: (i, 0))...  7.98 us
  transfers between devices with their start and end apart: 4, of which 4 were waited for; matrix products, arithmetic and copies ran while one was open for 19% of the time, Pallas kernels for 9%

profile of v3, /device:TPU:6, one launch (start us, length us, event | category | flops | bytes accessed | tf_op | source)
XLA Modules:
  0.0 243.6 jit_solution(8764812338566354538)
XLA Ops:
  0.6 0.0 copy-start
  0.6 4.1 %shard_map.120 = (bf16[3072,512]{1,0:T(8,128)(2,1)}, s32[8,64]{1,0:T(8,128)}, f32[8,64]{1,0:T(8,128)}) custom-call(s32[8,64]{1,0:T(8,128)} %bitcast.43, f32[8,64]{1,0:T(8,128)} %bitcast.44, bf16[64,2048]{1,0:T(8,128)(2,1)} %refs_0_.2), custom_call_target="tpu_custom_call" | custom-call | flops 201326592 | bytes 3145728 | tf_op jit(solution)/shard_map/pallas_call | solution.py:126
  4.8 10.9 %all-to-all-start = ((bf16[128,24,512]{2,1,0:T(8,128)(2,1)}), bf16[128,24,512]{2,1,0:T(8,128)(2,1)}, u32[]{:S(2)}, u32[]{:S(2)}) async-start(bf16[128,24,512]{2,1,0:T(8,128)(2,1)} %bitcast.40), calls=%async_computation | async-start | bytes 6291456 | tf_op jit(solution)/shard_map/all_to_all | solution.py:240
  15.7 6.2 %shard_map.121 = (bf16[3072,1024]{1,0:T(8,128)(2,1)}, s32[8,64]{1,0:T(8,128)}, f32[8,64]{1,0:T(8,128)}) custom-call(s32[8,64]{1,0:T(8,128)} %bitcast.45, f32[8,64]{1,0:T(8,128)} %bitcast.46, bf16[64,2048]{1,0:T(8,128)(2,1)} %refs_0_.3, bf16[64,2048]{1,0:T(8,128)(2,1)} %refs_1_.1), custom_call_target="tpu_custom_call" | custom-call | flops 402653184 | bytes 6291456 | tf_op jit(solution)/shard_map/pallas_call | solution.py:126
  21.9 33.6 %all-to-all-done = bf16[128,24,512]{2,1,0:T(8,128)(2,1)} async-done(((bf16[128,24,512]{2,1,0:T(8,128)(2,1)}), bf16[128,24,512]{2,1,0:T(8,128)(2,1)}, u32[]{:S(2)}, u32[]{:S(2)}) %all-to-all-start) | async-done | bytes 3145760 | tf_op jit(solution)/shard_map/all_to_all | solution.py:240
  55.5 7.1 %all-to-all-start.1 = ((bf16[128,24,1024]{2,1,0:T(8,128)(2,1)}), bf16[128,24,1024]{2,1,0:T(8,128)(2,1)}, u32[]{:S(2)}, u32[]{:S(2)}) async-start(bf16[128,24,1024]{2,1,0:T(8,128)(2,1)} %bitcast.39), calls=%async_computation.1 | async-start | bytes 12582912 | tf_op jit(solution)/shard_map/all_to_all | solution.py:240
  62.6 3.7 %shard_map.122 = bf16[768,2048]{1,0:T(8,128)(2,1)} custom-call(bf16[3072,512]{1,0:T(8,128)(2,1)} %bitcast.5.got), custom_call_target="tpu_custom_call" | custom-call | flops 629145600 | bytes 6291456 | tf_op jit(solution)/shard_map/pallas_call | solution.py:158
  66.3 8.1 %fusion.5 = f32[768,1536]{1,0:T(8,128)S(1)} fusion(bf16[768,2048]{1,0:T(8,128)(2,1)} %shard_map.122, bf16[1,2048,1536]{2,1,0:T(8,128)(2,1)} %param.16), kind=kOutput, calls=%fused_computation.6 | convolution fusion | flops 4831838208 | bytes 14155776 | tf_op jit(solution)/shard_map/dot_general | solution.py:245
  74.4 0.0 copy-done
  74.4 4.1 %convolution_convert_fusion.2.rows = bf16[768,2048]{1,0:T(8,128)(2,1)} fusion(bf16[1,768,2048]{2,1,0:T(8,128)(2,1)S(1)} %copy-done, f32[768,1536]{1,0:T(8,128)S(1)} %fusion.5), kind=kOutput, calls=%fused_computation.9 | convolution fusion | flops 2421030912 | bytes 11010048 | tf_op jit(solution)/shard_map/dot_general | solution.py:248
  78.5 4.0 %shard_map.123 = bf16[3072,512]{1,0:T(8,128)(2,1)} custom-call(bf16[768,2048]{1,0:T(8,128)(2,1)} %convolution_convert_fusion.2.rows), custom_call_target="tpu_custom_call" | custom-call | flops 629145600 | bytes 6291456 | tf_op jit(solution)/shard_map/pallas_call | solution.py:182
  82.5 56.0 %all-to-all-done.1 = bf16[128,24,1024]{2,1,0:T(8,128)(2,1)} async-done(((bf16[128,24,1024]{2,1,0:T(8,128)(2,1)}), bf16[128,24,1024]{2,1,0:T(8,128)(2,1)}, u32[]{:S(2)}, u32[]{:S(2)}) %all-to-all-start.1) | async-done | bytes 6291488 | tf_op jit(solution)/shard_map/all_to_all | solution.py:240
  138.5 6.1 %shard_map.124 = (bf16[768,2048]{1,0:T(8,128)(2,1)}, bf16[768,2048]{1,0:T(8,128)(2,1)}) custom-call(bf16[3072,1024]{1,0:T(8,128)(2,1)} %bitcast.9.got), custom_call_target="tpu_custom_call" | custom-call | flops 1258291200 | bytes 12582912 | tf_op jit(solution)/shard_map/pallas_call | solution.py:158
  144.5 8.3 %all-to-all-start.2 = ((bf16[128,24,512]{2,1,0:T(8,128)(2,1)}), bf16[128,24,512]{2,1,0:T(8,128)(2,1)}, u32[]{:S(2)}, u32[]{:S(2)}) async-start(bf16[128,24,512]{2,1,0:T(8,128)(2,1)} %bitcast.37), calls=%async_computation.2 | async-start | bytes 6291456 | tf_op jit(solution)/shard_map/all_to_all | solution.py:240
  152.8 0.0 slice-start
  152.8 8.2 %fusion.3 = f32[768,1536]{1,0:T(8,128)S(1)} fusion(bf16[768,2048]{1,0:T(8,128)(2,1)} %get-tuple-element.26, bf16[1,2048,1536]{2,1,0:T(8,128)(2,1)} %param.16), kind=kOutput, calls=%fused_computation.4 | convolution fusion | flops 4831838208 | bytes 14155776 | tf_op jit(solution)/shard_map/dot_general | solution.py:253
  161.1 0.0 copy-start.4
  161.1 0.0 copy-done.3
  161.1 0.0 slice-start.1
  161.1 3.3 %multiply_convert_fusion.2 = (bf16[768,768]{1,0:T(8,128)(2,1)S(1)}, bf16[768,768]{1,0:T(8,128)(2,1)S(1)}) fusion(f32[768,1536]{1,0:T(8,128)S(1)} %fusion.3, bf16[768,2048]{1,0:T(8,128)(2,1)S(1)} %copy-done.3, bf16[1,768,2048]{2,1,0:T(8,128)(2,1)S(1)} %copy-done), kind=kOutput, calls=%fused_computation.20 | convolution fusion | flops 2423586816 | bytes 13369344 | tf_op jit(solution)/shard_map/dot_general | solution.py:257
  164.5 1.0 copy-done.5
  165.5 0.4 copy-done.7
  165.8 0.0 slice-done
  165.8 6.4 %fusion.7.rows = bf16[768,2048]{1,0:T(8,128)(2,1)} fusion(bf16[1,2048,1536]{2,1,0:T(8,128)(2,1)S(1)} %bitcast.42, bf16[768,768]{1,0:T(8,128)(2,1)S(1)} %get-tuple-element.33, bf16[768,768]{1,0:T(8,128)(2,1)S(1)} %get-tuple-element.32), kind=kOutput, calls=%fused_computation.10 | convolution fusion | flops 4838129664 | bytes 11796480 | tf_op jit(solution)/shard_map/dot_general | solution.py:261
  172.2 4.0 %shard_map.125 = bf16[3072,512]{1,0:T(8,128)(2,1)} custom-call(bf16[768,2048]{1,0:T(8,128)(2,1)} %fusion.7.rows), custom_call_target="tpu_custom_call" | custom-call | flops 629145600 | bytes 6291456 | tf_op jit(solution)/shard_map/pallas_call | solution.py:182
  176.2 16.4 %all-to-all-done.2 = bf16[128,24,512]{2,1,0:T(8,128)(2,1)} async-done(((bf16[128,24,512]{2,1,0:T(8,128)(2,1)}), bf16[128,24,512]{2,1,0:T(8,128)(2,1)}, u32[]{:S(2)}, u32[]{:S(2)}) %all-to-all-start.2) | async-done | bytes 3145760 | tf_op jit(solution)/shard_map/all_to_all | solution.py:240
  192.6 7.1 %all-to-all-start.3 = ((bf16[128,24,512]{2,1,0:T(8,128)(2,1)}), bf16[128,24,512]{2,1,0:T(8,128)(2,1)}, u32[]{:S(2)}, u32[]{:S(2)}) async-start(bf16[128,24,512]{2,1,0:T(8,128)(2,1)} %bitcast.38), calls=%async_computation.3 | async-start | bytes 6291456 | tf_op jit(solution)/shard_map/all_to_all | solution.py:240
  199.7 7.8 %fusion.13 = bf16[1,768,2048]{2,1,0:T(8,128)(2,1)} fusion(bf16[768,2048]{1,0:T(8,128)(2,1)} %get-tuple-element.25, f32[768,1536]{1,0:T(8,128)} %copy-done.4), kind=kOutput, calls=%fused_computation.14 | convolution fusion | flops 2421030912 | bytes 11010048 | tf_op jit(solution)/shard_map/dot_general | solution.py:297
  207.6 7.2 %fusion = bf16[1,2048,1536]{2,1,0:T(8,128)(2,1)} fusion(bf16[768,2048]{1,0:T(8,128)(2,1)S(1)} %copy-done.2, bf16[768,768]{1,0:T(8,128)(2,1)S(1)} %copy-done.8, bf16[768,768]{1,0:T(8,128)(2,1)S(1)} %copy-done.6), kind=kOutput, calls=%fused_computation.1 | convolution fusion | flops 4839702528 | bytes 11796480 | tf_op jit(solution)/shard_map/dot_general | solution.py:300
  214.8 4.7 %shard_map.126 = bf16[64,2048]{1,0:T(8,128)(2,1)} custom-call(s32[8,64]{1,0:T(8,128)} %get-tuple-element.18.key, f32[8,64]{1,0:T(8,128)} %get-tuple-element.19.wgt, bf16[3072,512]{1,0:T(8,128)(2,1)} %bitcast.11.got), custom_call_target="tpu_custom_call" | custom-call | flops 402653184 | bytes 3145728 | tf_op jit(solution)/shard_map/pallas_call | solution.py:228
  219.5 20.1 %all-to-all-done.3 = bf16[128,24,512]{2,1,0:T(8,128)(2,1)} async-done(((bf16[128,24,512]{2,1,0:T(8,128)(2,1)}), bf16[128,24,512]{2,1,0:T(8,128)(2,1)}, u32[]{:S(2)}, u32[]{:S(2)}) %all-to-all-start.3) | async-done | bytes 3145760 | tf_op jit(solution)/shard_map/all_to_all | solution.py:240
  239.6 4.0 %shard_map.127 = bf16[64,2048]{1,0:T(8,128)(2,1)} custom-call(s32[8,64]{1,0:T(8,128)} %get-tuple-element.29.key, f32[8,64]{1,0:T(8,128)} %get-tuple-element.30.wgt, bf16[3072,512]{1,0:T(8,128)(2,1)} %bitcast.13.got), custom_call_target="tpu_custom_call" | custom-call | flops 402653184 | bytes 3145728 | tf_op jit(solution)/shard_map/pallas_call | solution.py:228
  (14 shorter events, 0.0 us)
Async XLA Ops:
  0.6 73.8 %copy-start = (bf16[1,768,2048]{2,1,0:T(8,128)(2,1)S(1)}, bf16[1,768,2048]{2,1,0:T(8,128)(2,1)}, u32[]{:S(2)}) copy-start(bf16[1,768,2048]{2,1,0:T(8,128)(2,1)} %param.17) | copy-start | bytes 9437188
  4.8 50.7 %all-to-all-start = ((bf16[128,24,512]{2,1,0:T(8,128)(2,1)}), bf16[128,24,512]{2,1,0:T(8,128)(2,1)}, u32[]{:S(2)}, u32[]{:S(2)}) async-start(bf16[128,24,512]{2,1,0:T(8,128)(2,1)} %bitcast.40), calls=%async_computation | async-start | bytes 6291456 | tf_op jit(solution)/shard_map/all_to_all | solution.py:240
  55.5 83.0 %all-to-all-start.1 = ((bf16[128,24,1024]{2,1,0:T(8,128)(2,1)}), bf16[128,24,1024]{2,1,0:T(8,128)(2,1)}, u32[]{:S(2)}, u32[]{:S(2)}) async-start(bf16[128,24,1024]{2,1,0:T(8,128)(2,1)} %bitcast.39), calls=%async_computation.1 | async-start | bytes 12582912 | tf_op jit(solution)/shard_map/all_to_all | solution.py:240
  144.5 48.1 %all-to-all-start.2 = ((bf16[128,24,512]{2,1,0:T(8,128)(2,1)}), bf16[128,24,512]{2,1,0:T(8,128)(2,1)}, u32[]{:S(2)}, u32[]{:S(2)}) async-start(bf16[128,24,512]{2,1,0:T(8,128)(2,1)} %bitcast.37), calls=%async_computation.2 | async-start | bytes 6291456 | tf_op jit(solution)/shard_map/all_to_all | solution.py:240
  152.8 8.3 %copy-start.3 = (bf16[768,2048]{1,0:T(8,128)(2,1)S(1)}, bf16[768,2048]{1,0:T(8,128)(2,1)}, u32[]{:S(2)}) copy-start(bf16[768,2048]{1,0:T(8,128)(2,1)} %get-tuple-element.25) | copy-start | bytes 9437188
  152.8 13.0 %slice-start = ((s8[6291456]{0:T(1024)(128)(4,1)}), s8[4194304]{0:T(1024)(128)(4,1)S(1)}, s32[]{:S(2)}) async-start(s8[6291456]{0:T(1024)(128)(4,1)} %bitcast.41), calls=%async_computation.4 | async-start | bytes 8388608
  161.1 3.3 %copy-start.4 = (f32[768,1536]{1,0:T(8,128)}, f32[768,1536]{1,0:T(8,128)S(1)}, u32[]{:S(2)}) copy-start(f32[768,1536]{1,0:T(8,128)S(1)} %fusion.3) | copy-start | bytes 14155780
  161.1 4.7 %slice-start.1 = ((s8[6291456]{0:T(1024)(128)(4,1)}), s8[2097152]{0:T(1024)(128)(4,1)S(1)}, s32[]{:S(2)}) async-start(s8[6291456]{0:T(1024)(128)(4,1)} %bitcast.41), calls=%async_computation.5 | async-start | bytes 4194304
  164.4 1.0 copy-start.5
  164.4 1.4 copy-start.7
  192.6 47.0 %all-to-all-start.3 = ((bf16[128,24,512]{2,1,0:T(8,128)(2,1)}), bf16[128,24,512]{2,1,0:T(8,128)(2,1)}, u32[]{:S(2)}, u32[]{:S(2)}) async-start(bf16[128,24,512]{2,1,0:T(8,128)(2,1)} %bitcast.38), calls=%async_computation.3 | async-start | bytes 6291456 | tf_op jit(solution)/shard_map/all_to_all | solution.py:240
  199.7 7.9 %copy-start.2 = (bf16[768,2048]{1,0:T(8,128)(2,1)S(1)}, bf16[768,2048]{1,0:T(8,128)(2,1)}, u32[]{:S(2)}) copy-start(bf16[768,2048]{1,0:T(8,128)(2,1)} %get-tuple-element.26) | copy-start | bytes 9437188
  199.7 7.9 %copy-start.6 = (bf16[768,768]{1,0:T(8,128)(2,1)S(1)}, bf16[768,768]{1,0:T(8,128)(2,1)}, u32[]{:S(2)}) copy-start(bf16[768,768]{1,0:T(8,128)(2,1)} %copy-done.5) | copy-start | bytes 3538948
  199.7 7.8 %copy-start.8 = (bf16[768,768]{1,0:T(8,128)(2,1)S(1)}, bf16[768,768]{1,0:T(8,128)(2,1)}, u32[]{:S(2)}) copy-start(bf16[768,768]{1,0:T(8,128)(2,1)} %copy-done.7) | copy-start | bytes 3538948
  214.8 28.8 %copy-start.1 = (bf16[1,768,2048]{2,1,0:T(8,128)(2,1)S(1)}, bf16[1,768,2048]{2,1,0:T(8,128)(2,1)}, u32[]{:S(2)}) copy-start(bf16[1,768,2048]{2,1,0:T(8,128)(2,1)} %param.17) | copy-start | bytes 9437188

commit v4 on v3

--- a/solution.py
+++ b/solution.py
@@ -5,10 +5,12 @@
 from jax import lax
 from jax.experimental import pallas as pl
 from jax.experimental.pallas import tpu as pltpu
+from jax.sharding import Mesh
 from jax.sharding import PartitionSpec as P
 
 
-AXES = ("group", "inner")
+FINE = ("y", "z", "x", "c")
+TOP = 8
 PARTS = 4
 LANES = 128
 F32 = jnp.float32
@@ -87,83 +89,221 @@
     wgt[...] = share / jnp.sum(share, axis=0, keepdims=True)
 
 
-def send_body(experts, capacity, weighted, ids, sc, *refs):
-    *tables, out, key, wgt, pieces = refs
-    top, tok = ids.shape
-    rows = out.shape[0] // PARTS
-    piece = tables[0].shape[1] // PARTS
-
-    @pl.when(pl.program_id(0) == 0)
-    def _():
-        place(experts, capacity, ids, sc, key, wgt)
-
+def payload_body(experts, capacity, ids, sc, *refs):
+    *refs, key, wgt = refs
+    tables, outs = refs[: len(refs) // 2], refs[len(refs) // 2 :]
+    tok = ids.shape[1]
+    place(experts, capacity, ids, sc, key, wgt)
+    slot = key[...] - ids[...] * capacity
+    share = wgt[...]
+    first = share.astype(BF16)
+    rest = share - first.astype(F32)
+    second = rest.astype(BF16)
+    third = (rest - second.astype(F32)).astype(BF16)
+    facts = (ids[...].astype(F32), slot.astype(F32), first, second, third)
+    for table, out in zip(tables, outs):
+        out[:tok, :] = table[...]
+        out[tok:, :] = jnp.zeros((out.shape[0] - tok, out.shape[1]), BF16)
+        for k, fact in enumerate(facts):
+            out[tok:, k * LANES : k * LANES + tok] = fact.astype(BF16)
+
+
+def payload(experts, capacity, ids, sc, tables):
+    tok, width = tables[0].shape
+    n = len(tables)
+    tall = (tok + ids.shape[0], width)
+    return call(
+        functools.partial(payload_body, experts, capacity),
+        (1,),
+        [whole(ids.shape)] * 2 + [whole((tok, width))] * n,
+        [whole(tall)] * n + [whole(ids.shape)] * 2,
+        [jax.ShapeDtypeStruct(tall, BF16)] * n
+        + [jax.ShapeDtypeStruct(ids.shape, jnp.int32), jax.ShapeDtypeStruct(ids.shape, F32)],
+        (50_000_000, 4 * n * tok * width),
+    )(ids, sc, *tables)
+
+
+def fact(pay, tok, k):
+    return pay[tok:, k * LANES : k * LANES + tok].astype(F32)
+
+
+def coordinates(ids):
+    return ids >> 5, (ids >> 3) & 3, (ids >> 1) & 3, ids & 1
+
+
+def plane_body(along, capacity, *refs):
+    *pays, out, pieces = refs
+    dests = out.shape[0]
+    rows = dests * capacity
+    tok = pays[0].shape[0] - TOP
+    here = lax.axis_index(along)
     mine = pl.program_id(0) * rows + lax.broadcasted_iota(jnp.int32, (rows, tok), 0)
-    pick = jnp.zeros((rows, tok), F32)
-    load = jnp.zeros((rows, tok), F32)
-    for j in range(top):
-        hit = mine == key[j : j + 1, :]
-        pick = jnp.where(hit, 1.0, pick)
-        load = jnp.where(hit, wgt[j : j + 1, :], load)
-    pick = pick.astype(BF16)
-    scale = jnp.sum(load, axis=1, keepdims=True)
-    for i, table in enumerate(tables):
+    for s, pay in enumerate(pays):
+        ids = fact(pay, tok, 0).astype(jnp.int32)
+        slot = fact(pay, tok, 1).astype(jnp.int32)
+        y, z, x, c = coordinates(ids)
+        near, far = (y, z) if along == "y" else (z, y)
+        want = jnp.where(near == here, ((far * 4 + x) * 2 + c) * capacity + slot, -1)
+        pick = jnp.zeros((rows, tok), F32)
+        for j in range(TOP):
+            pick = jnp.where(mine == want[j : j + 1, :], 1.0, pick)
+        pick = pick.astype(BF16)
+        piece = pay.shape[1] // PARTS
         for q in range(PARTS):
             got = jnp.dot(
-                pick, table[:, q * piece : (q + 1) * piece], preferred_element_type=F32
+                pick, pay[:tok, q * piece : (q + 1) * piece], preferred_element_type=F32
             )
-            if weighted[i]:
-                got = got * scale
             spread(pieces, q, got)
-        flush(pieces, out, i * piece)
-
-
-def send(experts, capacity, ids, sc, tables, weighted):
-    tok, width = tables[0].shape
-    n = len(tables)
-    total = experts * capacity * PARTS
+        for k in range(pieces.shape[0]):
+            out[:, s, :, k * LANES : (k + 1) * LANES] = (
+                pieces[k].reshape(dests, capacity * PARTS, LANES).astype(BF16)
+            )
+
+
+def plane(along, capacity, pays):
+    tall, width = pays[0].shape
+    steps = 2
+    shape = (32, len(pays), capacity * PARTS, width // PARTS)
+    return call(
+        functools.partial(plane_body, along, capacity),
+        (steps,),
+        [whole((tall, width))] * len(pays),
+        pl.BlockSpec((shape[0] // steps,) + shape[1:], lambda i: (i, 0, 0, 0)),
+        jax.ShapeDtypeStruct(shape, BF16),
+        (2_000_000_000, 8_000_000),
+        [pltpu.VMEM((width // PARTS // LANES, 32 // steps * capacity * PARTS, LANES), F32)],
+    )(*pays)
+
+
+def rings_body(capacity, own, other, o0, o1, o2, o3, pieces):
+    tall, width = own.shape[1:]
+    tok = tall - TOP
     piece = width // PARTS
-    steps = 2
-    return call(
-        functools.partial(send_body, experts, capacity, weighted),
-        (steps,),
-        [whole(ids.shape)] * 2 + [whole((tok, width))] * n,
-        [
-            pl.BlockSpec((total // steps, n * piece), lambda i: (i, 0)),
-            whole(ids.shape),
-            whole(ids.shape),
-        ],
-        [
-            jax.ShapeDtypeStruct((total, n * piece), BF16),
-            jax.ShapeDtypeStruct(ids.shape, jnp.int32),
-            jax.ShapeDtypeStruct(ids.shape, F32),
-        ],
-        (2 * total * tok * n * piece, 2 * total * n * piece),
-        [pltpu.VMEM((piece // LANES, total // steps, LANES), F32)],
-    )(ids, sc, *tables)
-
-
-def unpack_body(n, got, *refs):
-    *outs, pieces = refs
-    piece = got.shape[1] // n
-    fill(pieces, got)
-    for i, out in enumerate(outs):
-        for q in range(PARTS):
-            out[:, q * piece : (q + 1) * piece] = collected(pieces, q, i * piece, piece)
-
-
-def unpack(got, n):
-    total, wide = got.shape
-    steps = 2
-    width = PARTS * wide // n
-    return call(
-        functools.partial(unpack_body, n),
-        (steps,),
-        [pl.BlockSpec((total // steps, wide), lambda i: (i, 0))],
-        [pl.BlockSpec((total // PARTS // steps, width), lambda i: (i, 0))] * n,
-        [jax.ShapeDtypeStruct((total // PARTS, width), BF16)] * n,
-        (400 * total * wide, 4 * total * wide),
-        [pltpu.VMEM((wide // LANES, total // steps, LANES), F32)],
-    )(got)
+    rows = 16 * capacity
+    my_y, my_z = lax.axis_index("y"), lax.axis_index("z")
+    my_x, my_c = lax.axis_index("x"), lax.axis_index("c")
+    mine = lax.broadcasted_iota(jnp.int32, (rows, tok), 0)
+    for half, blocks in enumerate((own, other)):
+
+        @pl.loop(0, blocks.shape[0])
+        def _(i):
+            pay = blocks.at[i]
+            ids = fact(pay, tok, 0).astype(jnp.int32)
+            slot = fact(pay, tok, 1).astype(jnp.int32)
+            share = fact(pay, tok, 2) + fact(pay, tok, 3) + fact(pay, tok, 4)
+            y, z, x, c = coordinates(ids)
+            turn = ((y - my_y) & 3) * 4 + ((z - my_z) & 3)
+            want = jnp.where((x == my_x) & (c == my_c), turn * capacity + slot, -1)
+            pick = jnp.zeros((rows, tok), F32)
+            load = jnp.zeros((rows, tok), F32)
+            for j in range(TOP):
+                hit = mine == want[j : j + 1, :]
+                pick = jnp.where(hit, 1.0, pick)
+                load = jnp.where(hit, share[j : j + 1, :], load)
+            pick = pick.astype(BF16)
+            scale = jnp.sum(load, axis=1, keepdims=True)
+            for q in range(PARTS):
+                got = jnp.dot(
+                    pick, pay[:tok, q * piece : (q + 1) * piece], preferred_element_type=F32
+                )
+                spread(pieces, q, got * scale)
+            for k in range(pieces.shape[0]):
+                chunks = pieces[k].reshape(4, 4, capacity * PARTS, LANES).astype(BF16)
+                for s, out in enumerate((o0, o1, o2, o3)):
+                    out[:, half * 4 + i, :, k * LANES : (k + 1) * LANES] = chunks[s]
+
+
+def rings(capacity, own, other):
+    count, _, width = own.shape
+    shape = (4, 2 * count, capacity * PARTS, width // PARTS)
+    return call(
+        functools.partial(rings_body, capacity),
+        (1,),
+        [whole(own.shape), whole(other.shape)],
+        [whole(shape)] * 4,
+        [jax.ShapeDtypeStruct(shape, BF16)] * 4,
+        (2_000_000_000, 8_000_000),
+        [pltpu.VMEM((width // PARTS // LANES, 16 * capacity * PARTS, LANES), F32)],
+    )(own, other)
+
+
+def regroup_body(*refs):
+    parts, outs = refs[:4], refs[4:]
+    for turn, out in enumerate(outs):
+        for s, part in enumerate(parts):
+            out[s] = part[turn]
+
+
+def regroup(parts):
+    shape = parts[0].shape
+    return call(
+        regroup_body,
+        (1,),
+        [whole(shape)] * 4,
+        [whole(shape)] * 4,
+        [jax.ShapeDtypeStruct(shape, BF16)] * 4,
+        (1_000_000_000, 8_000_000),
+    )(*parts)
+
+
+def settle(pieces, source, pos):
+    size = source.shape[0]
+    start = pl.multiple_of(pos * size, 8)
+    for k in range(pieces.shape[0]):
+        pieces[k, pl.ds(start, size), :] = source[:, k * LANES : (k + 1) * LANES].astype(F32)
+
+
+def lay_out(pieces, out):
+    piece = out.shape[1] // PARTS
+    for q in range(PARTS):
+        out[:, q * piece : (q + 1) * piece] = collected(pieces, q, 0, piece)
+
+
+def unplane_body(along, got, out, pieces):
+    here = lax.axis_index(along)
+
+    @pl.loop(0, got.shape[0])
+    def _(d):
+        for s in range(got.shape[1]):
+            back = (here - s) & 3
+            if along == "y":
+                pos = back * 32 + d
+            else:
+                pos = (d >> 3) * 32 + back * 8 + (d & 7)
+            settle(pieces, got.at[d, s], pos)
+
+    lay_out(pieces, out)
+
+
+def unrings_body(t0, t1, t2, t3, out, pieces):
+    my_y, my_z = lax.axis_index("y"), lax.axis_index("z")
+    my_x, my_c = lax.axis_index("x"), lax.axis_index("c")
+    for turn, got in enumerate((t0, t1, t2, t3)):
+        z = (my_z - turn) & 3
+
+        @pl.loop(0, got.shape[0])
+        def _(s):
+            y = (my_y - s) & 3
+            for b in range(got.shape[1]):
+                x = (my_x - b % 4) & 3
+                c = my_c if b < 4 else 1 - my_c
+                settle(pieces, got.at[s, b], ((y * 4 + z) * 4 + x) * 2 + c)
+
+    lay_out(pieces, out)
+
+
+def rows_of(body, *got):
+    _, piece = got[0].shape[-2:]
+    total = sum(g.size for g in got) // piece
+    return call(
+        body,
+        (1,),
+        [whole(g.shape) for g in got],
+        whole((total // PARTS, piece * PARTS)),
+        jax.ShapeDtypeStruct((total // PARTS, piece * PARTS), BF16),
+        (400 * total * piece, 4 * total * piece),
+        [pltpu.VMEM((piece // LANES, total, LANES), F32)],
+    )(*got)
 
 
 def pack_body(rows, out, pieces):
@@ -236,8 +376,20 @@
     )(key, wgt, got)
 
 
-def exchange(x):
-    return lax.all_to_all(x, AXES, split_axis=0, concat_axis=0, tiled=True)
+def exchange(x, axes=FINE):
+    return lax.all_to_all(x, axes, split_axis=0, concat_axis=0, tiled=True)
+
+
+def turned(x, axis, turn):
+    return lax.ppermute(x, axis, [(i, (i + turn) % 4) for i in range(4)])
+
+
+def gathered(x, axis):
+    return [x] + [turned(x, axis, turn) for turn in (1, 3, 2)]
+
+
+def in_order(parts):
+    return [parts[0], parts[1], parts[3], parts[2]]
 
 
 def expert_forward(x, w_in, w_down):
@@ -248,9 +400,8 @@
     return jnp.dot(hidden, w_down, preferred_element_type=F32).astype(BF16)
 
 
-def expert_backward(x, cot, w_in, w_down):
+def expert_backward(projected, cot, w_in, w_down):
     width = w_down.shape[0]
-    projected = jnp.dot(x, w_in, preferred_element_type=F32)
     g, u = projected[:, :width], projected[:, width:]
     s = jax.nn.sigmoid(g)
     hidden = (g * s * u).astype(BF16)
@@ -267,28 +418,44 @@
 def layer(
     tokens_fwd, experts_fwd, scores_fwd, tokens_bwd, experts_bwd, scores_bwd, cotangent, w_in, w_down
 ):
-    devices = lax.axis_size("group") * lax.axis_size("inner")
+    devices = lax.axis_size(FINE)
     tok, top = experts_fwd.shape
     capacity = max(2, 3 * tok * top // (2 * devices))
     w_in, w_down = w_in[0], w_down[0]
 
-    out_f, key_f, wgt_f = send(
-        devices, capacity, experts_fwd.T, scores_fwd.T, (tokens_fwd,), (False,)
-    )
-    in_f = exchange(out_f)
-    out_b, key_b, wgt_b = send(
-        devices, capacity, experts_bwd.T, scores_bwd.T, (tokens_bwd, cotangent), (False, True)
-    )
+    pay_f, key_f, wgt_f = payload(
+        devices, capacity, experts_fwd.T, scores_fwd.T, (tokens_fwd,)
+    )
+    near_f = in_order(gathered(pay_f, "y"))
+    pay_b, pay_c, key_b, wgt_b = payload(
+        devices, capacity, experts_bwd.T, scores_bwd.T, (tokens_bwd, cotangent)
+    )
+    near_c = in_order(gathered(pay_c, "x"))
+    near_b = in_order(gathered(pay_b, "z"))
+
+    out_f = plane("y", capacity, near_f)
+    in_f = exchange(out_f, ("z", "x", "c"))
+
+    own_c = jnp.stack(near_c)
+    other_c = lax.ppermute(own_c, "c", [(0, 1), (1, 0)])
+    out_c = rings(capacity, own_c, other_c)
+    by_y = [out_c[0]] + [turned(out_c[s], "y", s) for s in (1, 2, 3)]
+    out_b = plane("z", capacity, near_b)
     out_b, in_f = lax.optimization_barrier((out_b, in_f))
-    in_b = exchange(out_b)
-
-    (rows_f,) = unpack(in_f, 1)
-    back_f = pack(expert_forward(rows_f, w_in, w_down))
+    in_b = exchange(out_b, ("y", "x", "c"))
+
+    rows_f = rows_of(functools.partial(unplane_body, "y"), in_f)
+    by_z = regroup(by_y)
+    in_c = [by_z[0]] + [turned(by_z[turn], "z", turn) for turn in (1, 2, 3)]
+    out_rows = expert_forward(rows_f, w_in, w_down)
+    back_f = pack(out_rows)
     back_f, in_b = lax.optimization_barrier((back_f, in_b))
     home_f = exchange(back_f)
 
-    rows_b, cot_b = unpack(in_b, 2)
-    row_grad, hidden, d_proj = expert_backward(rows_b, cot_b, w_in, w_down)
+    rows_b = rows_of(functools.partial(unplane_body, "z"), in_b)
+    projected = jnp.dot(rows_b, w_in, preferred_element_type=F32)
+    cot_b = rows_of(unrings_body, *in_c)
+    row_grad, hidden, d_proj = expert_backward(projected, cot_b, w_in, w_down)
     back_b = pack(row_grad)
     back_b, home_f = lax.optimization_barrier((back_b, home_f))
     home_b = exchange(back_b)
@@ -305,11 +472,12 @@
 
 
 def solution(mesh):
-    rows = P(AXES, None)
-    cube = P(AXES, None, None)
+    rows = P(FINE, None)
+    cube = P(FINE, None, None)
+    fine = Mesh(mesh.devices.reshape(4, 4, 4, 2), FINE)
     return jax.shard_map(
         layer,
-        mesh=mesh,
+        mesh=fine,
         in_specs=(rows,) * 7 + (cube,) * 2,
         out_specs=(rows, rows, cube, cube),
         check_vma=False,

time: 247 us -> 312 us (1.26)
  starting transfers between devices: 33.4 us -> 55.9 us
  waiting for transfers between devices: 126 us -> 144 us
  Pallas kernels: 36.8 us -> 52.8 us
  matrix products: 45.1 us -> 49.5 us
    ppermute x0 -> x16, waiting for transfers between devices: none -> 112 us  [the longest x15 109 us: turned(): return lax.ppermute(x, axis, [(i, (i + turn) % 4) for i in range(4)])]
    all_to_all x4, waiting for transfers between devices: 126 us -> 32.8 us  [exchange(): return lax.all_to_all(x, axes, split_axis=0, concat_axis=0, tiled=True)]
    ppermute x0 -> x16, starting transfers between devices: none -> 23.4 us  [the longest x15 23.4 us: turned(): return lax.ppermute(x, axis, [(i, (i + turn) % 4) for i in range(4)])]
    pallas_call x4 -> x9, Pallas kernels: 20.1 us -> 36.4 us  [the longest x3 14.5 us: rows_of(): call(body, (1,), [whole(g.shape) for g in got], whole((total // PARTS, pi...]
  transfers between devices with their start and end apart: 4 -> 20, of which waited for: 4 -> 14; matrix products, arithmetic and copies ran while one was open for 19% -> 16% of each run, Pallas kernels for 9% -> 12%
where the time goes in v4:
time: 312 us; the launch traced here: 308 us
  waiting for transfers between devices  144 us (46%)
  starting transfers between devices  55.9 us (18%)
  Pallas kernels  52.8 us (17%)
  matrix products  49.5 us (16%)
  local copies, waits for them, and re-layouts  3.83 us (1%)
    ppermute x15, waiting for transfers between devices, turned(): return lax.ppermute(x, axis, [(i, (i + turn) % 4) for i in range(4)])  109 us
    all_to_all x4, waiting for transfers between devices, exchange(): return lax.all_to_all(x, axes, split_axis=0, concat_axis=0, tiled=True)  32.8 us
    all_to_all x4, starting transfers between devices, exchange(): return lax.all_to_all(x, axes, split_axis=0, concat_axis=0, tiled=True)  32.5 us
    ppermute x15, starting transfers between devices, turned(): return lax.ppermute(x, axis, [(i, (i + turn) % 4) for i in range(4)])  23.4 us
    pallas_call x3, Pallas kernels, rows_of(): call(body, (1,), [whole(g.shape) for g in got], whole((total // PARTS, pi...  14.5 us
    dot_general x1, matrix products, expert_backward(): lax.dot_general(d_proj, w_in, COLS_BY_COLS, preferred_element_type=F32)  9.38 us
    dot_general x1, matrix products, layer(): projected = jnp.dot(rows_b, w_in, preferred_element_type=F32)  8.6 us
    pallas_call x2, Pallas kernels, combine(): call(functools.partial(combine_body, weighted), (steps,), [whole((top, to...  8.51 us
  transfers between devices with their start and end apart: 20, of which 14 were waited for; matrix products, arithmetic and copies ran while one was open for 16% of the time, Pallas kernels for 12%

profile of v4, /device:TPU:6, one launch (start us, length us, event | category | flops | bytes accessed | tf_op | source)
XLA Modules:
  0.0 308.4 jit_solution(5553537502702906746)
XLA Ops:
  7.3 11.3 %collective-permute-done.15.refs_3_ = bf16[72,2048]{1,0:T(8,128)(2,1)S(1)} collective-permute-done((bf16[72,2048]{1,0:T(8,128)(2,1)}, bf16[72,2048]{1,0:T(8,128)(2,1)S(1)}, u32[]{:S(2)}, u32[]{:S(2)}) %collective-permute-start.15) | collective-permute-done | bytes 294944 | tf_op jit(solution)/shard_map/ppermute | solution.py:384
  18.7 3.7 %collective-permute-done.13.refs_1_ = bf16[72,2048]{1,0:T(8,128)(2,1)} collective-permute-done((bf16[72,2048]{1,0:T(8,128)(2,1)}, bf16[72,2048]{1,0:T(8,128)(2,1)}, u32[]{:S(2)}, u32[]{:S(2)}) %collective-permute-start.13) | collective-permute-done | bytes 294944 | tf_op jit(solution)/shard_map/ppermute | solution.py:384
  22.4 4.0 %shard_map.126 = bf16[32,4,24,512]{3,2,1,0:T(8,128)(2,1)} custom-call(bf16[72,2048]{1,0:T(8,128)(2,1)} %get-tuple-element.37.refs_0_, bf16[72,2048]{1,0:T(8,128)(2,1)} %collective-permute-done.13.refs_1_, bf16[72,2048]{1,0:T(8,128)(2,1)} %collective-permute-done.14.refs_2_, bf16[72,2048]{1,0:T(8,128)(2,1)} %copy-done.5), custom_call_target="tpu_custom_call" | custom-call | flops 2000000000 | bytes 8000000 | tf_op jit(solution)/shard_map/pallas_call | solution.py:167
  26.4 8.4 %all-to-all-start = ((bf16[32,4,24,512]{3,2,1,0:T(8,128)(2,1)}), bf16[32,4,24,512]{3,2,1,0:T(8,128)(2,1)}, u32[]{:S(2)}, u32[]{:S(2)}) async-start(bf16[32,4,24,512]{3,2,1,0:T(8,128)(2,1)} %shard_map.126), calls=%async_computation | async-start | bytes 6291456 | tf_op jit(solution)/shard_map/all_to_all | solution.py:380
  41.1 36.2 %collective-permute-done.2 = bf16[72,2048]{1,0:T(8,128)(2,1)S(1)} collective-permute-done((bf16[72,2048]{1,0:T(8,128)(2,1)}, bf16[72,2048]{1,0:T(8,128)(2,1)S(1)}, u32[]{:S(2)}, u32[]{:S(2)}) %collective-permute-start.2) | collective-permute-done | bytes 294944 | tf_op jit(solution)/shard_map/ppermute | solution.py:384
  77.3 6.8 %collective-permute-done.1 = bf16[72,2048]{1,0:T(8,128)(2,1)S(1)} collective-permute-done((bf16[72,2048]{1,0:T(8,128)(2,1)}, bf16[72,2048]{1,0:T(8,128)(2,1)S(1)}, u32[]{:S(2)}, u32[]{:S(2)}) %collective-permute-start.1) | collective-permute-done | bytes 294944 | tf_op jit(solution)/shard_map/ppermute | solution.py:384
  90.2 6.0 %shard_map.122 = (bf16[4,8,24,512]{3,2,1,0:T(8,128)(2,1)}, bf16[4,8,24,512]{3,2,1,0:T(8,128)(2,1)}, bf16[4,8,24,512]{3,2,1,0:T(8,128)(2,1)}, bf16[4,8,24,512]{3,2,1,0:T(8,128)(2,1)}) custom-call(bf16[4,72,2048]{2,1,0:T(8,128)(2,1)} %copy-done.3, bf16[4,72,2048]{2,1,0:T(8,128)(2,1)} %collective-permute-done.3.other), custom_call_target="tpu_custom_call" | custom-call | flops 2000000000 | bytes 8000000 | tf_op jit(solution)/shard_map/pallas_call | solution.py:219
  103.3 11.3 %collective-permute-done.12.refs_3_ = bf16[72,2048]{1,0:T(8,128)(2,1)S(1)} collective-permute-done((bf16[72,2048]{1,0:T(8,128)(2,1)S(1)}, bf16[72,2048]{1,0:T(8,128)(2,1)S(1)}, u32[]{:S(2)}, u32[]{:S(2)}) %collective-permute-start.12) | collective-permute-done | bytes 294944 | tf_op jit(solution)/shard_map/ppermute | solution.py:384
  116.0 7.1 %collective-permute-done.10.refs_1_ = bf16[72,2048]{1,0:T(8,128)(2,1)} collective-permute-done((bf16[72,2048]{1,0:T(8,128)(2,1)S(1)}, bf16[72,2048]{1,0:T(8,128)(2,1)}, u32[]{:S(2)}, u32[]{:S(2)}) %collective-permute-start.10) | collective-permute-done | bytes 294944 | tf_op jit(solution)/shard_map/ppermute | solution.py:384
  123.1 4.0 %shard_map.125 = bf16[32,4,24,512]{3,2,1,0:T(8,128)(2,1)} custom-call(bf16[72,2048]{1,0:T(8,128)(2,1)} %get-tuple-element.36.refs_0_, bf16[72,2048]{1,0:T(8,128)(2,1)} %collective-permute-done.10.refs_1_, bf16[72,2048]{1,0:T(8,128)(2,1)} %copy-done.7, bf16[72,2048]{1,0:T(8,128)(2,1)} %copy-done.6), custom_call_target="tpu_custom_call" | custom-call | flops 2000000000 | bytes 8000000 | tf_op jit(solution)/shard_map/pallas_call | solution.py:167
  127.2 6.8 %all-to-all-start.1 = ((bf16[32,4,24,512]{3,2,1,0:T(8,128)(2,1)}), bf16[32,4,24,512]{3,2,1,0:T(8,128)(2,1)}, u32[]{:S(2)}, u32[]{:S(2)}) async-start(bf16[32,4,24,512]{3,2,1,0:T(8,128)(2,1)} %shard_map.125), calls=%async_computation.1 | async-start | bytes 6291456 | tf_op jit(solution)/shard_map/all_to_all | solution.py:380
  134.8 3.6 %shard_map.123 = (bf16[4,8,24,512]{3,2,1,0:T(8,128)(2,1)}, bf16[4,8,24,512]{3,2,1,0:T(8,128)(2,1)}, bf16[4,8,24,512]{3,2,1,0:T(8,128)(2,1)}, bf16[4,8,24,512]{3,2,1,0:T(8,128)(2,1)}) custom-call(bf16[4,8,24,512]{3,2,1,0:T(8,128)(2,1)} %get-tuple-element.28.refs_0_, bf16[4,8,24,512]{3,2,1,0:T(8,128)(2,1)} %collective-permute-done.4.refs_1_, ...), custom_call_target="tpu_custom_call" | custom-call | flops 1000000000 | bytes 8000000 | tf_op jit(solution)/shard_map/pallas_call | solution.py:239
  138.4 4.9 %collective-permute-start.7 = (bf16[4,8,24,512]{3,2,1,0:T(8,128)(2,1)}, bf16[4,8,24,512]{3,2,1,0:T(8,128)(2,1)}, u32[]{:S(2)}, u32[]{:S(2)}) collective-permute-start(bf16[4,8,24,512]{3,2,1,0:T(8,128)(2,1)} %get-tuple-element.33), channel_id=1, source_target_pairs={{0,8},{8,16},{16,24},{24,0},{1,9},{9,17},{17,25},{25,1},{2,10},{10... | collective-permute-start | bytes 2359304 | tf_op jit(solution)/shard_map/ppermute | solution.py:384
  146.0 15.6 %collective-permute-done.7.t1 = bf16[4,8,24,512]{3,2,1,0:T(8,128)(2,1)} collective-permute-done((bf16[4,8,24,512]{3,2,1,0:T(8,128)(2,1)}, bf16[4,8,24,512]{3,2,1,0:T(8,128)(2,1)}, u32[]{:S(2)}, u32[]{:S(2)}) %collective-permute-start.7) | collective-permute-done | bytes 786464 | tf_op jit(solution)/shard_map/ppermute | solution.py:384
  161.5 14.7 %collective-permute-done.8.t2 = bf16[4,8,24,512]{3,2,1,0:T(8,128)(2,1)} collective-permute-done((bf16[4,8,24,512]{3,2,1,0:T(8,128)(2,1)}, bf16[4,8,24,512]{3,2,1,0:T(8,128)(2,1)}, u32[]{:S(2)}, u32[]{:S(2)}) %collective-permute-start.8) | collective-permute-done | bytes 786464 | tf_op jit(solution)/shard_map/ppermute | solution.py:384
  176.3 4.8 %shard_map.124 = bf16[768,2048]{1,0:T(8,128)(2,1)} custom-call(bf16[4,8,24,512]{3,2,1,0:T(8,128)(2,1)} %get-tuple-element.32.t0, bf16[4,8,24,512]{3,2,1,0:T(8,128)(2,1)} %collective-permute-done.7.t1, bf16[4,8,24,512]{3,2,1,0:T(8,128)(2,1)} %collective-permute-done.8.t2, bf16[4,8,24,512]{3,2,1,0:T(8,128)(2,1)} %collective-permute-done.9.t3), custom_call_target="tpu_custom_call" | custom-call | flops 629145600 | bytes 6291456 | tf_op jit(solution)/shard_map/pallas_call | solution.py:298
  181.1 4.8 %shard_map.127 = bf16[768,2048]{1,0:T(8,128)(2,1)} custom-call(bf16[32,4,24,512]{3,2,1,0:T(8,128)(2,1)} %all-to-all-done.got), custom_call_target="tpu_custom_call" | custom-call | flops 629145600 | bytes 6291456 | tf_op jit(solution)/shard_map/pallas_call | solution.py:298
  185.9 8.4 %fusion.5 = f32[768,1536]{0,1:T(8,128)S(1)} fusion(bf16[768,2048]{1,0:T(8,128)(2,1)} %shard_map.127, bf16[1,2048,1536]{2,1,0:T(8,128)(2,1)} %param.16), kind=kOutput, calls=%fused_computation.6 | convolution fusion | flops 4831838208 | bytes 14155776 | tf_op jit(solution)/shard_map/dot_general | solution.py:397
  194.4 4.2 %convolution_convert_fusion.2.rows = bf16[768,2048]{1,0:T(8,128)(2,1)} fusion(bf16[1,768,2048]{2,1,0:T(8,128)(2,1)S(1)} %copy-done, f32[768,1536]{0,1:T(8,128)S(1)} %fusion.5), kind=kOutput, calls=%fused_computation.9 | convolution fusion | flops 2421030912 | bytes 11010048 | tf_op jit(solution)/shard_map/dot_general | solution.py:400
  198.6 4.0 %shard_map.128 = bf16[3072,512]{1,0:T(8,128)(2,1)} custom-call(bf16[768,2048]{1,0:T(8,128)(2,1)} %convolution_convert_fusion.2.rows), custom_call_target="tpu_custom_call" | custom-call | flops 629145600 | bytes 6291456 | tf_op jit(solution)/shard_map/pallas_call | solution.py:322
  202.6 4.9 %shard_map.129 = bf16[768,2048]{1,0:T(8,128)(2,1)} custom-call(bf16[32,4,24,512]{3,2,1,0:T(8,128)(2,1)} %all-to-all-done.1.got), custom_call_target="tpu_custom_call" | custom-call | flops 629145600 | bytes 6291456 | tf_op jit(solution)/shard_map/pallas_call | solution.py:298
  207.4 10.2 %all-to-all-start.2 = ((bf16[128,24,512]{2,1,0:T(8,128)(2,1)}), bf16[128,24,512]{2,1,0:T(8,128)(2,1)}, u32[]{:S(2)}, u32[]{:S(2)}) async-start(bf16[128,24,512]{2,1,0:T(8,128)(2,1)} %bitcast.38), calls=%async_computation.2 | async-start | bytes 6291456 | tf_op jit(solution)/shard_map/all_to_all | solution.py:380
  217.6 8.6 %fusion.3 = f32[768,1536]{0,1:T(8,128)S(1)} fusion(bf16[768,2048]{1,0:T(8,128)(2,1)} %shard_map.129, bf16[1,2048,1536]{2,1,0:T(8,128)(2,1)} %param.16), kind=kOutput, calls=%fused_computation.4 | convolution fusion | flops 4831838208 | bytes 14155776 | tf_op jit(solution)/shard_map/dot_general | solution.py:456
  231.0 9.4 %fusion.7.rows = bf16[768,2048]{1,0:T(8,128)(2,1)} fusion(bf16[1,2048,1536]{2,1,0:T(8,128)(2,1)} %param.16, bf16[768,768]{0,1:T(8,128)(2,1)S(1)} %get-tuple-element.47, bf16[768,768]{0,1:T(8,128)(2,1)S(1)} %get-tuple-element.46), kind=kOutput, calls=%fused_computation.10 | convolution fusion | flops 4838129664 | bytes 11796480 | tf_op jit(solution)/shard_map/dot_general | solution.py:412
  240.4 4.0 %shard_map.130 = bf16[3072,512]{1,0:T(8,128)(2,1)} custom-call(bf16[768,2048]{1,0:T(8,128)(2,1)} %fusion.7.rows), custom_call_target="tpu_custom_call" | custom-call | flops 629145600 | bytes 6291456 | tf_op jit(solution)/shard_map/pallas_call | solution.py:322
  244.3 13.1 %all-to-all-done.2 = bf16[128,24,512]{2,1,0:T(8,128)(2,1)} async-done(((bf16[128,24,512]{2,1,0:T(8,128)(2,1)}), bf16[128,24,512]{2,1,0:T(8,128)(2,1)}, u32[]{:S(2)}, u32[]{:S(2)}) %all-to-all-start.2) | async-done | bytes 3145760 | tf_op jit(solution)/shard_map/all_to_all | solution.py:380
  257.4 7.1 %all-to-all-start.3 = ((bf16[128,24,512]{2,1,0:T(8,128)(2,1)}), bf16[128,24,512]{2,1,0:T(8,128)(2,1)}, u32[]{:S(2)}, u32[]{:S(2)}) async-start(bf16[128,24,512]{2,1,0:T(8,128)(2,1)} %bitcast.37), calls=%async_computation.3 | async-start | bytes 6291456 | tf_op jit(solution)/shard_map/all_to_all | solution.py:380
  264.5 7.8 %fusion.13 = bf16[1,768,2048]{2,1,0:T(8,128)(2,1)} fusion(bf16[768,2048]{1,0:T(8,128)(2,1)} %shard_map.124, f32[768,1536]{0,1:T(8,128)} %copy-done.8), kind=kOutput, calls=%fused_computation.14 | convolution fusion | flops 2421030912 | bytes 11010048 | tf_op jit(solution)/shard_map/dot_general | solution.py:464
  272.3 7.8 %fusion = bf16[1,2048,1536]{2,1,0:T(8,128)(2,1)} fusion(bf16[768,2048]{1,0:T(8,128)(2,1)S(1)} %copy-done.2, bf16[768,768]{0,1:T(8,128)(2,1)S(1)} %copy-done.12, bf16[768,768]{0,1:T(8,128)(2,1)S(1)} %copy-done.10), kind=kOutput, calls=%fused_computation.1 | convolution fusion | flops 4839702528 | bytes 11796480 | tf_op jit(solution)/shard_map/dot_general | solution.py:467
  280.1 4.5 %shard_map.131 = bf16[64,2048]{1,0:T(8,128)(2,1)} custom-call(s32[8,64]{1,0:T(8,128)} %get-tuple-element.25.key, f32[8,64]{1,0:T(8,128)} %get-tuple-element.26.wgt, bf16[3072,512]{1,0:T(8,128)(2,1)} %bitcast.11.got), custom_call_target="tpu_custom_call" | custom-call | flops 402653184 | bytes 3145728 | tf_op jit(solution)/shard_map/pallas_call | solution.py:368
  284.7 19.7 %all-to-all-done.3 = bf16[128,24,512]{2,1,0:T(8,128)(2,1)} async-done(((bf16[128,24,512]{2,1,0:T(8,128)(2,1)}), bf16[128,24,512]{2,1,0:T(8,128)(2,1)}, u32[]{:S(2)}, u32[]{:S(2)}) %all-to-all-start.3) | async-done | bytes 3145760 | tf_op jit(solution)/shard_map/all_to_all | solution.py:380
  304.4 4.0 %shard_map.132 = bf16[64,2048]{1,0:T(8,128)(2,1)} custom-call(s32[8,64]{1,0:T(8,128)} %get-tuple-element.43.key, f32[8,64]{1,0:T(8,128)} %get-tuple-element.44.wgt, bf16[3072,512]{1,0:T(8,128)(2,1)} %bitcast.13.got), custom_call_target="tpu_custom_call" | custom-call | flops 402653184 | bytes 3145728 | tf_op jit(solution)/shard_map/pallas_call | solution.py:368
  (55 shorter events, 35.8 us)
Async XLA Ops:
  0.6 193.8 %copy-start = (bf16[1,768,2048]{2,1,0:T(8,128)(2,1)S(1)}, bf16[1,768,2048]{2,1,0:T(8,128)(2,1)}, u32[]{:S(2)}) copy-start(bf16[1,768,2048]{2,1,0:T(8,128)(2,1)} %param.17) | copy-start | bytes 9437188
  2.7 15.9 %collective-permute-start.15 = (bf16[72,2048]{1,0:T(8,128)(2,1)}, bf16[72,2048]{1,0:T(8,128)(2,1)S(1)}, u32[]{:S(2)}, u32[]{:S(2)}) collective-permute-start(bf16[72,2048]{1,0:T(8,128)(2,1)} %get-tuple-element.37.refs_0_), channel_id=1, source_target_pairs={{0,96},{32,0},{64,32},{96,64},{1,97},{33,1},{65,33},{97,65},{2,98}... | collective-permute-start | bytes 884744 | tf_op jit(solution)/shard_map/ppermute | solution.py:384
  5.7 12.9 %collective-permute-start.14 = (bf16[72,2048]{1,0:T(8,128)(2,1)}, bf16[72,2048]{1,0:T(8,128)(2,1)}, u32[]{:S(2)}, u32[]{:S(2)}) collective-permute-start(bf16[72,2048]{1,0:T(8,128)(2,1)} %get-tuple-element.37.refs_0_), channel_id=1, source_target_pairs={{0,64},{32,96},{64,0},{96,32},{1,65},{33,97},{65,1},{97,33},{2,66}... | collective-permute-start | bytes 884744 | tf_op jit(solution)/shard_map/ppermute | solution.py:384
  6.4 16.0 %collective-permute-start.13 = (bf16[72,2048]{1,0:T(8,128)(2,1)}, bf16[72,2048]{1,0:T(8,128)(2,1)}, u32[]{:S(2)}, u32[]{:S(2)}) collective-permute-start(bf16[72,2048]{1,0:T(8,128)(2,1)} %get-tuple-element.37.refs_0_), channel_id=1, source_target_pairs={{0,32},{32,64},{64,96},{96,0},{1,33},{33,65},{65,97},{97,1},{2,34}... | collective-permute-start | bytes 884744 | tf_op jit(solution)/shard_map/ppermute | solution.py:384
  18.7 3.7 %copy-start.5 = (bf16[72,2048]{1,0:T(8,128)(2,1)}, bf16[72,2048]{1,0:T(8,128)(2,1)S(1)}, u32[]{:S(2)}) copy-start(bf16[72,2048]{1,0:T(8,128)(2,1)S(1)} %collective-permute-done.15.refs_3_) | copy-start | bytes 884740
  26.4 100.8 %all-to-all-start = ((bf16[32,4,24,512]{3,2,1,0:T(8,128)(2,1)}), bf16[32,4,24,512]{3,2,1,0:T(8,128)(2,1)}, u32[]{:S(2)}, u32[]{:S(2)}) async-start(bf16[32,4,24,512]{3,2,1,0:T(8,128)(2,1)} %shard_map.126), calls=%async_computation | async-start | bytes 6291456 | tf_op jit(solution)/shard_map/all_to_all | solution.py:380
  37.0 40.3 %collective-permute-start.2 = (bf16[72,2048]{1,0:T(8,128)(2,1)}, bf16[72,2048]{1,0:T(8,128)(2,1)S(1)}, u32[]{:S(2)}, u32[]{:S(2)}) collective-permute-start(bf16[72,2048]{1,0:T(8,128)(2,1)} %get-tuple-element.27), channel_id=1, source_target_pairs={{0,6},{2,0},{4,2},{6,4},{1,7},{3,1},{5,3},{7,5},{8,14},{10,8},{12,... | collective-permute-start | bytes 884744 | tf_op jit(solution)/shard_map/ppermute | solution.py:384
  37.8 46.2 %collective-permute-start.1 = (bf16[72,2048]{1,0:T(8,128)(2,1)}, bf16[72,2048]{1,0:T(8,128)(2,1)S(1)}, u32[]{:S(2)}, u32[]{:S(2)}) collective-permute-start(bf16[72,2048]{1,0:T(8,128)(2,1)} %get-tuple-element.27), channel_id=1, source_target_pairs={{0,4},{2,6},{4,0},{6,2},{1,5},{3,7},{5,1},{7,3},{8,12},{10,14},{12... | collective-permute-start | bytes 884744 | tf_op jit(solution)/shard_map/ppermute | solution.py:384
  38.7 46.4 %collective-permute-start = (bf16[72,2048]{1,0:T(8,128)(2,1)}, bf16[72,2048]{1,0:T(8,128)(2,1)S(1)}, u32[]{:S(2)}, u32[]{:S(2)}) collective-permute-start(bf16[72,2048]{1,0:T(8,128)(2,1)} %get-tuple-element.27), channel_id=1, source_target_pairs={{0,2},{2,4},{4,6},{6,0},{1,3},{3,5},{5,7},{7,1},{8,10},{10,12},{12... | collective-permute-start | bytes 884744 | tf_op jit(solution)/shard_map/ppermute | solution.py:384
  86.2 1.0 copy-start.3
  87.2 12.3 %copy-start.4 = (bf16[72,2048]{1,0:T(8,128)(2,1)S(1)}, bf16[72,2048]{1,0:T(8,128)(2,1)}, u32[]{:S(2)}) copy-start(bf16[72,2048]{1,0:T(8,128)(2,1)} %get-tuple-element.36.refs_0_) | copy-start | bytes 884740
  87.2 3.0 collective-permute-start.3
  96.2 38.0 %collective-permute-start.4 = (bf16[4,8,24,512]{3,2,1,0:T(8,128)(2,1)}, bf16[4,8,24,512]{3,2,1,0:T(8,128)(2,1)}, u32[]{:S(2)}, u32[]{:S(2)}) collective-permute-start(bf16[4,8,24,512]{3,2,1,0:T(8,128)(2,1)} %get-tuple-element.29), channel_id=1, source_target_pairs={{0,32},{32,64},{64,96},{96,0},{1,33},{33,65},{65,97},{97,1},{2,34}... | collective-permute-start | bytes 2359304 | tf_op jit(solution)/shard_map/ppermute | solution.py:384
  96.2 38.0 %collective-permute-start.5 = (bf16[4,8,24,512]{3,2,1,0:T(8,128)(2,1)}, bf16[4,8,24,512]{3,2,1,0:T(8,128)(2,1)}, u32[]{:S(2)}, u32[]{:S(2)}) collective-permute-start(bf16[4,8,24,512]{3,2,1,0:T(8,128)(2,1)} %get-tuple-element.30), channel_id=1, source_target_pairs={{0,64},{32,96},{64,0},{96,32},{1,65},{33,97},{65,1},{97,33},{2,66}... | collective-permute-start | bytes 2359304 | tf_op jit(solution)/shard_map/ppermute | solution.py:384
  98.3 36.5 %collective-permute-start.6 = (bf16[4,8,24,512]{3,2,1,0:T(8,128)(2,1)}, bf16[4,8,24,512]{3,2,1,0:T(8,128)(2,1)}, u32[]{:S(2)}, u32[]{:S(2)}) collective-permute-start(bf16[4,8,24,512]{3,2,1,0:T(8,128)(2,1)} %get-tuple-element.31), channel_id=1, source_target_pairs={{0,96},{32,0},{64,32},{96,64},{1,97},{33,1},{65,33},{97,65},{2,98}... | collective-permute-start | bytes 2359304 | tf_op jit(solution)/shard_map/ppermute | solution.py:384
  99.5 15.1 %collective-permute-start.12 = (bf16[72,2048]{1,0:T(8,128)(2,1)S(1)}, bf16[72,2048]{1,0:T(8,128)(2,1)S(1)}, u32[]{:S(2)}, u32[]{:S(2)}) collective-permute-start(bf16[72,2048]{1,0:T(8,128)(2,1)S(1)} %copy-done.4), channel_id=1, source_target_pairs={{0,24},{8,0},{16,8},{24,16},{1,25},{9,1},{17,9},{25,17},{2,26},{10... | collective-permute-start | bytes 884744 | tf_op jit(solution)/shard_map/ppermute | solution.py:384
  102.3 12.3 %collective-permute-start.11 = (bf16[72,2048]{1,0:T(8,128)(2,1)S(1)}, bf16[72,2048]{1,0:T(8,128)(2,1)S(1)}, u32[]{:S(2)}, u32[]{:S(2)}) collective-permute-start(bf16[72,2048]{1,0:T(8,128)(2,1)S(1)} %copy-done.4), channel_id=1, source_target_pairs={{0,16},{8,24},{16,0},{24,8},{1,17},{9,25},{17,1},{25,9},{2,18},{10... | collective-permute-start | bytes 884744 | tf_op jit(solution)/shard_map/ppermute | solution.py:384
  114.6 0.7 copy-start.6
  114.6 8.5 %collective-permute-start.10 = (bf16[72,2048]{1,0:T(8,128)(2,1)S(1)}, bf16[72,2048]{1,0:T(8,128)(2,1)}, u32[]{:S(2)}, u32[]{:S(2)}) collective-permute-start(bf16[72,2048]{1,0:T(8,128)(2,1)S(1)} %copy-done.4), channel_id=1, source_target_pairs={{0,8},{8,16},{16,24},{24,0},{1,9},{9,17},{17,25},{25,1},{2,10},{10... | collective-permute-start | bytes 884744 | tf_op jit(solution)/shard_map/ppermute | solution.py:384
  127.2 75.4 %all-to-all-start.1 = ((bf16[32,4,24,512]{3,2,1,0:T(8,128)(2,1)}), bf16[32,4,24,512]{3,2,1,0:T(8,128)(2,1)}, u32[]{:S(2)}, u32[]{:S(2)}) async-start(bf16[32,4,24,512]{3,2,1,0:T(8,128)(2,1)} %shard_map.125), calls=%async_computation.1 | async-start | bytes 6291456 | tf_op jit(solution)/shard_map/all_to_all | solution.py:380
  138.4 23.2 %collective-permute-start.7 = (bf16[4,8,24,512]{3,2,1,0:T(8,128)(2,1)}, bf16[4,8,24,512]{3,2,1,0:T(8,128)(2,1)}, u32[]{:S(2)}, u32[]{:S(2)}) collective-permute-start(bf16[4,8,24,512]{3,2,1,0:T(8,128)(2,1)} %get-tuple-element.33), channel_id=1, source_target_pairs={{0,8},{8,16},{16,24},{24,0},{1,9},{9,17},{17,25},{25,1},{2,10},{10... | collective-permute-start | bytes 2359304 | tf_op jit(solution)/shard_map/ppermute | solution.py:384
  143.3 33.0 %collective-permute-start.8 = (bf16[4,8,24,512]{3,2,1,0:T(8,128)(2,1)}, bf16[4,8,24,512]{3,2,1,0:T(8,128)(2,1)}, u32[]{:S(2)}, u32[]{:S(2)}) collective-permute-start(bf16[4,8,24,512]{3,2,1,0:T(8,128)(2,1)} %get-tuple-element.34), channel_id=1, source_target_pairs={{0,16},{8,24},{16,0},{24,8},{1,17},{9,25},{17,1},{25,9},{2,18},{10... | collective-permute-start | bytes 2359304 | tf_op jit(solution)/shard_map/ppermute | solution.py:384
  143.3 33.0 %collective-permute-start.9 = (bf16[4,8,24,512]{3,2,1,0:T(8,128)(2,1)}, bf16[4,8,24,512]{3,2,1,0:T(8,128)(2,1)}, u32[]{:S(2)}, u32[]{:S(2)}) collective-permute-start(bf16[4,8,24,512]{3,2,1,0:T(8,128)(2,1)} %get-tuple-element.35), channel_id=1, source_target_pairs={{0,24},{8,0},{16,8},{24,16},{1,25},{9,1},{17,9},{25,17},{2,26},{10... | collective-permute-start | bytes 2359304 | tf_op jit(solution)/shard_map/ppermute | solution.py:384
  207.4 50.0 %all-to-all-start.2 = ((bf16[128,24,512]{2,1,0:T(8,128)(2,1)}), bf16[128,24,512]{2,1,0:T(8,128)(2,1)}, u32[]{:S(2)}, u32[]{:S(2)}) async-start(bf16[128,24,512]{2,1,0:T(8,128)(2,1)} %bitcast.38), calls=%async_computation.2 | async-start | bytes 6291456 | tf_op jit(solution)/shard_map/all_to_all | solution.py:380
  217.6 8.6 %copy-start.1 = (bf16[768,2048]{1,0:T(8,128)(2,1)S(1)}, bf16[768,2048]{1,0:T(8,128)(2,1)}, u32[]{:S(2)}) copy-start(bf16[768,2048]{1,0:T(8,128)(2,1)} %shard_map.124) | copy-start | bytes 9437188
  226.2 3.3 %copy-start.8 = (f32[768,1536]{0,1:T(8,128)}, f32[768,1536]{0,1:T(8,128)S(1)}, u32[]{:S(2)}) copy-start(f32[768,1536]{0,1:T(8,128)S(1)} %fusion.3) | copy-start | bytes 14155780
  229.6 1.0 copy-start.9
  229.6 1.4 copy-start.11
  257.4 47.0 %all-to-all-start.3 = ((bf16[128,24,512]{2,1,0:T(8,128)(2,1)}), bf16[128,24,512]{2,1,0:T(8,128)(2,1)}, u32[]{:S(2)}, u32[]{:S(2)}) async-start(bf16[128,24,512]{2,1,0:T(8,128)(2,1)} %bitcast.37), calls=%async_computation.3 | async-start | bytes 6291456 | tf_op jit(solution)/shard_map/all_to_all | solution.py:380
  264.5 7.8 %copy-start.2 = (bf16[768,2048]{1,0:T(8,128)(2,1)S(1)}, bf16[768,2048]{1,0:T(8,128)(2,1)}, u32[]{:S(2)}) copy-start(bf16[768,2048]{1,0:T(8,128)(2,1)} %shard_map.129) | copy-start | bytes 9437188
  264.5 7.8 %copy-start.10 = (bf16[768,768]{0,1:T(8,128)(2,1)S(1)}, bf16[768,768]{0,1:T(8,128)(2,1)}, u32[]{:S(2)}) copy-start(bf16[768,768]{0,1:T(8,128)(2,1)} %copy-done.9) | copy-start | bytes 3538948
  264.5 7.8 %copy-start.12 = (bf16[768,768]{0,1:T(8,128)(2,1)S(1)}, bf16[768,768]{0,1:T(8,128)(2,1)}, u32[]{:S(2)}) copy-start(bf16[768,768]{0,1:T(8,128)(2,1)} %copy-done.11) | copy-start | bytes 3538948
  (1 other events, 0.7 us)

commit v5 on v4

--- a/solution.py
+++ b/solution.py
@@ -60,11 +60,6 @@
 def fill(pieces, chunks):
     for k in range(pieces.shape[0]):
         pieces[k] = chunks[:, k * LANES : (k + 1) * LANES].astype(F32)
-
-
-def flush(pieces, out, first):
-    for k in range(pieces.shape[0]):
-        out[:, first + k * LANES : first + (k + 1) * LANES] = pieces[k].astype(BF16)
 
 
 def place(experts, capacity, ids, sc, key, wgt):
@@ -132,46 +127,43 @@
 
 
 def plane_body(along, capacity, *refs):
-    *pays, out, pieces = refs
-    dests = out.shape[0]
-    rows = dests * capacity
+    *pays, out = refs
+    rows, width = out.shape
     tok = pays[0].shape[0] - TOP
     here = lax.axis_index(along)
     mine = pl.program_id(0) * rows + lax.broadcasted_iota(jnp.int32, (rows, tok), 0)
+    picks = []
     for s, pay in enumerate(pays):
         ids = fact(pay, tok, 0).astype(jnp.int32)
         slot = fact(pay, tok, 1).astype(jnp.int32)
         y, z, x, c = coordinates(ids)
         near, far = (y, z) if along == "y" else (z, y)
-        want = jnp.where(near == here, ((far * 4 + x) * 2 + c) * capacity + slot, -1)
+        place_of = ((far * 4 + x) * 2 + c) * len(pays) + s
+        want = jnp.where(near == here, place_of * capacity + slot, -1)
         pick = jnp.zeros((rows, tok), F32)
         for j in range(TOP):
             pick = jnp.where(mine == want[j : j + 1, :], 1.0, pick)
-        pick = pick.astype(BF16)
-        piece = pay.shape[1] // PARTS
-        for q in range(PARTS):
-            got = jnp.dot(
-                pick, pay[:tok, q * piece : (q + 1) * piece], preferred_element_type=F32
-            )
-            spread(pieces, q, got)
-        for k in range(pieces.shape[0]):
-            out[:, s, :, k * LANES : (k + 1) * LANES] = (
-                pieces[k].reshape(dests, capacity * PARTS, LANES).astype(BF16)
-            )
+        picks.append(pick.astype(BF16))
+    piece = width // PARTS
+    for q in range(PARTS):
+        lanes = slice(q * piece, (q + 1) * piece)
+        got = jnp.zeros((rows, piece), F32)
+        for pick, pay in zip(picks, pays):
+            got = got + jnp.dot(pick, pay[:tok, lanes], preferred_element_type=F32)
+        out[:, lanes] = got.astype(BF16)
 
 
 def plane(along, capacity, pays):
     tall, width = pays[0].shape
     steps = 2
-    shape = (32, len(pays), capacity * PARTS, width // PARTS)
+    rows = 32 * len(pays) * capacity
     return call(
         functools.partial(plane_body, along, capacity),
         (steps,),
         [whole((tall, width))] * len(pays),
-        pl.BlockSpec((shape[0] // steps,) + shape[1:], lambda i: (i, 0, 0, 0)),
-        jax.ShapeDtypeStruct(shape, BF16),
+        pl.BlockSpec((rows // steps, width), lambda i: (i, 0)),
+        jax.ShapeDtypeStruct((rows, width), BF16),
         (2_000_000_000, 8_000_000),
-        [pltpu.VMEM((width // PARTS // LANES, 32 // steps * capacity * PARTS, LANES), F32)],
     )(*pays)
 
 
@@ -259,27 +251,9 @@
         out[:, q * piece : (q + 1) * piece] = collected(pieces, q, 0, piece)
 
 
-def unplane_body(along, got, out, pieces):
-    here = lax.axis_index(along)
-
-    @pl.loop(0, got.shape[0])
-    def _(d):
-        for s in range(got.shape[1]):
-            back = (here - s) & 3
-            if along == "y":
-                pos = back * 32 + d
-            else:
-                pos = (d >> 3) * 32 + back * 8 + (d & 7)
-            settle(pieces, got.at[d, s], pos)
-
-    lay_out(pieces, out)
-
-
 def unrings_body(t0, t1, t2, t3, out, pieces):
-    my_y, my_z = lax.axis_index("y"), lax.axis_index("z")
-    my_x, my_c = lax.axis_index("x"), lax.axis_index("c")
+    my_y, my_x, my_c = lax.axis_index("y"), lax.axis_index("x"), lax.axis_index("c")
     for turn, got in enumerate((t0, t1, t2, t3)):
-        z = (my_z - turn) & 3
 
         @pl.loop(0, got.shape[0])
         def _(s):
@@ -287,7 +261,7 @@
             for b in range(got.shape[1]):
                 x = (my_x - b % 4) & 3
                 c = my_c if b < 4 else 1 - my_c
-                settle(pieces, got.at[s, b], ((y * 4 + z) * 4 + x) * 2 + c)
+                settle(pieces, got.at[s, b], ((y * 4 + x) * 2 + c) * 4 + turn)
 
     lay_out(pieces, out)
 
@@ -306,28 +280,41 @@
     )(*got)
 
 
-def pack_body(rows, out, pieces):
-    width = rows.shape[1]
-    piece = width // PARTS
+def pack_body(along, rows, out, pieces):
+    piece = rows.shape[1] // PARTS
+    size = out.shape[1]
+    here = lax.axis_index(along)
     for q in range(PARTS):
         spread(pieces, q, rows[:, q * piece : (q + 1) * piece].astype(F32))
-    flush(pieces, out, 0)
-
-
-def pack(rows):
+
+    @pl.loop(0, out.shape[0] // 4)
+    def _(d):
+        for s in range(4):
+            back = (here - s) & 3
+            if along == "y":
+                pos = back * 32 + d
+            else:
+                pos = (d >> 3) * 32 + back * 8 + (d & 7)
+            start = pl.multiple_of((d * 4 + s) * size, 8)
+            for k in range(pieces.shape[0]):
+                out[pos, :, k * LANES : (k + 1) * LANES] = pieces[
+                    k, pl.ds(start, size), :
+                ].astype(BF16)
+
+
+def pack(along, capacity, rows):
     total, width = rows.shape
-    steps = 2
     piece = width // PARTS
-    count = total // steps
-    return call(
-        pack_body,
-        (steps,),
-        [pl.BlockSpec((count, width), lambda i: (i, 0))],
-        pl.BlockSpec((count * PARTS, piece), lambda i: (i, 0)),
-        jax.ShapeDtypeStruct((total * PARTS, piece), BF16),
+    shape = (total // capacity, capacity * PARTS, piece)
+    return call(
+        functools.partial(pack_body, along),
+        (1,),
+        [whole((total, width))],
+        whole(shape),
+        jax.ShapeDtypeStruct(shape, BF16),
         (400 * total * width, 4 * total * width),
-        [pltpu.VMEM((piece // LANES, count * PARTS, LANES), F32)],
-    )(rows)
+        [pltpu.VMEM((piece // LANES, total * PARTS, LANES), F32)],
+    )(rows).reshape(total * PARTS, piece)
 
 
 def combine_body(weighted, key, wgt, got, out, total, pieces):
@@ -444,19 +431,18 @@
     out_b, in_f = lax.optimization_barrier((out_b, in_f))
     in_b = exchange(out_b, ("y", "x", "c"))
 
-    rows_f = rows_of(functools.partial(unplane_body, "y"), in_f)
     by_z = regroup(by_y)
     in_c = [by_z[0]] + [turned(by_z[turn], "z", turn) for turn in (1, 2, 3)]
-    out_rows = expert_forward(rows_f, w_in, w_down)
-    back_f = pack(out_rows)
+    out_rows = expert_forward(in_f, w_in, w_down)
+    back_f = pack("y", capacity, out_rows)
     back_f, in_b = lax.optimization_barrier((back_f, in_b))
     home_f = exchange(back_f)
 
-    rows_b = rows_of(functools.partial(unplane_body, "z"), in_b)
+    rows_b = in_b
     projected = jnp.dot(rows_b, w_in, preferred_element_type=F32)
     cot_b = rows_of(unrings_body, *in_c)
     row_grad, hidden, d_proj = expert_backward(projected, cot_b, w_in, w_down)
-    back_b = pack(row_grad)
+    back_b = pack("z", capacity, row_grad)
     back_b, home_f = lax.optimization_barrier((back_b, home_f))
     home_b = exchange(back_b)
 

time: 312 us -> 315 us (level)
  waiting for transfers between devices: 144 us -> 151 us
    ppermute x15, waiting for transfers between devices: 109 us -> 121 us  [turned(): return lax.ppermute(x, axis, [(i, (i + turn) % 4) for i in range(4)])]
    pallas_call x3 -> x1, Pallas kernels: 14.5 us -> 4.77 us  [rows_of(): call(body, (1,), [whole(g.shape) for g in got], whole((total // PARTS, pi...]
    pallas_call x2, Pallas kernels: 8.03 us -> 12.6 us  [plane(): call(functools.partial(plane_body, along, capacity), (steps,), [whole((ta...]
  transfers between devices with their start and end apart: 20 -> 20, of which waited for: 14 -> 14; matrix products, arithmetic and copies ran while one was open for 16% -> 17% of each run, Pallas kernels for 12% -> 12%
where the time goes in v5:
time: 315 us; the launch traced here: 311 us
  waiting for transfers between devices  151 us (48%)
  starting transfers between devices  54.2 us (17%)
  matrix products  51.3 us (16%)
  Pallas kernels  50 us (16%)
    ppermute x15, waiting for transfers between devices, turned(): return lax.ppermute(x, axis, [(i, (i + turn) % 4) for i in range(4)])  121 us
    all_to_all x4, starting transfers between devices, exchange(): return lax.all_to_all(x, axes, split_axis=0, concat_axis=0, tiled=True)  30.4 us
    all_to_all x4, waiting for transfers between devices, exchange(): return lax.all_to_all(x, axes, split_axis=0, concat_axis=0, tiled=True)  29.9 us
    ppermute x15, starting transfers between devices, turned(): return lax.ppermute(x, axis, [(i, (i + turn) % 4) for i in range(4)])  23.9 us
    pallas_call x2, Pallas kernels, plane(): call(functools.partial(plane_body, along, capacity), (steps,), [whole((ta...  12.6 us
    pallas_call x2, Pallas kernels, pack(): call(functools.partial(pack_body, along), (1,), [whole((total, width))],...  10.3 us
    dot_general x1, matrix products, layer(): lax.dot_general(rows_b, d_proj, ROWS_BY_ROWS, preferred_element_type=F32)  9.6 us
    dot_general x1, matrix products, expert_backward(): lax.dot_general(d_proj, w_in, COLS_BY_COLS, preferred_element_type=F32)  9.38 us
  transfers between devices with their start and end apart: 20, of which 14 were waited for; matrix products, arithmetic and copies ran while one was open for 17% of the time, Pallas kernels for 12%

profile of v5, /device:TPU:6, one launch (start us, length us, event | category | flops | bytes accessed | tf_op | source)
XLA Modules:
  0.0 311.4 jit_solution(2972102387404749164)
XLA Ops:
  7.3 11.3 %collective-permute-done.15.refs_3_ = bf16[72,2048]{1,0:T(8,128)(2,1)S(1)} collective-permute-done((bf16[72,2048]{1,0:T(8,128)(2,1)}, bf16[72,2048]{1,0:T(8,128)(2,1)S(1)}, u32[]{:S(2)}, u32[]{:S(2)}) %collective-permute-start.15) | collective-permute-done | bytes 294944 | tf_op jit(solution)/shard_map/ppermute | solution.py:371
  18.7 3.7 %collective-permute-done.13.refs_1_ = bf16[72,2048]{1,0:T(8,128)(2,1)} collective-permute-done((bf16[72,2048]{1,0:T(8,128)(2,1)}, bf16[72,2048]{1,0:T(8,128)(2,1)}, u32[]{:S(2)}, u32[]{:S(2)}) %collective-permute-start.13) | collective-permute-done | bytes 294944 | tf_op jit(solution)/shard_map/ppermute | solution.py:371
  22.4 6.3 %shard_map.126 = bf16[768,2048]{1,0:T(8,128)(2,1)} custom-call(bf16[72,2048]{1,0:T(8,128)(2,1)} %get-tuple-element.37.refs_0_, bf16[72,2048]{1,0:T(8,128)(2,1)} %collective-permute-done.13.refs_1_, bf16[72,2048]{1,0:T(8,128)(2,1)} %collective-permute-done.14.refs_2_, bf16[72,2048]{1,0:T(8,128)(2,1)} %copy-done.4), custom_call_target="tpu_custom_call" | custom-call | flops 2000000000 | bytes 8000000 | tf_op jit(solution)/shard_map/pallas_call | solution.py:160
  28.6 8.5 %all-to-all-start = ((bf16[32,24,2048]{2,1,0:T(8,128)(2,1)}), bf16[32,24,2048]{2,1,0:T(8,128)(2,1)}, u32[]{:S(2)}, u32[]{:S(2)}) async-start(bf16[32,24,2048]{2,1,0:T(8,128)(2,1)} %bitcast.43), calls=%async_computation | async-start | bytes 6291456 | tf_op jit(solution)/shard_map/all_to_all | solution.py:367
  43.3 36.2 %collective-permute-done.2 = bf16[72,2048]{1,0:T(8,128)(2,1)S(1)} collective-permute-done((bf16[72,2048]{1,0:T(8,128)(2,1)}, bf16[72,2048]{1,0:T(8,128)(2,1)S(1)}, u32[]{:S(2)}, u32[]{:S(2)}) %collective-permute-start.2) | collective-permute-done | bytes 294944 | tf_op jit(solution)/shard_map/ppermute | solution.py:371
  79.6 6.8 %collective-permute-done.1 = bf16[72,2048]{1,0:T(8,128)(2,1)S(1)} collective-permute-done((bf16[72,2048]{1,0:T(8,128)(2,1)}, bf16[72,2048]{1,0:T(8,128)(2,1)S(1)}, u32[]{:S(2)}, u32[]{:S(2)}) %collective-permute-start.1) | collective-permute-done | bytes 294944 | tf_op jit(solution)/shard_map/ppermute | solution.py:371
  92.5 6.1 %shard_map.122 = (bf16[4,8,24,512]{3,2,1,0:T(8,128)(2,1)}, bf16[4,8,24,512]{3,2,1,0:T(8,128)(2,1)}, bf16[4,8,24,512]{3,2,1,0:T(8,128)(2,1)}, bf16[4,8,24,512]{3,2,1,0:T(8,128)(2,1)}) custom-call(bf16[4,72,2048]{2,1,0:T(8,128)(2,1)} %copy-done.2, bf16[4,72,2048]{2,1,0:T(8,128)(2,1)} %collective-permute-done.3.other), custom_call_target="tpu_custom_call" | custom-call | flops 2000000000 | bytes 8000000 | tf_op jit(solution)/shard_map/pallas_call | solution.py:211
  105.5 7.7 %collective-permute-done.11.refs_2_ = bf16[72,2048]{1,0:T(8,128)(2,1)S(1)} collective-permute-done((bf16[72,2048]{1,0:T(8,128)(2,1)S(1)}, bf16[72,2048]{1,0:T(8,128)(2,1)S(1)}, u32[]{:S(2)}, u32[]{:S(2)}) %collective-permute-start.11) | collective-permute-done | bytes 294944 | tf_op jit(solution)/shard_map/ppermute | solution.py:371
  113.9 4.3 %collective-permute-done.10.refs_1_ = bf16[72,2048]{1,0:T(8,128)(2,1)} collective-permute-done((bf16[72,2048]{1,0:T(8,128)(2,1)S(1)}, bf16[72,2048]{1,0:T(8,128)(2,1)}, u32[]{:S(2)}, u32[]{:S(2)}) %collective-permute-start.10) | collective-permute-done | bytes 294944 | tf_op jit(solution)/shard_map/ppermute | solution.py:371
  118.2 6.3 %shard_map.125 = bf16[768,2048]{1,0:T(8,128)(2,1)} custom-call(bf16[72,2048]{1,0:T(8,128)(2,1)} %get-tuple-element.36.refs_0_, bf16[72,2048]{1,0:T(8,128)(2,1)} %collective-permute-done.10.refs_1_, bf16[72,2048]{1,0:T(8,128)(2,1)} %copy-done.5, bf16[72,2048]{1,0:T(8,128)(2,1)} %collective-permute-done.12.refs_3_), custom_call_target="tpu_custom_call" | custom-call | flops 2000000000 | bytes 8000000 | tf_op jit(solution)/shard_map/pallas_call | solution.py:160
  124.5 7.0 %all-to-all-start.1 = ((bf16[32,24,2048]{2,1,0:T(8,128)(2,1)}), bf16[32,24,2048]{2,1,0:T(8,128)(2,1)}, u32[]{:S(2)}, u32[]{:S(2)}) async-start(bf16[32,24,2048]{2,1,0:T(8,128)(2,1)} %bitcast.44), calls=%async_computation.1 | async-start | bytes 6291456 | tf_op jit(solution)/shard_map/all_to_all | solution.py:367
  131.4 6.1 %collective-permute-done.4.refs_1_ = bf16[4,8,24,512]{3,2,1,0:T(8,128)(2,1)} collective-permute-done((bf16[4,8,24,512]{3,2,1,0:T(8,128)(2,1)}, bf16[4,8,24,512]{3,2,1,0:T(8,128)(2,1)}, u32[]{:S(2)}, u32[]{:S(2)}) %collective-permute-start.4) | collective-permute-done | bytes 786464 | tf_op jit(solution)/shard_map/ppermute | solution.py:371
  137.5 12.2 %collective-permute-done.6.refs_3_ = bf16[4,8,24,512]{3,2,1,0:T(8,128)(2,1)} collective-permute-done((bf16[4,8,24,512]{3,2,1,0:T(8,128)(2,1)}, bf16[4,8,24,512]{3,2,1,0:T(8,128)(2,1)}, u32[]{:S(2)}, u32[]{:S(2)}) %collective-permute-start.6) | collective-permute-done | bytes 786464 | tf_op jit(solution)/shard_map/ppermute | solution.py:371
  149.8 3.5 %shard_map.123 = (bf16[4,8,24,512]{3,2,1,0:T(8,128)(2,1)}, bf16[4,8,24,512]{3,2,1,0:T(8,128)(2,1)}, bf16[4,8,24,512]{3,2,1,0:T(8,128)(2,1)}, bf16[4,8,24,512]{3,2,1,0:T(8,128)(2,1)}) custom-call(bf16[4,8,24,512]{3,2,1,0:T(8,128)(2,1)} %get-tuple-element.28.refs_0_, bf16[4,8,24,512]{3,2,1,0:T(8,128)(2,1)} %collective-permute-done.4.refs_1_, ...), custom_call_target="tpu_custom_call" | custom-call | flops 1000000000 | bytes 8000000 | tf_op jit(solution)/shard_map/pallas_call | solution.py:231
  155.1 3.6 %collective-permute-start.8 = (bf16[4,8,24,512]{3,2,1,0:T(8,128)(2,1)}, bf16[4,8,24,512]{3,2,1,0:T(8,128)(2,1)}, u32[]{:S(2)}, u32[]{:S(2)}) collective-permute-start(bf16[4,8,24,512]{3,2,1,0:T(8,128)(2,1)} %get-tuple-element.34), channel_id=1, source_target_pairs={{0,16},{8,24},{16,0},{24,8},{1,17},{9,25},{17,1},{25,9},{2,18},{10... | collective-permute-start | bytes 2359304 | tf_op jit(solution)/shard_map/ppermute | solution.py:371
  158.7 16.3 %collective-permute-done.7.t1 = bf16[4,8,24,512]{3,2,1,0:T(8,128)(2,1)} collective-permute-done((bf16[4,8,24,512]{3,2,1,0:T(8,128)(2,1)}, bf16[4,8,24,512]{3,2,1,0:T(8,128)(2,1)}, u32[]{:S(2)}, u32[]{:S(2)}) %collective-permute-start.7) | collective-permute-done | bytes 786464 | tf_op jit(solution)/shard_map/ppermute | solution.py:371
  175.0 15.2 %collective-permute-done.8.t2 = bf16[4,8,24,512]{3,2,1,0:T(8,128)(2,1)} collective-permute-done((bf16[4,8,24,512]{3,2,1,0:T(8,128)(2,1)}, bf16[4,8,24,512]{3,2,1,0:T(8,128)(2,1)}, u32[]{:S(2)}, u32[]{:S(2)}) %collective-permute-start.8) | collective-permute-done | bytes 786464 | tf_op jit(solution)/shard_map/ppermute | solution.py:371
  190.2 4.8 %shard_map.124 = bf16[768,2048]{1,0:T(8,128)(2,1)} custom-call(bf16[4,8,24,512]{3,2,1,0:T(8,128)(2,1)} %get-tuple-element.32.t0, bf16[4,8,24,512]{3,2,1,0:T(8,128)(2,1)} %collective-permute-done.7.t1, bf16[4,8,24,512]{3,2,1,0:T(8,128)(2,1)} %collective-permute-done.8.t2, bf16[4,8,24,512]{3,2,1,0:T(8,128)(2,1)} %collective-permute-done.9.t3), custom_call_target="tpu_custom_call" | custom-call | flops 629145600 | bytes 6291456 | tf_op jit(solution)/shard_map/pallas_call | solution.py:272
  194.9 8.5 %fusion.5 = f32[768,1536]{0,1:T(8,128)S(1)} fusion(bf16[768,2048]{1,0:T(8,128)(2,1)} %bitcast.10, bf16[1,2048,1536]{2,1,0:T(8,128)(2,1)} %param.16), kind=kOutput, calls=%fused_computation.6 | convolution fusion | flops 4831838208 | bytes 14155776 | tf_op jit(solution)/shard_map/dot_general | solution.py:384
  203.4 4.2 %convolution_convert_fusion.2.rows = bf16[768,2048]{1,0:T(8,128)(2,1)} fusion(bf16[1,768,2048]{2,1,0:T(8,128)(2,1)S(1)} %copy-done, f32[768,1536]{0,1:T(8,128)S(1)} %fusion.5), kind=kOutput, calls=%fused_computation.9 | convolution fusion | flops 2421030912 | bytes 11010048 | tf_op jit(solution)/shard_map/dot_general | solution.py:387
  207.6 5.2 %shard_map.127 = bf16[128,24,512]{2,1,0:T(8,128)(2,1)} custom-call(bf16[768,2048]{1,0:T(8,128)(2,1)} %convolution_convert_fusion.2.rows), custom_call_target="tpu_custom_call" | custom-call | flops 629145600 | bytes 6291456 | tf_op jit(solution)/shard_map/pallas_call | solution.py:309
  212.8 7.9 %all-to-all-start.2 = ((bf16[128,24,512]{2,1,0:T(8,128)(2,1)}), bf16[128,24,512]{2,1,0:T(8,128)(2,1)}, u32[]{:S(2)}, u32[]{:S(2)}) async-start(bf16[128,24,512]{2,1,0:T(8,128)(2,1)} %shard_map.127), calls=%async_computation.2 | async-start | bytes 6291456 | tf_op jit(solution)/shard_map/all_to_all | solution.py:367
  220.7 8.6 %fusion.3 = f32[768,1536]{0,1:T(8,128)S(1)} fusion(bf16[768,2048]{1,0:T(8,128)(2,1)} %bitcast.14, bf16[1,2048,1536]{2,1,0:T(8,128)(2,1)} %param.16), kind=kOutput, calls=%fused_computation.4 | convolution fusion | flops 4831838208 | bytes 14155776 | tf_op jit(solution)/shard_map/dot_general | solution.py:442
  234.0 9.4 %fusion.7.rows = bf16[768,2048]{1,0:T(8,128)(2,1)} fusion(bf16[1,2048,1536]{2,1,0:T(8,128)(2,1)} %param.16, bf16[768,768]{0,1:T(8,128)(2,1)S(1)} %get-tuple-element.47, bf16[768,768]{0,1:T(8,128)(2,1)S(1)} %get-tuple-element.46), kind=kOutput, calls=%fused_computation.10 | convolution fusion | flops 4838129664 | bytes 11796480 | tf_op jit(solution)/shard_map/dot_general | solution.py:399
  243.4 5.2 %shard_map.128 = bf16[128,24,512]{2,1,0:T(8,128)(2,1)} custom-call(bf16[768,2048]{1,0:T(8,128)(2,1)} %fusion.7.rows), custom_call_target="tpu_custom_call" | custom-call | flops 629145600 | bytes 6291456 | tf_op jit(solution)/shard_map/pallas_call | solution.py:309
  248.6 11.9 %all-to-all-done.2 = bf16[128,24,512]{2,1,0:T(8,128)(2,1)} async-done(((bf16[128,24,512]{2,1,0:T(8,128)(2,1)}), bf16[128,24,512]{2,1,0:T(8,128)(2,1)}, u32[]{:S(2)}, u32[]{:S(2)}) %all-to-all-start.2) | async-done | bytes 3145760 | tf_op jit(solution)/shard_map/all_to_all | solution.py:367
  260.5 7.1 %all-to-all-start.3 = ((bf16[128,24,512]{2,1,0:T(8,128)(2,1)}), bf16[128,24,512]{2,1,0:T(8,128)(2,1)}, u32[]{:S(2)}, u32[]{:S(2)}) async-start(bf16[128,24,512]{2,1,0:T(8,128)(2,1)} %shard_map.128), calls=%async_computation.3 | async-start | bytes 6291456 | tf_op jit(solution)/shard_map/all_to_all | solution.py:367
  267.6 7.8 %fusion.13 = bf16[1,768,2048]{2,1,0:T(8,128)(2,1)} fusion(bf16[768,2048]{1,0:T(8,128)(2,1)} %shard_map.124, f32[768,1536]{0,1:T(8,128)} %copy-done.6), kind=kOutput, calls=%fused_computation.14 | convolution fusion | flops 2421030912 | bytes 11010048 | tf_op jit(solution)/shard_map/dot_general | solution.py:450
  275.3 9.6 %fusion = bf16[1,2048,1536]{2,1,0:T(8,128)(2,1)} fusion(bf16[768,2048]{1,0:T(8,128)(2,1)} %bitcast.14, bf16[768,768]{0,1:T(8,128)(2,1)S(1)} %copy-done.10, bf16[768,768]{0,1:T(8,128)(2,1)S(1)} %copy-done.8), kind=kOutput, calls=%fused_computation.1 | convolution fusion | flops 4839702528 | bytes 11796480 | tf_op jit(solution)/shard_map/dot_general | solution.py:453
  284.9 4.5 %shard_map.129 = bf16[64,2048]{1,0:T(8,128)(2,1)} custom-call(s32[8,64]{1,0:T(8,128)} %get-tuple-element.25.key, f32[8,64]{1,0:T(8,128)} %get-tuple-element.26.wgt, bf16[3072,512]{1,0:T(8,128)(2,1)} %bitcast.17.got), custom_call_target="tpu_custom_call" | custom-call | flops 402653184 | bytes 3145728 | tf_op jit(solution)/shard_map/pallas_call | solution.py:355
  289.5 18.0 %all-to-all-done.3 = bf16[128,24,512]{2,1,0:T(8,128)(2,1)} async-done(((bf16[128,24,512]{2,1,0:T(8,128)(2,1)}), bf16[128,24,512]{2,1,0:T(8,128)(2,1)}, u32[]{:S(2)}, u32[]{:S(2)}) %all-to-all-start.3) | async-done | bytes 3145760 | tf_op jit(solution)/shard_map/all_to_all | solution.py:367
  307.4 4.0 %shard_map.130 = bf16[64,2048]{1,0:T(8,128)(2,1)} custom-call(s32[8,64]{1,0:T(8,128)} %get-tuple-element.43.key, f32[8,64]{1,0:T(8,128)} %get-tuple-element.44.wgt, bf16[3072,512]{1,0:T(8,128)(2,1)} %bitcast.19.got), custom_call_target="tpu_custom_call" | custom-call | flops 402653184 | bytes 3145728 | tf_op jit(solution)/shard_map/pallas_call | solution.py:355
  (49 shorter events, 33.2 us)
Async XLA Ops:
  0.6 202.8 %copy-start = (bf16[1,768,2048]{2,1,0:T(8,128)(2,1)S(1)}, bf16[1,768,2048]{2,1,0:T(8,128)(2,1)}, u32[]{:S(2)}) copy-start(bf16[1,768,2048]{2,1,0:T(8,128)(2,1)} %param.17) | copy-start | bytes 9437188
  2.7 15.9 %collective-permute-start.15 = (bf16[72,2048]{1,0:T(8,128)(2,1)}, bf16[72,2048]{1,0:T(8,128)(2,1)S(1)}, u32[]{:S(2)}, u32[]{:S(2)}) collective-permute-start(bf16[72,2048]{1,0:T(8,128)(2,1)} %get-tuple-element.37.refs_0_), channel_id=1, source_target_pairs={{0,96},{32,0},{64,32},{96,64},{1,97},{33,1},{65,33},{97,65},{2,98}... | collective-permute-start | bytes 884744 | tf_op jit(solution)/shard_map/ppermute | solution.py:371
  5.7 12.9 %collective-permute-start.14 = (bf16[72,2048]{1,0:T(8,128)(2,1)}, bf16[72,2048]{1,0:T(8,128)(2,1)}, u32[]{:S(2)}, u32[]{:S(2)}) collective-permute-start(bf16[72,2048]{1,0:T(8,128)(2,1)} %get-tuple-element.37.refs_0_), channel_id=1, source_target_pairs={{0,64},{32,96},{64,0},{96,32},{1,65},{33,97},{65,1},{97,33},{2,66}... | collective-permute-start | bytes 884744 | tf_op jit(solution)/shard_map/ppermute | solution.py:371
  6.4 16.0 %collective-permute-start.13 = (bf16[72,2048]{1,0:T(8,128)(2,1)}, bf16[72,2048]{1,0:T(8,128)(2,1)}, u32[]{:S(2)}, u32[]{:S(2)}) collective-permute-start(bf16[72,2048]{1,0:T(8,128)(2,1)} %get-tuple-element.37.refs_0_), channel_id=1, source_target_pairs={{0,32},{32,64},{64,96},{96,0},{1,33},{33,65},{65,97},{97,1},{2,34}... | collective-permute-start | bytes 884744 | tf_op jit(solution)/shard_map/ppermute | solution.py:371
  18.7 3.7 %copy-start.4 = (bf16[72,2048]{1,0:T(8,128)(2,1)}, bf16[72,2048]{1,0:T(8,128)(2,1)S(1)}, u32[]{:S(2)}) copy-start(bf16[72,2048]{1,0:T(8,128)(2,1)S(1)} %collective-permute-done.15.refs_3_) | copy-start | bytes 884740
  28.6 95.8 %all-to-all-start = ((bf16[32,24,2048]{2,1,0:T(8,128)(2,1)}), bf16[32,24,2048]{2,1,0:T(8,128)(2,1)}, u32[]{:S(2)}, u32[]{:S(2)}) async-start(bf16[32,24,2048]{2,1,0:T(8,128)(2,1)} %bitcast.43), calls=%async_computation | async-start | bytes 6291456 | tf_op jit(solution)/shard_map/all_to_all | solution.py:367
  39.2 40.3 %collective-permute-start.2 = (bf16[72,2048]{1,0:T(8,128)(2,1)}, bf16[72,2048]{1,0:T(8,128)(2,1)S(1)}, u32[]{:S(2)}, u32[]{:S(2)}) collective-permute-start(bf16[72,2048]{1,0:T(8,128)(2,1)} %get-tuple-element.27), channel_id=1, source_target_pairs={{0,6},{2,0},{4,2},{6,4},{1,7},{3,1},{5,3},{7,5},{8,14},{10,8},{12,... | collective-permute-start | bytes 884744 | tf_op jit(solution)/shard_map/ppermute | solution.py:371
  40.1 46.2 %collective-permute-start.1 = (bf16[72,2048]{1,0:T(8,128)(2,1)}, bf16[72,2048]{1,0:T(8,128)(2,1)S(1)}, u32[]{:S(2)}, u32[]{:S(2)}) collective-permute-start(bf16[72,2048]{1,0:T(8,128)(2,1)} %get-tuple-element.27), channel_id=1, source_target_pairs={{0,4},{2,6},{4,0},{6,2},{1,5},{3,7},{5,1},{7,3},{8,12},{10,14},{12... | collective-permute-start | bytes 884744 | tf_op jit(solution)/shard_map/ppermute | solution.py:371
  41.0 46.4 %collective-permute-start = (bf16[72,2048]{1,0:T(8,128)(2,1)}, bf16[72,2048]{1,0:T(8,128)(2,1)S(1)}, u32[]{:S(2)}, u32[]{:S(2)}) collective-permute-start(bf16[72,2048]{1,0:T(8,128)(2,1)} %get-tuple-element.27), channel_id=1, source_target_pairs={{0,2},{2,4},{4,6},{6,0},{1,3},{3,5},{5,7},{7,1},{8,10},{10,12},{12... | collective-permute-start | bytes 884744 | tf_op jit(solution)/shard_map/ppermute | solution.py:371
  88.5 1.0 copy-start.2
  89.5 3.0 collective-permute-start.3
  89.5 12.3 %copy-start.3 = (bf16[72,2048]{1,0:T(8,128)(2,1)S(1)}, bf16[72,2048]{1,0:T(8,128)(2,1)}, u32[]{:S(2)}) copy-start(bf16[72,2048]{1,0:T(8,128)(2,1)} %get-tuple-element.36.refs_0_) | copy-start | bytes 884740
  89.5 15.0 %collective-permute-start.12 = (bf16[72,2048]{1,0:T(8,128)(2,1)}, bf16[72,2048]{1,0:T(8,128)(2,1)}, u32[]{:S(2)}, u32[]{:S(2)}) collective-permute-start(bf16[72,2048]{1,0:T(8,128)(2,1)} %get-tuple-element.36.refs_0_), channel_id=1, source_target_pairs={{0,24},{8,0},{16,8},{24,16},{1,25},{9,1},{17,9},{25,17},{2,26},{10... | collective-permute-start | bytes 884744 | tf_op jit(solution)/shard_map/ppermute | solution.py:371
  98.5 39.0 %collective-permute-start.4 = (bf16[4,8,24,512]{3,2,1,0:T(8,128)(2,1)}, bf16[4,8,24,512]{3,2,1,0:T(8,128)(2,1)}, u32[]{:S(2)}, u32[]{:S(2)}) collective-permute-start(bf16[4,8,24,512]{3,2,1,0:T(8,128)(2,1)} %get-tuple-element.29), channel_id=1, source_target_pairs={{0,32},{32,64},{64,96},{96,0},{1,33},{33,65},{65,97},{97,1},{2,34}... | collective-permute-start | bytes 2359304 | tf_op jit(solution)/shard_map/ppermute | solution.py:371
  98.5 39.0 %collective-permute-start.5 = (bf16[4,8,24,512]{3,2,1,0:T(8,128)(2,1)}, bf16[4,8,24,512]{3,2,1,0:T(8,128)(2,1)}, u32[]{:S(2)}, u32[]{:S(2)}) collective-permute-start(bf16[4,8,24,512]{3,2,1,0:T(8,128)(2,1)} %get-tuple-element.30), channel_id=1, source_target_pairs={{0,64},{32,96},{64,0},{96,32},{1,65},{33,97},{65,1},{97,33},{2,66}... | collective-permute-start | bytes 2359304 | tf_op jit(solution)/shard_map/ppermute | solution.py:371
  100.6 49.2 %collective-permute-start.6 = (bf16[4,8,24,512]{3,2,1,0:T(8,128)(2,1)}, bf16[4,8,24,512]{3,2,1,0:T(8,128)(2,1)}, u32[]{:S(2)}, u32[]{:S(2)}) collective-permute-start(bf16[4,8,24,512]{3,2,1,0:T(8,128)(2,1)} %get-tuple-element.31), channel_id=1, source_target_pairs={{0,96},{32,0},{64,32},{96,64},{1,97},{33,1},{65,33},{97,65},{2,98}... | collective-permute-start | bytes 2359304 | tf_op jit(solution)/shard_map/ppermute | solution.py:371
  101.8 11.4 %collective-permute-start.11 = (bf16[72,2048]{1,0:T(8,128)(2,1)S(1)}, bf16[72,2048]{1,0:T(8,128)(2,1)S(1)}, u32[]{:S(2)}, u32[]{:S(2)}) collective-permute-start(bf16[72,2048]{1,0:T(8,128)(2,1)S(1)} %copy-done.3), channel_id=1, source_target_pairs={{0,16},{8,24},{16,0},{24,8},{1,17},{9,25},{17,1},{25,9},{2,18},{10... | collective-permute-start | bytes 884744 | tf_op jit(solution)/shard_map/ppermute | solution.py:371
  104.5 13.6 %collective-permute-start.10 = (bf16[72,2048]{1,0:T(8,128)(2,1)S(1)}, bf16[72,2048]{1,0:T(8,128)(2,1)}, u32[]{:S(2)}, u32[]{:S(2)}) collective-permute-start(bf16[72,2048]{1,0:T(8,128)(2,1)S(1)} %copy-done.3), channel_id=1, source_target_pairs={{0,8},{8,16},{16,24},{24,0},{1,9},{9,17},{17,25},{25,1},{2,10},{10... | collective-permute-start | bytes 884744 | tf_op jit(solution)/shard_map/ppermute | solution.py:371
  113.2 0.7 copy-start.5
  124.5 88.3 %all-to-all-start.1 = ((bf16[32,24,2048]{2,1,0:T(8,128)(2,1)}), bf16[32,24,2048]{2,1,0:T(8,128)(2,1)}, u32[]{:S(2)}, u32[]{:S(2)}) async-start(bf16[32,24,2048]{2,1,0:T(8,128)(2,1)} %bitcast.44), calls=%async_computation.1 | async-start | bytes 6291456 | tf_op jit(solution)/shard_map/all_to_all | solution.py:367
  153.3 21.7 %collective-permute-start.7 = (bf16[4,8,24,512]{3,2,1,0:T(8,128)(2,1)}, bf16[4,8,24,512]{3,2,1,0:T(8,128)(2,1)}, u32[]{:S(2)}, u32[]{:S(2)}) collective-permute-start(bf16[4,8,24,512]{3,2,1,0:T(8,128)(2,1)} %get-tuple-element.33), channel_id=1, source_target_pairs={{0,8},{8,16},{16,24},{24,0},{1,9},{9,17},{17,25},{25,1},{2,10},{10... | collective-permute-start | bytes 2359304 | tf_op jit(solution)/shard_map/ppermute | solution.py:371
  155.1 35.1 %collective-permute-start.8 = (bf16[4,8,24,512]{3,2,1,0:T(8,128)(2,1)}, bf16[4,8,24,512]{3,2,1,0:T(8,128)(2,1)}, u32[]{:S(2)}, u32[]{:S(2)}) collective-permute-start(bf16[4,8,24,512]{3,2,1,0:T(8,128)(2,1)} %get-tuple-element.34), channel_id=1, source_target_pairs={{0,16},{8,24},{16,0},{24,8},{1,17},{9,25},{17,1},{25,9},{2,18},{10... | collective-permute-start | bytes 2359304 | tf_op jit(solution)/shard_map/ppermute | solution.py:371
  158.7 31.5 %collective-permute-start.9 = (bf16[4,8,24,512]{3,2,1,0:T(8,128)(2,1)}, bf16[4,8,24,512]{3,2,1,0:T(8,128)(2,1)}, u32[]{:S(2)}, u32[]{:S(2)}) collective-permute-start(bf16[4,8,24,512]{3,2,1,0:T(8,128)(2,1)} %get-tuple-element.35), channel_id=1, source_target_pairs={{0,24},{8,0},{16,8},{24,16},{1,25},{9,1},{17,9},{25,17},{2,26},{10... | collective-permute-start | bytes 2359304 | tf_op jit(solution)/shard_map/ppermute | solution.py:371
  212.8 47.7 %all-to-all-start.2 = ((bf16[128,24,512]{2,1,0:T(8,128)(2,1)}), bf16[128,24,512]{2,1,0:T(8,128)(2,1)}, u32[]{:S(2)}, u32[]{:S(2)}) async-start(bf16[128,24,512]{2,1,0:T(8,128)(2,1)} %shard_map.127), calls=%async_computation.2 | async-start | bytes 6291456 | tf_op jit(solution)/shard_map/all_to_all | solution.py:367
  220.7 8.6 %copy-start.1 = (bf16[768,2048]{1,0:T(8,128)(2,1)S(1)}, bf16[768,2048]{1,0:T(8,128)(2,1)}, u32[]{:S(2)}) copy-start(bf16[768,2048]{1,0:T(8,128)(2,1)} %shard_map.124) | copy-start | bytes 9437188
  229.3 3.3 %copy-start.6 = (f32[768,1536]{0,1:T(8,128)}, f32[768,1536]{0,1:T(8,128)S(1)}, u32[]{:S(2)}) copy-start(f32[768,1536]{0,1:T(8,128)S(1)} %fusion.3) | copy-start | bytes 14155780
  232.6 1.0 copy-start.7
  232.6 1.4 copy-start.9
  260.5 47.0 %all-to-all-start.3 = ((bf16[128,24,512]{2,1,0:T(8,128)(2,1)}), bf16[128,24,512]{2,1,0:T(8,128)(2,1)}, u32[]{:S(2)}, u32[]{:S(2)}) async-start(bf16[128,24,512]{2,1,0:T(8,128)(2,1)} %shard_map.128), calls=%async_computation.3 | async-start | bytes 6291456 | tf_op jit(solution)/shard_map/all_to_all | solution.py:367
  267.5 7.8 %copy-start.8 = (bf16[768,768]{0,1:T(8,128)(2,1)S(1)}, bf16[768,768]{0,1:T(8,128)(2,1)}, u32[]{:S(2)}) copy-start(bf16[768,768]{0,1:T(8,128)(2,1)} %copy-done.7) | copy-start | bytes 3538948
  267.5 7.8 %copy-start.10 = (bf16[768,768]{0,1:T(8,128)(2,1)S(1)}, bf16[768,768]{0,1:T(8,128)(2,1)}, u32[]{:S(2)}) copy-start(bf16[768,768]{0,1:T(8,128)(2,1)} %copy-done.9) | copy-start | bytes 3538948

commit v6 on v5

--- a/solution.py
+++ b/solution.py
@@ -127,30 +127,30 @@
 
 
 def plane_body(along, capacity, *refs):
-    *pays, out = refs
-    rows, width = out.shape
+    *pays, out, want, table = refs
+    rows, _ = out.shape
     tok = pays[0].shape[0] - TOP
     here = lax.axis_index(along)
-    mine = pl.program_id(0) * rows + lax.broadcasted_iota(jnp.int32, (rows, tok), 0)
-    picks = []
-    for s, pay in enumerate(pays):
-        ids = fact(pay, tok, 0).astype(jnp.int32)
-        slot = fact(pay, tok, 1).astype(jnp.int32)
-        y, z, x, c = coordinates(ids)
-        near, far = (y, z) if along == "y" else (z, y)
-        place_of = ((far * 4 + x) * 2 + c) * len(pays) + s
-        want = jnp.where(near == here, place_of * capacity + slot, -1)
-        pick = jnp.zeros((rows, tok), F32)
-        for j in range(TOP):
-            pick = jnp.where(mine == want[j : j + 1, :], 1.0, pick)
-        picks.append(pick.astype(BF16))
-    piece = width // PARTS
-    for q in range(PARTS):
-        lanes = slice(q * piece, (q + 1) * piece)
-        got = jnp.zeros((rows, piece), F32)
-        for pick, pay in zip(picks, pays):
-            got = got + jnp.dot(pick, pay[:tok, lanes], preferred_element_type=F32)
-        out[:, lanes] = got.astype(BF16)
+
+    @pl.when(pl.program_id(0) == 0)
+    def _():
+        for s, pay in enumerate(pays):
+            ids = fact(pay, tok, 0).astype(jnp.int32)
+            slot = fact(pay, tok, 1).astype(jnp.int32)
+            y, z, x, c = coordinates(ids)
+            near, far = (y, z) if along == "y" else (z, y)
+            place_of = ((far * 4 + x) * 2 + c) * len(pays) + s
+            want[:, s * tok : (s + 1) * tok] = jnp.where(
+                near == here, place_of * capacity + slot, -1
+            )
+            table[s * tok : (s + 1) * tok, :] = pay[:tok, :]
+
+    wide = want.shape[1]
+    mine = pl.program_id(0) * rows + lax.broadcasted_iota(jnp.int32, (rows, wide), 0)
+    pick = jnp.zeros((rows, wide), F32)
+    for j in range(TOP):
+        pick = jnp.where(mine == want[j : j + 1, :], 1.0, pick)
+    out[...] = jnp.dot(pick.astype(BF16), table[...], preferred_element_type=F32).astype(BF16)
 
 
 def plane(along, capacity, pays):
@@ -164,6 +164,10 @@
         pl.BlockSpec((rows // steps, width), lambda i: (i, 0)),
         jax.ShapeDtypeStruct((rows, width), BF16),
         (2_000_000_000, 8_000_000),
+        [
+            pltpu.VMEM((TOP, len(pays) * (tall - TOP)), jnp.int32),
+            pltpu.VMEM((len(pays) * (tall - TOP), width), BF16),
+        ],
     )(*pays)
 
 

time: 315 us -> 315 us (level)
  starting transfers between devices: 54.2 us -> 62.5 us
  Pallas kernels: 50 us -> 45.2 us
    ppermute x15, starting transfers between devices: 23.9 us -> 30.4 us  [turned(): return lax.ppermute(x, axis, [(i, (i + turn) % 4) for i in range(4)])]
    pallas_call x2, Pallas kernels: 12.6 us -> 7.8 us  [plane(): call(functools.partial(plane_body, along, capacity), (steps,), [whole((ta...]
  transfers between devices with their start and end apart: 20 -> 20, of which waited for: 14 -> 14; matrix products, arithmetic and copies ran while one was open for 17% -> 17% of each run, Pallas kernels for 12% -> 11%
where the time goes in v6:
time: 315 us; the launch traced here: 312 us
  waiting for transfers between devices  148 us (47%)
  starting transfers between devices  62.5 us (20%)
  matrix products  51.3 us (16%)
  Pallas kernels  45.2 us (14%)
    ppermute x15, waiting for transfers between devices, turned(): return lax.ppermute(x, axis, [(i, (i + turn) % 4) for i in range(4)])  118 us
    all_to_all x4, starting transfers between devices, exchange(): return lax.all_to_all(x, axes, split_axis=0, concat_axis=0, tiled=True)  32.1 us
    ppermute x15, starting transfers between devices, turned(): return lax.ppermute(x, axis, [(i, (i + turn) % 4) for i in range(4)])  30.4 us
    all_to_all x4, waiting for transfers between devices, exchange(): return lax.all_to_all(x, axes, split_axis=0, concat_axis=0, tiled=True)  29.9 us
    pallas_call x2, Pallas kernels, pack(): call(functools.partial(pack_body, along), (1,), [whole((total, width))],...  10.3 us
    dot_general x1, matrix products, layer(): lax.dot_general(rows_b, d_proj, ROWS_BY_ROWS, preferred_element_type=F32)  9.6 us
    dot_general x1, matrix products, expert_backward(): lax.dot_general(d_proj, w_in, COLS_BY_COLS, preferred_element_type=F32)  9.38 us
    dot_general x1, matrix products, layer(): projected = jnp.dot(rows_b, w_in, preferred_element_type=F32)  8.6 us
  transfers between devices with their start and end apart: 20, of which 14 were waited for; matrix products, arithmetic and copies ran while one was open for 17% of the time, Pallas kernels for 11%

profile of v6, /device:TPU:6, one launch (start us, length us, event | category | flops | bytes accessed | tf_op | source)
XLA Modules:
  0.0 311.8 jit_solution(11568940038513732149)
XLA Ops:
  7.3 11.3 %collective-permute-done.15.refs_3_ = bf16[72,2048]{1,0:T(8,128)(2,1)S(1)} collective-permute-done((bf16[72,2048]{1,0:T(8,128)(2,1)}, bf16[72,2048]{1,0:T(8,128)(2,1)S(1)}, u32[]{:S(2)}, u32[]{:S(2)}) %collective-permute-start.15) | collective-permute-done | bytes 294944 | tf_op jit(solution)/shard_map/ppermute | solution.py:375
  18.7 3.7 %collective-permute-done.13.refs_1_ = bf16[72,2048]{1,0:T(8,128)(2,1)} collective-permute-done((bf16[72,2048]{1,0:T(8,128)(2,1)}, bf16[72,2048]{1,0:T(8,128)(2,1)}, u32[]{:S(2)}, u32[]{:S(2)}) %collective-permute-start.13) | collective-permute-done | bytes 294944 | tf_op jit(solution)/shard_map/ppermute | solution.py:375
  22.4 3.9 %shard_map.126 = bf16[768,2048]{1,0:T(8,128)(2,1)} custom-call(bf16[72,2048]{1,0:T(8,128)(2,1)} %get-tuple-element.37.refs_0_, bf16[72,2048]{1,0:T(8,128)(2,1)} %collective-permute-done.13.refs_1_, bf16[72,2048]{1,0:T(8,128)(2,1)} %collective-permute-done.14.refs_2_, bf16[72,2048]{1,0:T(8,128)(2,1)} %copy-done.4), custom_call_target="tpu_custom_call" | custom-call | flops 2000000000 | bytes 8000000 | tf_op jit(solution)/shard_map/pallas_call | solution.py:160
  26.3 8.5 %all-to-all-start = ((bf16[32,24,2048]{2,1,0:T(8,128)(2,1)}), bf16[32,24,2048]{2,1,0:T(8,128)(2,1)}, u32[]{:S(2)}, u32[]{:S(2)}) async-start(bf16[32,24,2048]{2,1,0:T(8,128)(2,1)} %bitcast.43), calls=%async_computation | async-start | bytes 6291456 | tf_op jit(solution)/shard_map/all_to_all | solution.py:371
  41.0 36.2 %collective-permute-done.2 = bf16[72,2048]{1,0:T(8,128)(2,1)S(1)} collective-permute-done((bf16[72,2048]{1,0:T(8,128)(2,1)}, bf16[72,2048]{1,0:T(8,128)(2,1)S(1)}, u32[]{:S(2)}, u32[]{:S(2)}) %collective-permute-start.2) | collective-permute-done | bytes 294944 | tf_op jit(solution)/shard_map/ppermute | solution.py:375
  77.2 6.8 %collective-permute-done.1 = bf16[72,2048]{1,0:T(8,128)(2,1)S(1)} collective-permute-done((bf16[72,2048]{1,0:T(8,128)(2,1)}, bf16[72,2048]{1,0:T(8,128)(2,1)S(1)}, u32[]{:S(2)}, u32[]{:S(2)}) %collective-permute-start.1) | collective-permute-done | bytes 294944 | tf_op jit(solution)/shard_map/ppermute | solution.py:375
  90.1 6.1 %shard_map.122 = (bf16[4,8,24,512]{3,2,1,0:T(8,128)(2,1)}, bf16[4,8,24,512]{3,2,1,0:T(8,128)(2,1)}, bf16[4,8,24,512]{3,2,1,0:T(8,128)(2,1)}, bf16[4,8,24,512]{3,2,1,0:T(8,128)(2,1)}) custom-call(bf16[4,72,2048]{2,1,0:T(8,128)(2,1)} %copy-done.2, bf16[4,72,2048]{2,1,0:T(8,128)(2,1)} %collective-permute-done.3.other), custom_call_target="tpu_custom_call" | custom-call | flops 2000000000 | bytes 8000000 | tf_op jit(solution)/shard_map/pallas_call | solution.py:215
  103.1 7.7 %collective-permute-done.11.refs_2_ = bf16[72,2048]{1,0:T(8,128)(2,1)S(1)} collective-permute-done((bf16[72,2048]{1,0:T(8,128)(2,1)S(1)}, bf16[72,2048]{1,0:T(8,128)(2,1)S(1)}, u32[]{:S(2)}, u32[]{:S(2)}) %collective-permute-start.11) | collective-permute-done | bytes 294944 | tf_op jit(solution)/shard_map/ppermute | solution.py:375
  111.5 4.3 %collective-permute-done.10.refs_1_ = bf16[72,2048]{1,0:T(8,128)(2,1)} collective-permute-done((bf16[72,2048]{1,0:T(8,128)(2,1)S(1)}, bf16[72,2048]{1,0:T(8,128)(2,1)}, u32[]{:S(2)}, u32[]{:S(2)}) %collective-permute-start.10) | collective-permute-done | bytes 294944 | tf_op jit(solution)/shard_map/ppermute | solution.py:375
  115.8 3.9 %shard_map.125 = bf16[768,2048]{1,0:T(8,128)(2,1)} custom-call(bf16[72,2048]{1,0:T(8,128)(2,1)} %get-tuple-element.36.refs_0_, bf16[72,2048]{1,0:T(8,128)(2,1)} %collective-permute-done.10.refs_1_, bf16[72,2048]{1,0:T(8,128)(2,1)} %copy-done.5, bf16[72,2048]{1,0:T(8,128)(2,1)} %collective-permute-done.12.refs_3_), custom_call_target="tpu_custom_call" | custom-call | flops 2000000000 | bytes 8000000 | tf_op jit(solution)/shard_map/pallas_call | solution.py:160
  119.7 7.0 %all-to-all-start.1 = ((bf16[32,24,2048]{2,1,0:T(8,128)(2,1)}), bf16[32,24,2048]{2,1,0:T(8,128)(2,1)}, u32[]{:S(2)}, u32[]{:S(2)}) async-start(bf16[32,24,2048]{2,1,0:T(8,128)(2,1)} %bitcast.44), calls=%async_computation.1 | async-start | bytes 6291456 | tf_op jit(solution)/shard_map/all_to_all | solution.py:371
  126.7 19.8 %collective-permute-done.4.refs_1_ = bf16[4,8,24,512]{3,2,1,0:T(8,128)(2,1)} collective-permute-done((bf16[4,8,24,512]{3,2,1,0:T(8,128)(2,1)}, bf16[4,8,24,512]{3,2,1,0:T(8,128)(2,1)}, u32[]{:S(2)}, u32[]{:S(2)}) %collective-permute-start.4) | collective-permute-done | bytes 786464 | tf_op jit(solution)/shard_map/ppermute | solution.py:375
  148.4 3.5 %shard_map.123 = (bf16[4,8,24,512]{3,2,1,0:T(8,128)(2,1)}, bf16[4,8,24,512]{3,2,1,0:T(8,128)(2,1)}, bf16[4,8,24,512]{3,2,1,0:T(8,128)(2,1)}, bf16[4,8,24,512]{3,2,1,0:T(8,128)(2,1)}) custom-call(bf16[4,8,24,512]{3,2,1,0:T(8,128)(2,1)} %get-tuple-element.28.refs_0_, bf16[4,8,24,512]{3,2,1,0:T(8,128)(2,1)} %collective-permute-done.4.refs_1_, ...), custom_call_target="tpu_custom_call" | custom-call | flops 1000000000 | bytes 8000000 | tf_op jit(solution)/shard_map/pallas_call | solution.py:235
  154.0 9.9 %collective-permute-start.8 = (bf16[4,8,24,512]{3,2,1,0:T(8,128)(2,1)}, bf16[4,8,24,512]{3,2,1,0:T(8,128)(2,1)}, u32[]{:S(2)}, u32[]{:S(2)}) collective-permute-start(bf16[4,8,24,512]{3,2,1,0:T(8,128)(2,1)} %get-tuple-element.34), channel_id=1, source_target_pairs={{0,16},{8,24},{16,0},{24,8},{1,17},{9,25},{17,1},{25,9},{2,18},{10... | collective-permute-start | bytes 2359304 | tf_op jit(solution)/shard_map/ppermute | solution.py:375
  163.9 16.5 %collective-permute-done.7.t1 = bf16[4,8,24,512]{3,2,1,0:T(8,128)(2,1)} collective-permute-done((bf16[4,8,24,512]{3,2,1,0:T(8,128)(2,1)}, bf16[4,8,24,512]{3,2,1,0:T(8,128)(2,1)}, u32[]{:S(2)}, u32[]{:S(2)}) %collective-permute-start.7) | collective-permute-done | bytes 786464 | tf_op jit(solution)/shard_map/ppermute | solution.py:375
  180.4 8.4 %collective-permute-done.8.t2 = bf16[4,8,24,512]{3,2,1,0:T(8,128)(2,1)} collective-permute-done((bf16[4,8,24,512]{3,2,1,0:T(8,128)(2,1)}, bf16[4,8,24,512]{3,2,1,0:T(8,128)(2,1)}, u32[]{:S(2)}, u32[]{:S(2)}) %collective-permute-start.8) | collective-permute-done | bytes 786464 | tf_op jit(solution)/shard_map/ppermute | solution.py:375
  188.8 4.8 %shard_map.124 = bf16[768,2048]{1,0:T(8,128)(2,1)} custom-call(bf16[4,8,24,512]{3,2,1,0:T(8,128)(2,1)} %get-tuple-element.32.t0, bf16[4,8,24,512]{3,2,1,0:T(8,128)(2,1)} %collective-permute-done.7.t1, bf16[4,8,24,512]{3,2,1,0:T(8,128)(2,1)} %collective-permute-done.8.t2, bf16[4,8,24,512]{3,2,1,0:T(8,128)(2,1)} %collective-permute-done.9.t3), custom_call_target="tpu_custom_call" | custom-call | flops 629145600 | bytes 6291456 | tf_op jit(solution)/shard_map/pallas_call | solution.py:276
  193.6 8.5 %fusion.5 = f32[768,1536]{0,1:T(8,128)S(1)} fusion(bf16[768,2048]{1,0:T(8,128)(2,1)} %bitcast.10, bf16[1,2048,1536]{2,1,0:T(8,128)(2,1)} %param.16), kind=kOutput, calls=%fused_computation.6 | convolution fusion | flops 4831838208 | bytes 14155776 | tf_op jit(solution)/shard_map/dot_general | solution.py:388
  202.1 4.2 %convolution_convert_fusion.2.rows = bf16[768,2048]{1,0:T(8,128)(2,1)} fusion(bf16[1,768,2048]{2,1,0:T(8,128)(2,1)S(1)} %copy-done, f32[768,1536]{0,1:T(8,128)S(1)} %fusion.5), kind=kOutput, calls=%fused_computation.9 | convolution fusion | flops 2421030912 | bytes 11010048 | tf_op jit(solution)/shard_map/dot_general | solution.py:391
  206.3 5.2 %shard_map.127 = bf16[128,24,512]{2,1,0:T(8,128)(2,1)} custom-call(bf16[768,2048]{1,0:T(8,128)(2,1)} %convolution_convert_fusion.2.rows), custom_call_target="tpu_custom_call" | custom-call | flops 629145600 | bytes 6291456 | tf_op jit(solution)/shard_map/pallas_call | solution.py:313
  211.4 9.6 %all-to-all-start.2 = ((bf16[128,24,512]{2,1,0:T(8,128)(2,1)}), bf16[128,24,512]{2,1,0:T(8,128)(2,1)}, u32[]{:S(2)}, u32[]{:S(2)}) async-start(bf16[128,24,512]{2,1,0:T(8,128)(2,1)} %shard_map.127), calls=%async_computation.2 | async-start | bytes 6291456 | tf_op jit(solution)/shard_map/all_to_all | solution.py:371
  221.0 8.6 %fusion.3 = f32[768,1536]{0,1:T(8,128)S(1)} fusion(bf16[768,2048]{1,0:T(8,128)(2,1)} %bitcast.14, bf16[1,2048,1536]{2,1,0:T(8,128)(2,1)} %param.16), kind=kOutput, calls=%fused_computation.4 | convolution fusion | flops 4831838208 | bytes 14155776 | tf_op jit(solution)/shard_map/dot_general | solution.py:446
  229.7 3.3 %multiply_convert_fusion.2 = (bf16[768,768]{0,1:T(8,128)(2,1)S(1)}, bf16[768,768]{0,1:T(8,128)(2,1)S(1)}) fusion(f32[768,1536]{0,1:T(8,128)S(1)} %fusion.3, bf16[768,2048]{1,0:T(8,128)(2,1)S(1)} %copy-done.1, bf16[1,768,2048]{2,1,0:T(8,128)(2,1)S(1)} %copy-done), kind=kOutput, calls=%fused_computation.20 | convolution fusion | flops 2423586816 | bytes 13369344 | tf_op jit(solution)/shard_map/dot_general | solution.py:399
  234.4 9.4 %fusion.7.rows = bf16[768,2048]{1,0:T(8,128)(2,1)} fusion(bf16[1,2048,1536]{2,1,0:T(8,128)(2,1)} %param.16, bf16[768,768]{0,1:T(8,128)(2,1)S(1)} %get-tuple-element.47, bf16[768,768]{0,1:T(8,128)(2,1)S(1)} %get-tuple-element.46), kind=kOutput, calls=%fused_computation.10 | convolution fusion | flops 4838129664 | bytes 11796480 | tf_op jit(solution)/shard_map/dot_general | solution.py:403
  243.8 5.2 %shard_map.128 = bf16[128,24,512]{2,1,0:T(8,128)(2,1)} custom-call(bf16[768,2048]{1,0:T(8,128)(2,1)} %fusion.7.rows), custom_call_target="tpu_custom_call" | custom-call | flops 629145600 | bytes 6291456 | tf_op jit(solution)/shard_map/pallas_call | solution.py:313
  248.9 11.9 %all-to-all-done.2 = bf16[128,24,512]{2,1,0:T(8,128)(2,1)} async-done(((bf16[128,24,512]{2,1,0:T(8,128)(2,1)}), bf16[128,24,512]{2,1,0:T(8,128)(2,1)}, u32[]{:S(2)}, u32[]{:S(2)}) %all-to-all-start.2) | async-done | bytes 3145760 | tf_op jit(solution)/shard_map/all_to_all | solution.py:371
  260.8 7.1 %all-to-all-start.3 = ((bf16[128,24,512]{2,1,0:T(8,128)(2,1)}), bf16[128,24,512]{2,1,0:T(8,128)(2,1)}, u32[]{:S(2)}, u32[]{:S(2)}) async-start(bf16[128,24,512]{2,1,0:T(8,128)(2,1)} %shard_map.128), calls=%async_computation.3 | async-start | bytes 6291456 | tf_op jit(solution)/shard_map/all_to_all | solution.py:371
  267.9 7.8 %fusion.13 = bf16[1,768,2048]{2,1,0:T(8,128)(2,1)} fusion(bf16[768,2048]{1,0:T(8,128)(2,1)} %shard_map.124, f32[768,1536]{0,1:T(8,128)} %copy-done.6), kind=kOutput, calls=%fused_computation.14 | convolution fusion | flops 2421030912 | bytes 11010048 | tf_op jit(solution)/shard_map/dot_general | solution.py:454
  275.7 9.6 %fusion = bf16[1,2048,1536]{2,1,0:T(8,128)(2,1)} fusion(bf16[768,2048]{1,0:T(8,128)(2,1)} %bitcast.14, bf16[768,768]{0,1:T(8,128)(2,1)S(1)} %copy-done.10, bf16[768,768]{0,1:T(8,128)(2,1)S(1)} %copy-done.8), kind=kOutput, calls=%fused_computation.1 | convolution fusion | flops 4839702528 | bytes 11796480 | tf_op jit(solution)/shard_map/dot_general | solution.py:457
  285.3 4.5 %shard_map.129 = bf16[64,2048]{1,0:T(8,128)(2,1)} custom-call(s32[8,64]{1,0:T(8,128)} %get-tuple-element.25.key, f32[8,64]{1,0:T(8,128)} %get-tuple-element.26.wgt, bf16[3072,512]{1,0:T(8,128)(2,1)} %bitcast.17.got), custom_call_target="tpu_custom_call" | custom-call | flops 402653184 | bytes 3145728 | tf_op jit(solution)/shard_map/pallas_call | solution.py:359
  289.8 18.0 %all-to-all-done.3 = bf16[128,24,512]{2,1,0:T(8,128)(2,1)} async-done(((bf16[128,24,512]{2,1,0:T(8,128)(2,1)}), bf16[128,24,512]{2,1,0:T(8,128)(2,1)}, u32[]{:S(2)}, u32[]{:S(2)}) %all-to-all-start.3) | async-done | bytes 3145760 | tf_op jit(solution)/shard_map/all_to_all | solution.py:371
  307.8 4.0 %shard_map.130 = bf16[64,2048]{1,0:T(8,128)(2,1)} custom-call(s32[8,64]{1,0:T(8,128)} %get-tuple-element.43.key, f32[8,64]{1,0:T(8,128)} %get-tuple-element.44.wgt, bf16[3072,512]{1,0:T(8,128)(2,1)} %bitcast.19.got), custom_call_target="tpu_custom_call" | custom-call | flops 402653184 | bytes 3145728 | tf_op jit(solution)/shard_map/pallas_call | solution.py:359
  (49 shorter events, 32.0 us)
Async XLA Ops:
  0.6 201.4 %copy-start = (bf16[1,768,2048]{2,1,0:T(8,128)(2,1)S(1)}, bf16[1,768,2048]{2,1,0:T(8,128)(2,1)}, u32[]{:S(2)}) copy-start(bf16[1,768,2048]{2,1,0:T(8,128)(2,1)} %param.17) | copy-start | bytes 9437188
  2.7 15.9 %collective-permute-start.15 = (bf16[72,2048]{1,0:T(8,128)(2,1)}, bf16[72,2048]{1,0:T(8,128)(2,1)S(1)}, u32[]{:S(2)}, u32[]{:S(2)}) collective-permute-start(bf16[72,2048]{1,0:T(8,128)(2,1)} %get-tuple-element.37.refs_0_), channel_id=1, source_target_pairs={{0,96},{32,0},{64,32},{96,64},{1,97},{33,1},{65,33},{97,65},{2,98}... | collective-permute-start | bytes 884744 | tf_op jit(solution)/shard_map/ppermute | solution.py:375
  5.7 12.9 %collective-permute-start.14 = (bf16[72,2048]{1,0:T(8,128)(2,1)}, bf16[72,2048]{1,0:T(8,128)(2,1)}, u32[]{:S(2)}, u32[]{:S(2)}) collective-permute-start(bf16[72,2048]{1,0:T(8,128)(2,1)} %get-tuple-element.37.refs_0_), channel_id=1, source_target_pairs={{0,64},{32,96},{64,0},{96,32},{1,65},{33,97},{65,1},{97,33},{2,66}... | collective-permute-start | bytes 884744 | tf_op jit(solution)/shard_map/ppermute | solution.py:375
  6.4 16.0 %collective-permute-start.13 = (bf16[72,2048]{1,0:T(8,128)(2,1)}, bf16[72,2048]{1,0:T(8,128)(2,1)}, u32[]{:S(2)}, u32[]{:S(2)}) collective-permute-start(bf16[72,2048]{1,0:T(8,128)(2,1)} %get-tuple-element.37.refs_0_), channel_id=1, source_target_pairs={{0,32},{32,64},{64,96},{96,0},{1,33},{33,65},{65,97},{97,1},{2,34}... | collective-permute-start | bytes 884744 | tf_op jit(solution)/shard_map/ppermute | solution.py:375
  18.7 3.7 %copy-start.4 = (bf16[72,2048]{1,0:T(8,128)(2,1)}, bf16[72,2048]{1,0:T(8,128)(2,1)S(1)}, u32[]{:S(2)}) copy-start(bf16[72,2048]{1,0:T(8,128)(2,1)S(1)} %collective-permute-done.15.refs_3_) | copy-start | bytes 884740
  26.3 93.5 %all-to-all-start = ((bf16[32,24,2048]{2,1,0:T(8,128)(2,1)}), bf16[32,24,2048]{2,1,0:T(8,128)(2,1)}, u32[]{:S(2)}, u32[]{:S(2)}) async-start(bf16[32,24,2048]{2,1,0:T(8,128)(2,1)} %bitcast.43), calls=%async_computation | async-start | bytes 6291456 | tf_op jit(solution)/shard_map/all_to_all | solution.py:371
  36.9 40.3 %collective-permute-start.2 = (bf16[72,2048]{1,0:T(8,128)(2,1)}, bf16[72,2048]{1,0:T(8,128)(2,1)S(1)}, u32[]{:S(2)}, u32[]{:S(2)}) collective-permute-start(bf16[72,2048]{1,0:T(8,128)(2,1)} %get-tuple-element.27), channel_id=1, source_target_pairs={{0,6},{2,0},{4,2},{6,4},{1,7},{3,1},{5,3},{7,5},{8,14},{10,8},{12,... | collective-permute-start | bytes 884744 | tf_op jit(solution)/shard_map/ppermute | solution.py:375
  37.7 46.2 %collective-permute-start.1 = (bf16[72,2048]{1,0:T(8,128)(2,1)}, bf16[72,2048]{1,0:T(8,128)(2,1)S(1)}, u32[]{:S(2)}, u32[]{:S(2)}) collective-permute-start(bf16[72,2048]{1,0:T(8,128)(2,1)} %get-tuple-element.27), channel_id=1, source_target_pairs={{0,4},{2,6},{4,0},{6,2},{1,5},{3,7},{5,1},{7,3},{8,12},{10,14},{12... | collective-permute-start | bytes 884744 | tf_op jit(solution)/shard_map/ppermute | solution.py:375
  38.6 46.4 %collective-permute-start = (bf16[72,2048]{1,0:T(8,128)(2,1)}, bf16[72,2048]{1,0:T(8,128)(2,1)S(1)}, u32[]{:S(2)}, u32[]{:S(2)}) collective-permute-start(bf16[72,2048]{1,0:T(8,128)(2,1)} %get-tuple-element.27), channel_id=1, source_target_pairs={{0,2},{2,4},{4,6},{6,0},{1,3},{3,5},{5,7},{7,1},{8,10},{10,12},{12... | collective-permute-start | bytes 884744 | tf_op jit(solution)/shard_map/ppermute | solution.py:375
  86.1 1.0 copy-start.2
  87.1 3.0 collective-permute-start.3
  87.1 12.3 %copy-start.3 = (bf16[72,2048]{1,0:T(8,128)(2,1)S(1)}, bf16[72,2048]{1,0:T(8,128)(2,1)}, u32[]{:S(2)}) copy-start(bf16[72,2048]{1,0:T(8,128)(2,1)} %get-tuple-element.36.refs_0_) | copy-start | bytes 884740
  87.1 15.0 %collective-permute-start.12 = (bf16[72,2048]{1,0:T(8,128)(2,1)}, bf16[72,2048]{1,0:T(8,128)(2,1)}, u32[]{:S(2)}, u32[]{:S(2)}) collective-permute-start(bf16[72,2048]{1,0:T(8,128)(2,1)} %get-tuple-element.36.refs_0_), channel_id=1, source_target_pairs={{0,24},{8,0},{16,8},{24,16},{1,25},{9,1},{17,9},{25,17},{2,26},{10... | collective-permute-start | bytes 884744 | tf_op jit(solution)/shard_map/ppermute | solution.py:375
  96.1 50.4 %collective-permute-start.4 = (bf16[4,8,24,512]{3,2,1,0:T(8,128)(2,1)}, bf16[4,8,24,512]{3,2,1,0:T(8,128)(2,1)}, u32[]{:S(2)}, u32[]{:S(2)}) collective-permute-start(bf16[4,8,24,512]{3,2,1,0:T(8,128)(2,1)} %get-tuple-element.29), channel_id=1, source_target_pairs={{0,32},{32,64},{64,96},{96,0},{1,33},{33,65},{65,97},{97,1},{2,34}... | collective-permute-start | bytes 2359304 | tf_op jit(solution)/shard_map/ppermute | solution.py:375
  96.1 50.4 %collective-permute-start.5 = (bf16[4,8,24,512]{3,2,1,0:T(8,128)(2,1)}, bf16[4,8,24,512]{3,2,1,0:T(8,128)(2,1)}, u32[]{:S(2)}, u32[]{:S(2)}) collective-permute-start(bf16[4,8,24,512]{3,2,1,0:T(8,128)(2,1)} %get-tuple-element.30), channel_id=1, source_target_pairs={{0,64},{32,96},{64,0},{96,32},{1,65},{33,97},{65,1},{97,33},{2,66}... | collective-permute-start | bytes 2359304 | tf_op jit(solution)/shard_map/ppermute | solution.py:375
  98.2 50.2 %collective-permute-start.6 = (bf16[4,8,24,512]{3,2,1,0:T(8,128)(2,1)}, bf16[4,8,24,512]{3,2,1,0:T(8,128)(2,1)}, u32[]{:S(2)}, u32[]{:S(2)}) collective-permute-start(bf16[4,8,24,512]{3,2,1,0:T(8,128)(2,1)} %get-tuple-element.31), channel_id=1, source_target_pairs={{0,96},{32,0},{64,32},{96,64},{1,97},{33,1},{65,33},{97,65},{2,98}... | collective-permute-start | bytes 2359304 | tf_op jit(solution)/shard_map/ppermute | solution.py:375
  99.4 11.4 %collective-permute-start.11 = (bf16[72,2048]{1,0:T(8,128)(2,1)S(1)}, bf16[72,2048]{1,0:T(8,128)(2,1)S(1)}, u32[]{:S(2)}, u32[]{:S(2)}) collective-permute-start(bf16[72,2048]{1,0:T(8,128)(2,1)S(1)} %copy-done.3), channel_id=1, source_target_pairs={{0,16},{8,24},{16,0},{24,8},{1,17},{9,25},{17,1},{25,9},{2,18},{10... | collective-permute-start | bytes 884744 | tf_op jit(solution)/shard_map/ppermute | solution.py:375
  102.2 13.6 %collective-permute-start.10 = (bf16[72,2048]{1,0:T(8,128)(2,1)S(1)}, bf16[72,2048]{1,0:T(8,128)(2,1)}, u32[]{:S(2)}, u32[]{:S(2)}) collective-permute-start(bf16[72,2048]{1,0:T(8,128)(2,1)S(1)} %copy-done.3), channel_id=1, source_target_pairs={{0,8},{8,16},{16,24},{24,0},{1,9},{9,17},{17,25},{25,1},{2,10},{10... | collective-permute-start | bytes 884744 | tf_op jit(solution)/shard_map/ppermute | solution.py:375
  110.8 0.7 copy-start.5
  119.7 91.7 %all-to-all-start.1 = ((bf16[32,24,2048]{2,1,0:T(8,128)(2,1)}), bf16[32,24,2048]{2,1,0:T(8,128)(2,1)}, u32[]{:S(2)}, u32[]{:S(2)}) async-start(bf16[32,24,2048]{2,1,0:T(8,128)(2,1)} %bitcast.44), calls=%async_computation.1 | async-start | bytes 6291456 | tf_op jit(solution)/shard_map/all_to_all | solution.py:371
  152.0 28.4 %collective-permute-start.7 = (bf16[4,8,24,512]{3,2,1,0:T(8,128)(2,1)}, bf16[4,8,24,512]{3,2,1,0:T(8,128)(2,1)}, u32[]{:S(2)}, u32[]{:S(2)}) collective-permute-start(bf16[4,8,24,512]{3,2,1,0:T(8,128)(2,1)} %get-tuple-element.33), channel_id=1, source_target_pairs={{0,8},{8,16},{16,24},{24,0},{1,9},{9,17},{17,25},{25,1},{2,10},{10... | collective-permute-start | bytes 2359304 | tf_op jit(solution)/shard_map/ppermute | solution.py:375
  154.0 34.8 %collective-permute-start.8 = (bf16[4,8,24,512]{3,2,1,0:T(8,128)(2,1)}, bf16[4,8,24,512]{3,2,1,0:T(8,128)(2,1)}, u32[]{:S(2)}, u32[]{:S(2)}) collective-permute-start(bf16[4,8,24,512]{3,2,1,0:T(8,128)(2,1)} %get-tuple-element.34), channel_id=1, source_target_pairs={{0,16},{8,24},{16,0},{24,8},{1,17},{9,25},{17,1},{25,9},{2,18},{10... | collective-permute-start | bytes 2359304 | tf_op jit(solution)/shard_map/ppermute | solution.py:375
  163.9 24.9 %collective-permute-start.9 = (bf16[4,8,24,512]{3,2,1,0:T(8,128)(2,1)}, bf16[4,8,24,512]{3,2,1,0:T(8,128)(2,1)}, u32[]{:S(2)}, u32[]{:S(2)}) collective-permute-start(bf16[4,8,24,512]{3,2,1,0:T(8,128)(2,1)} %get-tuple-element.35), channel_id=1, source_target_pairs={{0,24},{8,0},{16,8},{24,16},{1,25},{9,1},{17,9},{25,17},{2,26},{10... | collective-permute-start | bytes 2359304 | tf_op jit(solution)/shard_map/ppermute | solution.py:375
  211.4 49.4 %all-to-all-start.2 = ((bf16[128,24,512]{2,1,0:T(8,128)(2,1)}), bf16[128,24,512]{2,1,0:T(8,128)(2,1)}, u32[]{:S(2)}, u32[]{:S(2)}) async-start(bf16[128,24,512]{2,1,0:T(8,128)(2,1)} %shard_map.127), calls=%async_computation.2 | async-start | bytes 6291456 | tf_op jit(solution)/shard_map/all_to_all | solution.py:371
  221.0 8.6 %copy-start.1 = (bf16[768,2048]{1,0:T(8,128)(2,1)S(1)}, bf16[768,2048]{1,0:T(8,128)(2,1)}, u32[]{:S(2)}) copy-start(bf16[768,2048]{1,0:T(8,128)(2,1)} %shard_map.124) | copy-start | bytes 9437188
  229.7 3.3 %copy-start.6 = (f32[768,1536]{0,1:T(8,128)}, f32[768,1536]{0,1:T(8,128)S(1)}, u32[]{:S(2)}) copy-start(f32[768,1536]{0,1:T(8,128)S(1)} %fusion.3) | copy-start | bytes 14155780
  233.0 1.0 copy-start.7
  233.0 1.4 copy-start.9
  260.8 47.0 %all-to-all-start.3 = ((bf16[128,24,512]{2,1,0:T(8,128)(2,1)}), bf16[128,24,512]{2,1,0:T(8,128)(2,1)}, u32[]{:S(2)}, u32[]{:S(2)}) async-start(bf16[128,24,512]{2,1,0:T(8,128)(2,1)} %shard_map.128), calls=%async_computation.3 | async-start | bytes 6291456 | tf_op jit(solution)/shard_map/all_to_all | solution.py:371
  267.9 7.8 %copy-start.8 = (bf16[768,768]{0,1:T(8,128)(2,1)S(1)}, bf16[768,768]{0,1:T(8,128)(2,1)}, u32[]{:S(2)}) copy-start(bf16[768,768]{0,1:T(8,128)(2,1)} %copy-done.7) | copy-start | bytes 3538948
  267.9 7.8 %copy-start.10 = (bf16[768,768]{0,1:T(8,128)(2,1)S(1)}, bf16[768,768]{0,1:T(8,128)(2,1)}, u32[]{:S(2)}) copy-start(bf16[768,768]{0,1:T(8,128)(2,1)} %copy-done.9) | copy-start | bytes 3538948
